TPU v7x, 768 devices: a whole 4x8x12 slice. The times are simulated.
768 devices in a mesh: dp: 12 (over z), tensor: 64 (over y, x, core).
Axes of the slice: x: 4, y: 8, z: 12, core: 2. Of those that a mesh axis runs over, the one named last changes fastest.
Arguments:
- gradients: bfloat16 [12, 192, 512, 512], P('dp', None, 'tensor'), may hold values from -240 to 240
- momentum: bfloat16 [12, 36, 512, 512], P('dp', None, 'tensor'), may hold values from -36 to 36
- owners: int32 [192], replicated, may hold values from 0 to 11, as said below
Outputs:
- updates: float32 [12, 36, 512, 512], P('dp', None, 'tensor')
Inputs may be any that keep to these rules, and one draw needn't show every extreme that they name: `owners`: the blocks b with b // 16 == h give at most 3 blocks to any one owner, and exactly 3 to some owner, for every h; each owner holds at most 36 blocks, and some owner holds exactly 36.
All inputs are finite; a program needn't handle non-finite values.
Results may differ from a plain program's by a relative error of at most 0.018.
Values may be sent and summed in bfloat16 or wider, within the bound.
No kernel may reach another device: no remote copies, remote signals or barrier semaphores. Data moves between devices by JAX's collectives and lax.ppermute only.
A program may use at most 32 MiB of HBM per device.

v0:
```python
import math

import jax
import jax.numpy as jnp
from jax import lax
from jax.sharding import Mesh
from jax.sharding import PartitionSpec as P

ITERS = 3
TENSOR = ("tensor_0", "tensor_1", "tensor_2")


decay_rate = 0.95
newton_a = 3.4445
newton_b = -4.775
newton_c = 2.0315
norm_eps = 1e-07


def in_blocks(shard, dim, size):
    before, after = (shard.shape[:dim], shard.shape[dim + 1 :])
    return jnp.moveaxis(shard.reshape(*before, size, -1, *after), dim, 0)


def sum_at_owner(shard, axis, dim):
    pieces = in_blocks(shard, dim, lax.axis_size(axis))
    arrived = lax.all_to_all(pieces, axis, split_axis=0, concat_axis=0, tiled=True)
    return arrived.astype(jnp.float32).sum(axis=0)


def laid_out(pieces, dim):
    lengths = list(pieces.shape[1:])
    lengths[dim] *= pieces.shape[0]
    return jnp.moveaxis(pieces, 0, dim).reshape(lengths)


def moved_by_axis(pieces, axes, turns):
    inside = pieces.shape[1:]
    result = pieces.reshape(*(lax.axis_size(a) for a in axes), *inside)
    for k in turns:
        result = lax.all_to_all(result, axes[k], k, k, tiled=True)
    return result.reshape(-1, *inside)


def two_step_exchange(shard, groups, turns, split_dim, concat_dim):
    size = lax.axis_size(groups[0]) * lax.axis_size(groups[1])
    pieces = in_blocks(shard, split_dim, size)
    return laid_out(moved_by_axis(pieces, groups, turns), concat_dim)


def ranks_of(labels):
    length = labels.shape[0]
    places = jnp.arange(length, dtype=jnp.int32)
    earlier = (labels[None, :] == labels[:, None]) & (places[None, :] < places[:, None])
    return jnp.sum(earlier.astype(jnp.int32), axis=1)


def iterate(blocks):
    widened = blocks.astype(jnp.float32)
    lengths = jnp.sqrt(jnp.sum(widened * widened, axis=(1, 2), keepdims=True)) + norm_eps
    current = widened / lengths
    scale_up = math.sqrt(blocks.shape[1])
    for iteration in range(ITERS):
        squared = jnp.einsum("kij,klj->kil", current, current, preferred_element_type=jnp.float32)
        polynomial = newton_b * squared + newton_c * jnp.einsum(
            "kij,kjl->kil", squared, squared, preferred_element_type=jnp.float32
        )
        current = newton_a * current + jnp.einsum(
            "kij,kjl->kil", polynomial, current, preferred_element_type=jnp.float32
        )
    return current * scale_up


def body(gradients, momentum, owners):
    dp_count = lax.axis_size("dp")
    tp_count = lax.axis_size(TENSOR)
    my_group = lax.axis_index("dp")
    pieces = gradients[0]
    blocks_all = pieces.shape[0]
    per_group = blocks_all // dp_count
    capacity = momentum.shape[1]
    places = jnp.arange(blocks_all, dtype=jnp.int32)
    slot_rank = ranks_of(owners)
    slot_ids = jnp.arange(capacity, dtype=jnp.int32)
    groups = jnp.arange(dp_count, dtype=jnp.int32)
    my_slots = (owners[:, None] == my_group) & (slot_rank[:, None] == slot_ids[None, :])
    occupied = jnp.any(my_slots, axis=0)
    held_sum = sum_at_owner(pieces, "dp", 0).astype(jnp.bfloat16)
    pair_most = (2 * per_group + dp_count - 1) // dp_count
    held_owner = lax.dynamic_slice_in_dim(owners, my_group * per_group, per_group)
    held_rank = ranks_of(held_owner)
    held_places = jnp.arange(per_group, dtype=jnp.int32)
    pair_ids = jnp.arange(pair_most, dtype=jnp.int32)
    matched = (held_owner[:, None, None] == groups[None, :, None]) & (
        held_rank[:, None, None] == pair_ids[None, None, :]
    )
    source = jnp.sum(jnp.where(matched, held_places[:, None, None], 0), axis=0).reshape(-1)
    filled = jnp.any(matched, axis=0).reshape(-1)
    selected = jnp.take(held_sum, source, axis=0)
    outgoing = jnp.where(filled[:, None, None], selected, jnp.zeros_like(selected))
    outgoing = outgoing.reshape(dp_count, pair_most, pieces.shape[1], pieces.shape[2])
    incoming = lax.all_to_all(outgoing, "dp", split_axis=0, concat_axis=0, tiled=True)
    incoming = incoming.reshape(dp_count * pair_most, pieces.shape[1], pieces.shape[2])
    group_rank = ranks_of(owners * dp_count + places // per_group)
    position = places // per_group * pair_most + group_rank
    arriving = jnp.sum(jnp.where(my_slots, position[:, None], 0), axis=0)
    chosen = jnp.take(incoming, arriving, axis=0)
    gradient = jnp.where(occupied[:, None, None], chosen, jnp.zeros_like(chosen))
    widened_g = gradient.astype(jnp.float32)
    widened_m = momentum[0].astype(jnp.float32)
    blended = (widened_g + decay_rate * (decay_rate * widened_m + widened_g)).astype(jnp.bfloat16)
    per_device = (capacity + tp_count - 1) // tp_count
    total_slots = per_device * tp_count
    padded = jnp.pad(blended, ((0, total_slots - capacity), (0, 0), (0, 0)))
    padded = padded.reshape(tp_count, per_device, blended.shape[1], blended.shape[2])
    finished = iterate(lax.all_to_all(padded, TENSOR, split_axis=0, concat_axis=2, tiled=True)[0])[
        None
    ]
    result = two_step_exchange(
        finished.astype(jnp.bfloat16), (("tensor_0", "tensor_1"), "tensor_2"), (1, 0), 2, 0
    ).astype(finished.dtype)
    update = result.reshape(total_slots, blended.shape[1], blended.shape[2])[:capacity]
    update = jnp.where(occupied[:, None, None], update, jnp.zeros_like(update))
    return update[None]


def solution(mesh):
    split = Mesh(
        mesh.devices.reshape(mesh.shape["dp"], 8, 4, 2), ("dp", "tensor_0", "tensor_1", "tensor_2")
    )
    in_specs = (P("dp", None, TENSOR, None), P("dp", None, TENSOR, None), P())
    out_specs = P("dp", None, TENSOR, None)
    return jax.shard_map(body, mesh=split, in_specs=in_specs, out_specs=out_specs, check_vma=False)
```

profile of v0, /device:TPU:1, one launch (start us, length us, event | category | flops | bytes accessed | tf_op | source)
XLA Modules:
  0.0 156.4 jit_solution(5447328152672376103)
XLA Ops:
  0.0 15.8 %all-to-all-start = ((bf16[12,16,8,512]{3,2,1,0:T(8,128)(2,1)}), bf16[12,16,8,512]{3,2,1,0:T(8,128)(2,1)S(1)}, u32[]{:S(2)}, u32[]{:S(2)}) async-start(bf16[12,16,8,512]{3,2,1,0:T(8,128)(2,1)} %bitcast.35), calls=%async_computation | async-start | bytes 3145728 | tf_op jit(solution)/shard_map/all_to_all | solution.py:27
  15.9 0.1 dynamic_slice.3
  15.9 0.2 convert_reduce_fusion.2
  16.2 0.1 fusion.27
  16.3 0.1 copy.8
  16.4 0.1 copy.7
  16.5 0.1 and_reduce_fusion
  16.6 0.1 copy.6
  16.7 0.1 reshape.280
  16.8 0.2 convert_reduce_fusion
  17.1 52.1 %all-to-all-done = bf16[12,16,8,512]{3,2,1,0:T(8,128)(2,1)S(1)} async-done(((bf16[12,16,8,512]{3,2,1,0:T(8,128)(2,1)}), bf16[12,16,8,512]{3,2,1,0:T(8,128)(2,1)S(1)}, u32[]{:S(2)}, u32[]{:S(2)}) %all-to-all-start) | async-done | bytes 1572896 | tf_op jit(solution)/shard_map/all_to_all | solution.py:27
  69.1 0.2 reduce_sum.73
  69.3 0.6 gather_fusion
  69.9 0.9 select_select_fusion
  70.8 7.7 %all-to-all-start.1 = ((bf16[12,3,8,512]{3,2,1,0:T(8,128)(2,1)}), bf16[12,3,8,512]{3,2,1,0:T(8,128)(2,1)S(1)}, u32[]{:S(2)}, u32[]{:S(2)}) async-start(bf16[12,3,8,512]{3,2,1,0:T(8,128)(2,1)} %select_select_fusion), calls=%async_computation.1 | async-start | bytes 589824 | tf_op jit(solution)/shard_map/all_to_all | solution.py:102
  78.5 0.2 convert_reduce_fusion.1
  78.6 0.1 select_reduce_fusion
  78.8 0.1 fusion.26
  78.9 13.9 %all-to-all-done.1 = bf16[12,3,8,512]{3,2,1,0:T(8,128)(2,1)S(1)} async-done(((bf16[12,3,8,512]{3,2,1,0:T(8,128)(2,1)}), bf16[12,3,8,512]{3,2,1,0:T(8,128)(2,1)S(1)}, u32[]{:S(2)}, u32[]{:S(2)}) %all-to-all-start.1) | async-done | bytes 294944 | tf_op jit(solution)/shard_map/all_to_all | solution.py:102
  92.8 0.6 gather_fusion.1
  93.4 0.2 fusion.14
  93.7 31.0 %all_to_all.29 = bf16[64,1,8,512]{3,2,1,0:T(8,128)(2,1)S(1)} all-to-all(bf16[64,1,8,512]{3,2,1,0:T(8,128)(2,1)S(1)} %pad_bitcast_fusion), channel_id=1, replica_groups=mesh['dp'=12,'tensor_0'=8,'tensor_1'=4,'tensor_2'=2] {'tensor_0','tensor..., dimensions={0} | all-to-all | bytes 1048576 | tf_op jit(solution)/shard_map/all_to_all | solution.py:116
  124.7 0.9 fusion.5
  126.2 0.5 fusion.10
  126.7 0.8 convolution_add_fusion.2
  127.5 0.5 fusion.37
  128.0 0.7 convolution_add_fusion.1
  128.7 0.5 fusion.38
  129.2 0.7 fusion.4
  130.0 4.2 %all_to_all.30 = bf16[32,2,1,1,8,512]{5,4,0,3,2,1:T(8,128)(2,1)S(1)} all-to-all(bf16[32,2,1,1,8,512]{5,4,0,3,2,1:T(8,128)(2,1)S(1)} %copy.9), channel_id=1, replica_groups=mesh['dp'=12,'tensor_0'=8,'tensor_1'=4,'tensor_2'=2] {'tensor_2'}, dimensions={1} | all-to-all | bytes 1048576 | tf_op jit(solution)/shard_map/all_to_all | solution.py:41
  134.2 21.3 %all_to_all.31 = bf16[32,2,1,1,8,512]{5,4,1,3,2,0:T(8,128)(2,1)S(1)} all-to-all(bf16[32,2,1,1,8,512]{5,4,1,3,2,0:T(8,128)(2,1)S(1)} %copy.10), channel_id=1, replica_groups=mesh['dp'=12,'tensor_0'=8,'tensor_1'=4,'tensor_2'=2] {'tensor_0','tensor..., dimensions={0} | all-to-all | bytes 1048576 | tf_op jit(solution)/shard_map/all_to_all | solution.py:41
  155.5 0.9 convert_select_fusion
  (19 shorter events, 0.3 us)
Async XLA Ops:
  0.0 15.8 %copy-start.1 = (s32[192]{0:T(256)S(1)}, s32[192]{0:T(256)}, u32[]{:S(2)}) copy-start(s32[192]{0:T(256)} %param.5) | copy-start | bytes 2308
  0.0 69.1 %all-to-all-start = ((bf16[12,16,8,512]{3,2,1,0:T(8,128)(2,1)}), bf16[12,16,8,512]{3,2,1,0:T(8,128)(2,1)S(1)}, u32[]{:S(2)}, u32[]{:S(2)}) async-start(bf16[12,16,8,512]{3,2,1,0:T(8,128)(2,1)} %bitcast.35), calls=%async_computation | async-start | bytes 3145728 | tf_op jit(solution)/shard_map/all_to_all | solution.py:27
  69.3 24.1 %copy-start = (bf16[1,36,8,512]{3,2,1,0:T(8,128)(2,1)S(1)}, bf16[1,36,8,512]{3,2,1,0:T(8,128)(2,1)}, u32[]{:S(2)}) copy-start(bf16[1,36,8,512]{3,2,1,0:T(8,128)(2,1)} %param.4) | copy-start | bytes 884740
  70.8 22.1 %all-to-all-start.1 = ((bf16[12,3,8,512]{3,2,1,0:T(8,128)(2,1)}), bf16[12,3,8,512]{3,2,1,0:T(8,128)(2,1)S(1)}, u32[]{:S(2)}, u32[]{:S(2)}) async-start(bf16[12,3,8,512]{3,2,1,0:T(8,128)(2,1)} %select_select_fusion), calls=%async_computation.1 | async-start | bytes 589824 | tf_op jit(solution)/shard_map/all_to_all | solution.py:102
where the time goes:
time: 157 us; the launch traced here: 156 us
  waiting for transfers between devices  66 us (42%)
  blocking collectives  56.4 us (36%)
  starting transfers between devices  23.5 us (15%)
  other arithmetic  4.21 us (3%)
  matrix products  3.66 us (2%)
  local copies, waits for them, and re-layouts  1.78 us (1%)
    all_to_all x1, waiting for transfers between devices, sum_at_owner(): lax.all_to_all(pieces, axis, split_axis=0, concat_axis=0, tiled=True)  52.1 us
    all_to_all x1, blocking collectives, body(): lax.all_to_all(padded, TENSOR, split_axis=0, concat_axis=2, tiled=True)[0]  31 us
    all_to_all x2, blocking collectives, moved_by_axis(): result = lax.all_to_all(result, axes[k], k, k, tiled=True)  25.4 us
    all_to_all x1, starting transfers between devices, sum_at_owner(): lax.all_to_all(pieces, axis, split_axis=0, concat_axis=0, tiled=True)  15.8 us
    all_to_all x1, waiting for transfers between devices, body(): lax.all_to_all(outgoing, 'dp', split_axis=0, concat_axis=0, tiled=True)  13.9 us
    all_to_all x1, starting transfers between devices, body(): lax.all_to_all(outgoing, 'dp', split_axis=0, concat_axis=0, tiled=True)  7.66 us
  transfers between devices with their start and end apart: 2, of which 2 were waited for; matrix products, arithmetic and copies ran while one was open for 1% of the time, Pallas kernels for 0%

commit v1 on v0

v1 whole, which is shorter than its diff:
```python
import math

import jax
import jax.numpy as jnp
from jax import lax
from jax.sharding import Mesh
from jax.sharding import PartitionSpec as P

ITERS = 3
PAIR = 3
TENSOR = ("ty", "tx", "tc")
HOLD = ("ty", "tc")
SPLIT = (8, 4, 2)


decay_rate = 0.95
newton_a = 3.4445
newton_b = -4.775
newton_c = 2.0315
norm_eps = 1e-07


def exchange(pieces, axes):
    return lax.all_to_all(pieces, axes, split_axis=0, concat_axis=0, tiled=True)


def shifted(pieces, step):
    count = lax.axis_size("dp")
    return lax.ppermute(pieces, "dp", [(i, (i + step) % count) for i in range(count)])


def ranks_of(labels):
    length = labels.shape[0]
    places = jnp.arange(length, dtype=jnp.int32)
    earlier = (labels[None, :] == labels[:, None]) & (places[None, :] < places[:, None])
    return jnp.sum(earlier.astype(jnp.int32), axis=1)


def sum_at_holder(chunks):
    wide = lambda piece: piece.astype(jnp.float32)
    narrow = lambda piece: piece.astype(jnp.bfloat16)
    at = lambda k: chunks[k % 12]
    size = chunks.shape[1]
    half = size // 2
    ahead = shifted(jnp.concatenate([at(5), at(-3), at(2)]), 1)
    behind = shifted(jnp.concatenate([at(-5), at(3), at(-2)]), -1)
    ahead_far = shifted(at(6)[:half], 2)
    behind_far = shifted(at(6)[half:], -2)
    blank = jnp.zeros(ahead_far.shape, jnp.float32)
    to_far = wide(at(4)) + wide(ahead[:size]) + wide(behind[size : 2 * size])
    to_far = narrow(to_far + jnp.concatenate([wide(ahead_far), blank]))
    from_far = wide(at(-4)) + wide(behind[:size]) + wide(ahead[size : 2 * size])
    from_far = narrow(from_far + jnp.concatenate([blank, wide(behind_far)]))
    to_near = narrow(wide(at(1)) + wide(ahead[2 * size :]))
    from_near = narrow(wide(at(-1)) + wide(behind[2 * size :]))
    far = wide(shifted(to_far, 4)) + wide(shifted(from_far, -4))
    near = wide(shifted(to_near, 1)) + wide(shifted(from_near, -1))
    return narrow(wide(at(0)) + far + near)


def iterate(block, first_row, rows):
    widened = block.astype(jnp.float32) * (1.0 + decay_rate)
    length = jnp.sqrt(jnp.sum(widened * widened)) + norm_eps
    current = widened / length
    scale_up = math.sqrt(block.shape[0])
    dot = lambda a, b: jnp.dot(a, b, preferred_element_type=jnp.float32)
    for iteration in range(ITERS):
        squared = lax.dot_general(
            current, current, (((1,), (1,)), ((), ())), preferred_element_type=jnp.float32
        )
        if iteration == ITERS - 1:
            mine = lax.dynamic_slice_in_dim(squared, first_row, rows)
            kept = lax.dynamic_slice_in_dim(current, first_row, rows)
        else:
            mine, kept = squared, current
        polynomial = newton_b * mine + newton_c * dot(mine, squared)
        current = newton_a * kept + dot(polynomial, current)
    return current * scale_up


def body(gradients, momentum, owners):
    dp_count = lax.axis_size("dp")
    my_group = lax.axis_index("dp")
    tx_count = lax.axis_size("tx")
    pieces = gradients[0]
    blocks_all, piece_rows, width = pieces.shape
    per_group = blocks_all // dp_count
    capacity = momentum.shape[1]
    places = jnp.arange(blocks_all, dtype=jnp.int32)
    slot_rank = ranks_of(owners)
    slot_ids = jnp.arange(capacity, dtype=jnp.int32)
    mine = owners == my_group
    weight = decay_rate * decay_rate / (1.0 + decay_rate)
    order = jnp.arange(dp_count, dtype=jnp.int32) + my_group
    order = jnp.where(order >= dp_count, order - dp_count, order)
    turned = jnp.take(pieces.reshape(dp_count, per_group, piece_rows, width), order, axis=0)
    turned_places = (order[:, None] * per_group + jnp.arange(per_group)[None, :]).reshape(-1)
    turned_mine = jnp.take(mine, turned_places)
    own_slot = jnp.take(jnp.where(mine, slot_rank, 0), turned_places)
    own_momentum = jnp.take(momentum[0], own_slot, axis=0).astype(jnp.float32)
    joined = turned.reshape(pieces.shape).astype(jnp.float32) + jnp.where(
        turned_mine[:, None, None], weight * own_momentum, 0.0
    )
    joined = joined.astype(jnp.bfloat16)
    held = sum_at_holder(joined.reshape(dp_count, per_group, piece_rows, width))
    hold_rows = lax.axis_size("ty")
    copies = held.reshape(hold_rows, 1, -1, piece_rows, width)
    copies = jnp.broadcast_to(copies, (hold_rows, tx_count, *copies.shape[2:]))
    whole = exchange(copies.reshape(-1, piece_rows, width), TENSOR)
    whole = whole.reshape(hold_rows, tx_count, -1, width).swapaxes(0, 1).reshape(-1, width)
    slab = whole.shape[0] // tx_count
    finished = iterate(whole, lax.axis_index("tx") * slab, slab)
    back = exchange(finished.astype(jnp.bfloat16).reshape(-1, piece_rows, width), HOLD)
    groups = jnp.arange(dp_count, dtype=jnp.int32)
    held_owner = lax.dynamic_slice_in_dim(owners, my_group * per_group, per_group)
    held_rank = ranks_of(held_owner)
    held_places = jnp.arange(per_group, dtype=jnp.int32)
    pair_ids = jnp.arange(PAIR, dtype=jnp.int32)
    matched = (held_owner[:, None, None] == groups[None, :, None]) & (
        held_rank[:, None, None] == pair_ids[None, None, :]
    )
    source = jnp.sum(jnp.where(matched, held_places[:, None, None], 0), axis=0).reshape(-1)
    outgoing = jnp.take(back, source, axis=0)
    incoming = exchange(outgoing, "dp")
    group_rank = ranks_of(owners * dp_count + places // per_group)
    position = places // per_group * PAIR + group_rank
    my_slots = mine[:, None] & (slot_rank[:, None] == slot_ids[None, :])
    occupied = jnp.any(my_slots, axis=0)
    arriving = jnp.sum(jnp.where(my_slots, position[:, None], 0), axis=0)
    chosen = jnp.take(incoming, arriving, axis=0).astype(jnp.float32)
    update = jnp.where(occupied[:, None, None], chosen, 0.0)
    return update[None]


def solution(mesh):
    split = Mesh(mesh.devices.reshape(mesh.shape["dp"], *SPLIT), ("dp", *TENSOR))
    in_specs = (P("dp", None, TENSOR, None), P("dp", None, TENSOR, None), P())
    out_specs = P("dp", None, TENSOR, None)
    return jax.shard_map(body, mesh=split, in_specs=in_specs, out_specs=out_specs, check_vma=False)
```

time: 157 us -> 150 us (0.955)
  blocking collectives: 56.4 us -> 0 us
  starting transfers between devices: 23.5 us -> 64.1 us
  waiting for transfers between devices: 66 us -> 50.9 us
  matrix products: 3.66 us -> 15.7 us
  local copies, waits for them, and re-layouts: 1.78 us -> 8.66 us
  other arithmetic: 4.21 us -> 8.72 us
    all_to_all x3 -> x0, blocking collectives: 56.4 us -> none  [the longest x1 31 us: body(): lax.all_to_all(padded, TENSOR, split_axis=0, concat_axis=2, tiled=True)[0]]
    ppermute x0 -> x8, starting transfers between devices: none -> 40.1 us  [shifted(): lax.ppermute(pieces, 'dp', [(i, (i + step) % count) for i in range(count)])]
    all_to_all x2 -> x3, waiting for transfers between devices: 66 us -> 41 us  [exchange(): return lax.all_to_all(pieces, axes, split_axis=0, concat_axis=0, tiled=True)]
    dot_general x6, matrix products: 3.66 us -> 15.7 us  [the longest x3 9.69 us: iterate(): dot = lambda a, b: jnp.dot(a, b, preferred_element_type=jnp.float32)]
    ppermute x0 -> x8, waiting for transfers between devices: none -> 9.99 us  [shifted(): lax.ppermute(pieces, 'dp', [(i, (i + step) % count) for i in range(count)])]
    gather x2 -> x6, local copies, waits for them, and re-layouts: 1.14 us -> 6.99 us  [the longest x1 1.86 us: body(): jnp.take(pieces.reshape(dp_count, per_group, piece_rows, width), order, a...]
    convert_element_type x1 -> x3, other arithmetic: 0.23 us -> 3.22 us  [the longest x1 2.94 us: body(): joined = joined.astype(jnp.bfloat16)]
    all_to_all x2 -> x3, starting transfers between devices: 23.5 us -> 24 us  [exchange(): return lax.all_to_all(pieces, axes, split_axis=0, concat_axis=0, tiled=True)]
  transfers between devices with their start and end apart: 2 -> 11, of which waited for: 2 -> 8; matrix products, arithmetic and copies ran while one was open for 1% -> 1% of each run, Pallas kernels for 0% -> 0%
where the time goes in v1:
time: 150 us; the launch traced here: 149 us
  starting transfers between devices  64.1 us (43%)
  waiting for transfers between devices  50.9 us (34%)
  matrix products  15.7 us (10%)
  other arithmetic  8.72 us (6%)
  local copies, waits for them, and re-layouts  8.66 us (6%)
    all_to_all x3, waiting for transfers between devices, exchange(): return lax.all_to_all(pieces, axes, split_axis=0, concat_axis=0, tiled=True)  41 us
    ppermute x8, starting transfers between devices, shifted(): lax.ppermute(pieces, 'dp', [(i, (i + step) % count) for i in range(count)])  40.1 us
    all_to_all x3, starting transfers between devices, exchange(): return lax.all_to_all(pieces, axes, split_axis=0, concat_axis=0, tiled=True)  24 us
    ppermute x8, waiting for transfers between devices, shifted(): lax.ppermute(pieces, 'dp', [(i, (i + step) % count) for i in range(count)])  9.99 us
    dot_general x3, matrix products, iterate(): dot = lambda a, b: jnp.dot(a, b, preferred_element_type=jnp.float32)  9.69 us
    dot_general x3, matrix products, iterate(): lax.dot_general(current, current, (((1,), (1,)), ((), ())), preferred_ele...  6 us
  transfers between devices with their start and end apart: 11, of which 8 were waited for; matrix products, arithmetic and copies ran while one was open for 1% of the time, Pallas kernels for 0%

profile of v1, /device:TPU:1, one launch (start us, length us, event | category | flops | bytes accessed | tf_op | source)
XLA Modules:
  0.0 149.1 jit_solution(15057389631045363511)
XLA Ops:
  0.3 0.9 convert_reduce_fusion.1
  1.9 1.6 %gather_fusion.1 = pred[192]{0:T(512)(128)(4,1)S(1)} fusion(pred[192]{0:T(512)(128)(4,1)S(1)} %get-tuple-element.6, s32[1024]{0:T(1024)S(1)} %pad_clamp_fusion.3), kind=kCustom, calls=%fused_computation.1 | custom fusion | bytes 1152 | tf_op jit(solution)/shard_map/jit(_take)/gather | solution.py:98
  3.5 1.6 %gather_fusion.2 = s32[192]{0:T(256)S(1)} fusion(s32[192]{0:T(256)S(1)} %get-tuple-element.5, s32[1024]{0:T(1024)S(1)} %pad_clamp_fusion.3), kind=kCustom, calls=%fused_computation.2 | custom fusion | bytes 2304 | tf_op jit(solution)/shard_map/jit(_take)/gather | solution.py:99
  6.2 1.9 %gather_fusion = bf16[12,16,8,512]{3,2,1,0:T(8,128)(2,1)} fusion(bf16[12,16,8,512]{3,2,1,0:T(8,128)(2,1)S(1)} %bitcast.43, s32[1024]{0:T(1024)S(1)} %pad_clamp_fusion.4), kind=kCustom, calls=%fused_computation | custom fusion | bytes 3145776 | tf_op jit(solution)/shard_map/jit(_take)/gather | solution.py:96
  8.0 2.9 %add_convert_fusion = bf16[192,8,512]{2,1,0:T(8,128)(2,1)S(1)} fusion(bf16[12,16,8,512]{3,2,1,0:T(8,128)(2,1)} %gather_fusion, bf16[192,8,512]{2,1,0:T(8,128)(2,1)S(1)} %gather_fusion.3, pred[192]{0:T(512)(128)(4,1)S(1)} %get-tuple-element.21, pred[192]{0:T(512)(128)(4,1)S(1)} %get-tuple-element.20, pred[192]{0:T(512)(128)(4,1)S(1)} %broadcast_in_dim.148), kind=kLoop, calls=%fused_computation.6 | loop fusion | flops 6291456 | bytes 4719168 | tf_op jit(solution)/shard_map/convert_element_type | solution.py:104
  11.1 4.8 %collective-permute-start = (bf16[48,8,512]{2,1,0:T(8,128)(2,1)S(1)}, bf16[48,8,512]{2,1,0:T(8,128)(2,1)S(1)}, u32[]{:S(2)}, u32[]{:S(2)}) collective-permute-start(bf16[48,8,512]{2,1,0:T(8,128)(2,1)S(1)} %pad_maximum_fusion), channel_id=1, source_target_pairs={{0,64},{64,128},{128,192},{192,256},{256,320},{320,384},{384,448},... | collective-permute-start | bytes 1179656 | tf_op jit(solution)/shard_map/ppermute | solution.py:29
  16.0 12.2 %collective-permute-start.1 = (bf16[48,8,512]{2,1,0:T(8,128)(2,1)S(1)}, bf16[48,8,512]{2,1,0:T(8,128)(2,1)S(1)}, u32[]{:S(2)}, u32[]{:S(2)}) collective-permute-start(bf16[48,8,512]{2,1,0:T(8,128)(2,1)S(1)} %pad_maximum_fusion.1), channel_id=1, source_target_pairs={{0,704},{64,0},{128,64},{192,128},{256,192},{320,256},{384,320},{4... | collective-permute-start | bytes 1179656 | tf_op jit(solution)/shard_map/ppermute | solution.py:29
  28.2 1.9 %collective-permute-start.2 = (bf16[8,8,512]{2,1,0:T(8,128)(2,1)S(1)}, bf16[8,8,512]{2,1,0:T(8,128)(2,1)S(1)}, u32[]{:S(2)}, u32[]{:S(2)}) collective-permute-start(bf16[8,8,512]{2,1,0:T(8,128)(2,1)S(1)} %get-tuple-element.11), channel_id=1, source_target_pairs={{0,128},{64,192},{128,256},{192,320},{256,384},{320,448},{384,512}... | collective-permute-start | bytes 196616 | tf_op jit(solution)/shard_map/ppermute | solution.py:29
  30.2 5.5 %collective-permute-start.4 = (bf16[8,8,512]{2,1,0:T(8,128)(2,1)S(1)}, bf16[8,8,512]{2,1,0:T(8,128)(2,1)S(1)}, u32[]{:S(2)}, u32[]{:S(2)}) collective-permute-start(bf16[8,8,512]{2,1,0:T(8,128)(2,1)S(1)} %get-tuple-element.12), channel_id=1, source_target_pairs={{0,640},{64,704},{128,0},{192,64},{256,128},{320,192},{384,256},{4... | collective-permute-start | bytes 196616 | tf_op jit(solution)/shard_map/ppermute | solution.py:29
  35.6 2.1 %collective-permute-done.2 = bf16[8,8,512]{2,1,0:T(8,128)(2,1)S(1)} collective-permute-done((bf16[8,8,512]{2,1,0:T(8,128)(2,1)S(1)}, bf16[8,8,512]{2,1,0:T(8,128)(2,1)S(1)}, u32[]{:S(2)}, u32[]{:S(2)}) %collective-permute-start.2) | collective-permute-done | bytes 65568 | tf_op jit(solution)/shard_map/ppermute | solution.py:29
  37.7 0.9 collective-permute-done.4
  38.9 3.9 %collective-permute-start.3 = (bf16[16,8,512]{2,1,0:T(8,128)(2,1)S(1)}, bf16[16,8,512]{2,1,0:T(8,128)(2,1)S(1)}, u32[]{:S(2)}, u32[]{:S(2)}) collective-permute-start(bf16[16,8,512]{2,1,0:T(8,128)(2,1)S(1)} %get-tuple-element.7), channel_id=1, source_target_pairs={{0,256},{64,320},{128,384},{192,448},{256,512},{320,576},{384,640}... | collective-permute-start | bytes 393224 | tf_op jit(solution)/shard_map/ppermute | solution.py:29
  42.8 5.3 %collective-permute-start.5 = (bf16[16,8,512]{2,1,0:T(8,128)(2,1)S(1)}, bf16[16,8,512]{2,1,0:T(8,128)(2,1)S(1)}, u32[]{:S(2)}, u32[]{:S(2)}) collective-permute-start(bf16[16,8,512]{2,1,0:T(8,128)(2,1)S(1)} %get-tuple-element.8), channel_id=1, source_target_pairs={{0,512},{64,576},{128,640},{192,704},{256,0},{320,64},{384,128},{4... | collective-permute-start | bytes 393224 | tf_op jit(solution)/shard_map/ppermute | solution.py:29
  48.1 1.9 %collective-permute-start.6 = (bf16[16,8,512]{2,1,0:T(8,128)(2,1)S(1)}, bf16[16,8,512]{2,1,0:T(8,128)(2,1)S(1)}, u32[]{:S(2)}, u32[]{:S(2)}) collective-permute-start(bf16[16,8,512]{2,1,0:T(8,128)(2,1)S(1)} %get-tuple-element.9), channel_id=1, source_target_pairs={{0,64},{64,128},{128,192},{192,256},{256,320},{320,384},{384,448},... | collective-permute-start | bytes 393224 | tf_op jit(solution)/shard_map/ppermute | solution.py:29
  50.0 4.6 %collective-permute-start.7 = (bf16[16,8,512]{2,1,0:T(8,128)(2,1)S(1)}, bf16[16,8,512]{2,1,0:T(8,128)(2,1)S(1)}, u32[]{:S(2)}, u32[]{:S(2)}) collective-permute-start(bf16[16,8,512]{2,1,0:T(8,128)(2,1)S(1)} %get-tuple-element.10), channel_id=1, source_target_pairs={{0,704},{64,0},{128,64},{192,128},{256,192},{320,256},{384,320},{4... | collective-permute-start | bytes 393224 | tf_op jit(solution)/shard_map/ppermute | solution.py:29
  54.9 2.4 %collective-permute-done.6 = bf16[16,8,512]{2,1,0:T(8,128)(2,1)S(1)} collective-permute-done((bf16[16,8,512]{2,1,0:T(8,128)(2,1)S(1)}, bf16[16,8,512]{2,1,0:T(8,128)(2,1)S(1)}, u32[]{:S(2)}, u32[]{:S(2)}) %collective-permute-start.6) | collective-permute-done | bytes 131104 | tf_op jit(solution)/shard_map/ppermute | solution.py:29
  57.3 4.2 %collective-permute-done.7 = bf16[16,8,512]{2,1,0:T(8,128)(2,1)S(1)} collective-permute-done((bf16[16,8,512]{2,1,0:T(8,128)(2,1)S(1)}, bf16[16,8,512]{2,1,0:T(8,128)(2,1)S(1)}, u32[]{:S(2)}, u32[]{:S(2)}) %collective-permute-start.7) | collective-permute-done | bytes 131104 | tf_op jit(solution)/shard_map/ppermute | solution.py:29
  61.7 0.9 broadcast_in_dim.158
  62.5 11.3 %all-to-all-start = ((bf16[64,8,512]{2,1,0:T(8,128)(2,1)}), bf16[64,8,512]{2,1,0:T(8,128)(2,1)S(1)}, u32[]{:S(2)}, u32[]{:S(2)}) async-start(bf16[64,8,512]{2,1,0:T(8,128)(2,1)} %bitcast.8), calls=%async_computation | async-start | bytes 1048576 | tf_op jit(solution)/shard_map/all_to_all | solution.py:24
  74.7 16.8 %all-to-all-done = bf16[64,8,512]{2,1,0:T(8,128)(2,1)S(1)} async-done(((bf16[64,8,512]{2,1,0:T(8,128)(2,1)}), bf16[64,8,512]{2,1,0:T(8,128)(2,1)S(1)}, u32[]{:S(2)}, u32[]{:S(2)}) %all-to-all-start) | async-done | bytes 524320 | tf_op jit(solution)/shard_map/all_to_all | solution.py:24
  91.5 0.9 multiply_reduce_fusion
  93.3 1.5 %fusion.36 = f32[512,512]{1,0:T(8,128)} fusion(f32[512,512]{1,0:T(8,128)S(1)} %bitcast.44), kind=kOutput, calls=%fused_computation.104 | convolution fusion | flops 268435456 | bytes 2097152 | tf_op jit(solution)/shard_map/dot_general | solution.py:68
  94.8 4.0 %convolution_add_fusion.1 = f32[512,512]{1,0:T(8,128)} fusion(f32[512,512]{1,0:T(8,128)S(1)} %bitcast.45, f32[512,512]{1,0:T(8,128)} %fusion.36), kind=kOutput, calls=%fused_computation.11 | convolution fusion | flops 538181632 | bytes 3145728 | tf_op jit(solution)/shard_map/dot_general | solution.py:66
  98.8 3.0 %fusion.37 = f32[512,512]{1,0:T(8,128)} fusion(f32[512,512]{1,0:T(8,128)} %convolution_add_fusion.1), kind=kOutput, calls=%fused_computation.105 | convolution fusion | flops 268435456 | bytes 2097152 | tf_op jit(solution)/shard_map/dot_general | solution.py:68
  101.8 3.3 %convolution_add_fusion = f32[512,512]{1,0:T(8,128)S(1)} fusion(f32[512,512]{1,0:T(8,128)} %convolution_add_fusion.1, f32[512,512]{1,0:T(8,128)} %fusion.37), kind=kOutput, calls=%fused_computation.8 | convolution fusion | flops 538181632 | bytes 3145728 | tf_op jit(solution)/shard_map/dot_general | solution.py:66
  105.1 1.5 fusion.38
  106.6 2.4 %fusion.5 = bf16[16,8,512]{2,1,0:T(8,128)(2,1)} fusion(f32[512,512]{1,0:T(8,128)S(1)} %convolution_add_fusion, f32[512,512]{1,0:T(8,128)} %fusion.38, s32[]{:T(128)S(6)} %select_n.220), kind=kOutput, calls=%fused_computation.19 | convolution fusion | flops 134676480 | bytes 3016192 | tf_op jit(solution)/shard_map/dot_general | solution.py:66
  109.0 4.6 %all-to-all-start.1 = ((bf16[16,8,512]{2,1,0:T(8,128)(2,1)}), bf16[16,8,512]{2,1,0:T(8,128)(2,1)S(1)}, u32[]{:S(2)}, u32[]{:S(2)}) async-start(bf16[16,8,512]{2,1,0:T(8,128)(2,1)} %fusion.5), calls=%async_computation.1 | async-start | bytes 262144 | tf_op jit(solution)/shard_map/all_to_all | solution.py:24
  113.7 8.8 %all-to-all-done.1 = bf16[16,8,512]{2,1,0:T(8,128)(2,1)S(1)} async-done(((bf16[16,8,512]{2,1,0:T(8,128)(2,1)}), bf16[16,8,512]{2,1,0:T(8,128)(2,1)S(1)}, u32[]{:S(2)}, u32[]{:S(2)}) %all-to-all-start.1) | async-done | bytes 131104 | tf_op jit(solution)/shard_map/all_to_all | solution.py:24
  123.9 8.1 %all-to-all-start.2 = ((bf16[36,8,512]{2,1,0:T(8,128)(2,1)}), bf16[36,8,512]{2,1,0:T(8,128)(2,1)S(1)}, u32[]{:S(2)}, u32[]{:S(2)}) async-start(bf16[36,8,512]{2,1,0:T(8,128)(2,1)} %broadcast_select_fusion), calls=%async_computation.2 | async-start | bytes 589824 | tf_op jit(solution)/shard_map/all_to_all | solution.py:24
  132.3 15.3 %all-to-all-done.2 = bf16[36,8,512]{2,1,0:T(8,128)(2,1)S(1)} async-done(((bf16[36,8,512]{2,1,0:T(8,128)(2,1)}), bf16[36,8,512]{2,1,0:T(8,128)(2,1)S(1)}, u32[]{:S(2)}, u32[]{:S(2)}) %all-to-all-start.2) | async-done | bytes 294944 | tf_op jit(solution)/shard_map/all_to_all | solution.py:24
  148.2 1.0 convert_select_fusion
  (55 shorter events, 6.1 us)
Async XLA Ops:
  0.0 6.2 %copy-start = (bf16[1,192,8,512]{3,2,1,0:T(8,128)(2,1)S(1)}, bf16[1,192,8,512]{3,2,1,0:T(8,128)(2,1)}, u32[]{:S(2)}) copy-start(bf16[1,192,8,512]{3,2,1,0:T(8,128)(2,1)} %param.3) | copy-start | bytes 4718596
  0.0 5.3 %copy-start.1 = (bf16[1,36,8,512]{3,2,1,0:T(8,128)(2,1)S(1)}, bf16[1,36,8,512]{3,2,1,0:T(8,128)(2,1)}, u32[]{:S(2)}) copy-start(bf16[1,36,8,512]{3,2,1,0:T(8,128)(2,1)} %param.4) | copy-start | bytes 884740
  11.1 27.6 %collective-permute-start = (bf16[48,8,512]{2,1,0:T(8,128)(2,1)S(1)}, bf16[48,8,512]{2,1,0:T(8,128)(2,1)S(1)}, u32[]{:S(2)}, u32[]{:S(2)}) collective-permute-start(bf16[48,8,512]{2,1,0:T(8,128)(2,1)S(1)} %pad_maximum_fusion), channel_id=1, source_target_pairs={{0,64},{64,128},{128,192},{192,256},{256,320},{320,384},{384,448},... | collective-permute-start | bytes 1179656 | tf_op jit(solution)/shard_map/ppermute | solution.py:29
  16.0 22.7 %collective-permute-start.1 = (bf16[48,8,512]{2,1,0:T(8,128)(2,1)S(1)}, bf16[48,8,512]{2,1,0:T(8,128)(2,1)S(1)}, u32[]{:S(2)}, u32[]{:S(2)}) collective-permute-start(bf16[48,8,512]{2,1,0:T(8,128)(2,1)S(1)} %pad_maximum_fusion.1), channel_id=1, source_target_pairs={{0,704},{64,0},{128,64},{192,128},{256,192},{320,256},{384,320},{4... | collective-permute-start | bytes 1179656 | tf_op jit(solution)/shard_map/ppermute | solution.py:29
  28.2 9.5 %collective-permute-start.2 = (bf16[8,8,512]{2,1,0:T(8,128)(2,1)S(1)}, bf16[8,8,512]{2,1,0:T(8,128)(2,1)S(1)}, u32[]{:S(2)}, u32[]{:S(2)}) collective-permute-start(bf16[8,8,512]{2,1,0:T(8,128)(2,1)S(1)} %get-tuple-element.11), channel_id=1, source_target_pairs={{0,128},{64,192},{128,256},{192,320},{256,384},{320,448},{384,512}... | collective-permute-start | bytes 196616 | tf_op jit(solution)/shard_map/ppermute | solution.py:29
  30.2 8.5 %collective-permute-start.4 = (bf16[8,8,512]{2,1,0:T(8,128)(2,1)S(1)}, bf16[8,8,512]{2,1,0:T(8,128)(2,1)S(1)}, u32[]{:S(2)}, u32[]{:S(2)}) collective-permute-start(bf16[8,8,512]{2,1,0:T(8,128)(2,1)S(1)} %get-tuple-element.12), channel_id=1, source_target_pairs={{0,640},{64,704},{128,0},{192,64},{256,128},{320,192},{384,256},{4... | collective-permute-start | bytes 196616 | tf_op jit(solution)/shard_map/ppermute | solution.py:29
  38.9 35.0 %copy-start.2 = (s32[192]{0:T(256)S(1)}, s32[192]{0:T(256)}, u32[]{:S(2)}) copy-start(s32[192]{0:T(256)} %param.5) | copy-start | bytes 2308
  38.9 15.7 %collective-permute-start.3 = (bf16[16,8,512]{2,1,0:T(8,128)(2,1)S(1)}, bf16[16,8,512]{2,1,0:T(8,128)(2,1)S(1)}, u32[]{:S(2)}, u32[]{:S(2)}) collective-permute-start(bf16[16,8,512]{2,1,0:T(8,128)(2,1)S(1)} %get-tuple-element.7), channel_id=1, source_target_pairs={{0,256},{64,320},{128,384},{192,448},{256,512},{320,576},{384,640}... | collective-permute-start | bytes 393224 | tf_op jit(solution)/shard_map/ppermute | solution.py:29
  42.8 12.1 %collective-permute-start.5 = (bf16[16,8,512]{2,1,0:T(8,128)(2,1)S(1)}, bf16[16,8,512]{2,1,0:T(8,128)(2,1)S(1)}, u32[]{:S(2)}, u32[]{:S(2)}) collective-permute-start(bf16[16,8,512]{2,1,0:T(8,128)(2,1)S(1)} %get-tuple-element.8), channel_id=1, source_target_pairs={{0,512},{64,576},{128,640},{192,704},{256,0},{320,64},{384,128},{4... | collective-permute-start | bytes 393224 | tf_op jit(solution)/shard_map/ppermute | solution.py:29
  48.1 9.2 %collective-permute-start.6 = (bf16[16,8,512]{2,1,0:T(8,128)(2,1)S(1)}, bf16[16,8,512]{2,1,0:T(8,128)(2,1)S(1)}, u32[]{:S(2)}, u32[]{:S(2)}) collective-permute-start(bf16[16,8,512]{2,1,0:T(8,128)(2,1)S(1)} %get-tuple-element.9), channel_id=1, source_target_pairs={{0,64},{64,128},{128,192},{192,256},{256,320},{320,384},{384,448},... | collective-permute-start | bytes 393224 | tf_op jit(solution)/shard_map/ppermute | solution.py:29
  50.0 11.6 %collective-permute-start.7 = (bf16[16,8,512]{2,1,0:T(8,128)(2,1)S(1)}, bf16[16,8,512]{2,1,0:T(8,128)(2,1)S(1)}, u32[]{:S(2)}, u32[]{:S(2)}) collective-permute-start(bf16[16,8,512]{2,1,0:T(8,128)(2,1)S(1)} %get-tuple-element.10), channel_id=1, source_target_pairs={{0,704},{64,0},{128,64},{192,128},{256,192},{320,256},{384,320},{4... | collective-permute-start | bytes 393224 | tf_op jit(solution)/shard_map/ppermute | solution.py:29
  62.5 29.0 %all-to-all-start = ((bf16[64,8,512]{2,1,0:T(8,128)(2,1)}), bf16[64,8,512]{2,1,0:T(8,128)(2,1)S(1)}, u32[]{:S(2)}, u32[]{:S(2)}) async-start(bf16[64,8,512]{2,1,0:T(8,128)(2,1)} %bitcast.8), calls=%async_computation | async-start | bytes 1048576 | tf_op jit(solution)/shard_map/all_to_all | solution.py:24
  109.0 13.4 %all-to-all-start.1 = ((bf16[16,8,512]{2,1,0:T(8,128)(2,1)}), bf16[16,8,512]{2,1,0:T(8,128)(2,1)S(1)}, u32[]{:S(2)}, u32[]{:S(2)}) async-start(bf16[16,8,512]{2,1,0:T(8,128)(2,1)} %fusion.5), calls=%async_computation.1 | async-start | bytes 262144 | tf_op jit(solution)/shard_map/all_to_all | solution.py:24
  123.9 23.7 %all-to-all-start.2 = ((bf16[36,8,512]{2,1,0:T(8,128)(2,1)}), bf16[36,8,512]{2,1,0:T(8,128)(2,1)S(1)}, u32[]{:S(2)}, u32[]{:S(2)}) async-start(bf16[36,8,512]{2,1,0:T(8,128)(2,1)} %broadcast_select_fusion), calls=%async_computation.2 | async-start | bytes 589824 | tf_op jit(solution)/shard_map/all_to_all | solution.py:24

commit v2 on v1

v2 whole, which is shorter than its diff:
```python
import math

import jax
import jax.numpy as jnp
from jax import lax
from jax.experimental import pallas as pl
from jax.experimental.pallas import tpu as pltpu
from jax.sharding import Mesh
from jax.sharding import PartitionSpec as P

ITERS = 3
PAIR = 3
RING = ("da", "db")
TENSOR = ("ty", "tx", "tc")
HOLD = ("ty", "tc")
SPLIT = (8, 4, 2)
THIRDS = 3


decay_rate = 0.95
newton_a = 3.4445
newton_b = -4.775
newton_c = 2.0315
norm_eps = 1e-07


def exchange(pieces, axes):
    return lax.all_to_all(pieces, axes, split_axis=0, concat_axis=0, tiled=True)


def shifted(pieces, step):
    count = lax.axis_size(RING)
    return lax.ppermute(pieces, RING, [(i, (i + step) % count) for i in range(count)])


def ranks_of(labels):
    length = labels.shape[0]
    places = jnp.arange(length, dtype=jnp.int32)
    earlier = (labels[None, :] == labels[:, None]) & (places[None, :] < places[:, None])
    return jnp.sum(earlier.astype(jnp.int32), axis=1)


def join_kernel(where_ref, owners_ref, pieces_ref, momentum_ref, kept_ref, ahead_ref, behind_ref, found_ref, sems):
    weight = decay_rate * decay_rate / (1.0 + decay_rate)
    me, third = where_ref[0], where_ref[1]
    outs = (kept_ref, ahead_ref, behind_ref)
    quarters, _, per_group = pieces_ref.shape[:3]
    copies = []
    for step, out in enumerate(outs):
        which = lax.rem(third + step, THIRDS)
        for quarter in range(quarters):
            copies.append(
                pltpu.make_async_copy(
                    pieces_ref.at[quarter, which], out.at[quarter], sems.at[step * quarters + quarter]
                )
            )
    for copy in copies:
        copy.start()

    def look(place, count):
        found_ref[count] = place
        return count + (owners_ref[place] == me).astype(jnp.int32)

    total = lax.fori_loop(0, owners_ref.shape[0], look, 0, unroll=8)
    for copy in copies:
        copy.wait()

    def add(slot, carry):
        place = found_ref[slot]
        group = lax.div(place, per_group)
        inside = place - group * per_group
        quarter = lax.div(group, THIRDS)
        step = lax.rem(group - quarter * THIRDS - third + THIRDS, THIRDS)
        extra = weight * momentum_ref[slot].astype(jnp.float32)
        for index, out in enumerate(outs):

            @pl.when(step == index)
            def _():
                joined = out[quarter, inside].astype(jnp.float32) + extra
                out[quarter, inside] = joined.astype(out.dtype)

        return carry

    lax.fori_loop(0, total, add, 0)


def join_momentum(pieces, momentum, owners, where):
    quarters, thirds, *inside = pieces.shape
    out = jax.ShapeDtypeStruct((quarters, *inside), pieces.dtype)
    smem = pl.BlockSpec(memory_space=pltpu.SMEM)
    vmem = pl.BlockSpec(memory_space=pltpu.VMEM)
    return pl.pallas_call(
        join_kernel,
        out_shape=[out] * thirds,
        in_specs=[smem, smem, pl.BlockSpec(memory_space=pl.ANY), vmem],
        out_specs=[vmem] * thirds,
        scratch_shapes=[
            pltpu.SMEM((owners.shape[0] + 1,), jnp.int32),
            pltpu.SemaphoreType.DMA((thirds * quarters,)),
        ],
        cost_estimate=pl.CostEstimate(
            flops=2 * pieces.size, bytes_accessed=4 * pieces.size, transcendentals=0
        ),
        name="join_momentum",
    )(where, owners, pieces, momentum)


def iterate_kernel(slab_ref, pieces_ref, out_ref, wide_ref):
    count, piece_rows, width = pieces_ref.shape
    ty, tx, tc = SPLIT
    slab = count * piece_rows // tx
    square = jnp.zeros((piece_rows, width), jnp.float32)
    for y in range(ty):
        for x in range(tx):
            for c in range(tc):
                piece = pieces_ref[(y * tx + x) * tc + c].astype(jnp.float32)
                square = square + piece * piece
                row = x * slab + (y * tc + c) * piece_rows
                wide_ref[row : row + piece_rows, :] = piece
    blend = 1.0 + decay_rate
    total = jnp.sum(jnp.sum(square, axis=0, keepdims=True), axis=1, keepdims=True)
    scale = blend / (blend * jnp.sqrt(total) + norm_eps)
    wide_ref[...] = wide_ref[...] * scale

    def dot(left, right, across):
        return lax.dot_general(
            left, right, (((1,), (across,)), ((), ())), preferred_element_type=jnp.float32
        )

    narrow = lambda value: value.astype(jnp.bfloat16)
    for iteration in range(ITERS):
        last = iteration == ITERS - 1
        current = wide_ref[...]
        currents = narrow(current)
        if last:
            kept = wide_ref[pl.ds(slab_ref[0] * slab, slab), :]
            mine = dot(narrow(kept), currents, 1)
            squared = narrow(dot(currents, currents, 1))
            polynomial = newton_b * mine + newton_c * dot(narrow(mine), squared, 0)
        else:
            kept = current
            mine = dot(currents, currents, 1)
            squared = narrow(mine)
            polynomial = newton_b * mine + newton_c * dot(squared, squared, 0)
        following = newton_a * kept + dot(narrow(polynomial), currents, 0)
        if not last:
            wide_ref[...] = following
    result = following * math.sqrt(width)
    for piece in range(slab // piece_rows):
        rows = result[piece * piece_rows : (piece + 1) * piece_rows, :]
        out_ref[piece] = rows.astype(out_ref.dtype)


def iterate(pieces, slab_index):
    count, piece_rows, width = pieces.shape
    rows = count * piece_rows
    share = count // SPLIT[1]
    vmem = pl.BlockSpec(memory_space=pltpu.VMEM)
    return pl.pallas_call(
        iterate_kernel,
        out_shape=jax.ShapeDtypeStruct((share, piece_rows, width), pieces.dtype),
        in_specs=[pl.BlockSpec(memory_space=pltpu.SMEM), vmem],
        out_specs=vmem,
        scratch_shapes=[pltpu.VMEM((rows, width), jnp.float32)],
        cost_estimate=pl.CostEstimate(
            flops=3 * ITERS * 2 * rows * rows * width,
            bytes_accessed=4 * rows * width,
            transcendentals=0,
        ),
        name="iterate_block",
    )(slab_index, pieces)


def sum_at_holder(kept, ahead, behind):
    wide = lambda piece: piece.astype(jnp.float32)
    from_behind = shifted(ahead, 1)
    from_ahead = shifted(behind, -1)
    partial = (wide(kept) + wide(from_behind) + wide(from_ahead)).astype(jnp.bfloat16)
    return wide(exchange(partial, "da")).sum(axis=0).astype(jnp.bfloat16)


def body(gradients, momentum, owners):
    dp_count = lax.axis_size(RING)
    my_group = lax.axis_index(RING)
    tx_count = lax.axis_size("tx")
    pieces = gradients[0]
    blocks_all, piece_rows, width = pieces.shape
    per_group = blocks_all // dp_count
    capacity = momentum.shape[1]
    places = jnp.arange(blocks_all, dtype=jnp.int32)
    slot_rank = ranks_of(owners)
    slot_ids = jnp.arange(capacity, dtype=jnp.int32)
    mine = owners == my_group
    grouped = pieces.reshape(dp_count // THIRDS, THIRDS, per_group, piece_rows, width)
    where = jnp.stack([my_group, lax.axis_index("db")]).astype(jnp.int32)
    held = sum_at_holder(*join_momentum(grouped, momentum[0], owners, where))
    hold_rows = lax.axis_size("ty")
    copies = held.reshape(hold_rows, 1, -1, piece_rows, width)
    copies = jnp.broadcast_to(copies, (hold_rows, tx_count, *copies.shape[2:]))
    whole = exchange(copies.reshape(-1, piece_rows, width), TENSOR)
    slab_index = lax.axis_index("tx").astype(jnp.int32)[None]
    back = exchange(iterate(whole, slab_index), HOLD)
    groups = jnp.arange(dp_count, dtype=jnp.int32)
    held_owner = lax.dynamic_slice_in_dim(owners, my_group * per_group, per_group)
    held_rank = ranks_of(held_owner)
    held_places = jnp.arange(per_group, dtype=jnp.int32)
    pair_ids = jnp.arange(PAIR, dtype=jnp.int32)
    matched = (held_owner[:, None, None] == groups[None, :, None]) & (
        held_rank[:, None, None] == pair_ids[None, None, :]
    )
    source = jnp.sum(jnp.where(matched, held_places[:, None, None], 0), axis=0).reshape(-1)
    outgoing = jnp.take(back, source, axis=0, mode="clip")
    incoming = exchange(outgoing, RING)
    group_rank = ranks_of(owners * dp_count + places // per_group)
    position = places // per_group * PAIR + group_rank
    my_slots = mine[:, None] & (slot_rank[:, None] == slot_ids[None, :])
    occupied = jnp.any(my_slots, axis=0)
    arriving = jnp.sum(jnp.where(my_slots, position[:, None], 0), axis=0)
    chosen = jnp.take(incoming, arriving, axis=0, mode="clip").astype(jnp.float32)
    update = jnp.where(occupied[:, None, None], chosen, 0.0)
    return update[None]


def solution(mesh):
    split = Mesh(mesh.devices.reshape(-1, THIRDS, *SPLIT), (*RING, *TENSOR))
    in_specs = (P(RING, None, TENSOR, None), P(RING, None, TENSOR, None), P())
    out_specs = P(RING, None, TENSOR, None)
    return jax.shard_map(body, mesh=split, in_specs=in_specs, out_specs=out_specs, check_vma=False)
```

time: 150 us -> 136 us (0.907)
  starting transfers between devices: 64.1 us -> 42.3 us
  blocking collectives: 0 us -> 20.5 us
  matrix products: 15.7 us -> 0 us
  Pallas kernels: 0 us -> 9.13 us
  other arithmetic: 8.72 us -> 3.83 us
  local copies, waits for them, and re-layouts: 8.66 us -> 3.78 us
  waiting for transfers between devices: 50.9 us -> 54.9 us
    ppermute x8 -> x2, starting transfers between devices: 40.1 us -> 18 us  [shifted(): lax.ppermute(pieces, RING, [(i, (i + step) % count) for i in range(count)])]
    all_to_all x0 -> x1, blocking collectives: none -> 20.5 us  [exchange(): return lax.all_to_all(pieces, axes, split_axis=0, concat_axis=0, tiled=True)]
    dot_general x6 -> x0, matrix products: 15.7 us -> none  [the longest x3 9.69 us: iterate(): dot = lambda a, b: jnp.dot(a, b, preferred_element_type=jnp.float32)]
    pallas_call x0 -> x2, Pallas kernels: none -> 9.13 us  [the longest x1 4.93 us: iterate(): pl.pallas_call(iterate_kernel, out_shape=jax.ShapeDtypeStruct((share, pie...]
    gather x6 -> x2, local copies, waits for them, and re-layouts: 6.99 us -> 1.87 us  [the longest x1 1.3 us: body(): outgoing = jnp.take(back, source, axis=0, mode='clip')]
    ppermute x8 -> x2, waiting for transfers between devices: 9.99 us -> 13.9 us  [shifted(): lax.ppermute(pieces, RING, [(i, (i + step) % count) for i in range(count)])]
    convert_element_type x3 -> x1, other arithmetic: 3.22 us -> 1.25 us  [sum_at_holder(): (wide(kept) + wide(from_behind) + wide(from_ahead)).astype(jnp.bfloat16)]
    select_n x8 -> x0, other arithmetic: 1.55 us -> none  [the longest x2 0.83 us: body(): outgoing = jnp.take(back, source, axis=0)]
  transfers between devices with their start and end apart: 11 -> 5, of which waited for: 8 -> 5; matrix products, arithmetic and copies ran while one was open for 1% -> 1% of each run, Pallas kernels for 0% -> 0%
where the time goes in v2:
time: 136 us; the launch traced here: 135 us
  waiting for transfers between devices  54.9 us (40%)
  starting transfers between devices  42.3 us (31%)
  blocking collectives  20.5 us (15%)
  Pallas kernels  9.13 us (7%)
  other arithmetic  3.83 us (3%)
  local copies, waits for them, and re-layouts  3.78 us (3%)
    all_to_all x3, waiting for transfers between devices, exchange(): return lax.all_to_all(pieces, axes, split_axis=0, concat_axis=0, tiled=True)  41 us
    all_to_all x3, starting transfers between devices, exchange(): return lax.all_to_all(pieces, axes, split_axis=0, concat_axis=0, tiled=True)  24.3 us
    all_to_all x1, blocking collectives, exchange(): return lax.all_to_all(pieces, axes, split_axis=0, concat_axis=0, tiled=True)  20.5 us
    ppermute x2, starting transfers between devices, shifted(): lax.ppermute(pieces, RING, [(i, (i + step) % count) for i in range(count)])  18 us
    ppermute x2, waiting for transfers between devices, shifted(): lax.ppermute(pieces, RING, [(i, (i + step) % count) for i in range(count)])  13.9 us
    pallas_call x1, Pallas kernels, iterate(): pl.pallas_call(iterate_kernel, out_shape=jax.ShapeDtypeStruct((share, pie...  4.93 us
    pallas_call x1, Pallas kernels, join_momentum(): pl.pallas_call(join_kernel, out_shape=[out] * thirds, in_specs=[smem, sme...  4.2 us
  transfers between devices with their start and end apart: 5, of which 5 were waited for; matrix products, arithmetic and copies ran while one was open for 1% of the time, Pallas kernels for 0%

profile of v2, /device:TPU:1, one launch (start us, length us, event | category | flops | bytes accessed | tf_op | source)
XLA Modules:
  0.0 134.6 jit_solution(3537668657098216994)
XLA Ops:
  0.0 0.6 pad_add_fusion.where_ref
  0.6 4.2 %join_momentum.1 = (bf16[4,16,8,512]{3,2,1,0:T(8,128)(2,1)}, bf16[4,16,8,512]{3,2,1,0:T(8,128)(2,1)}, bf16[4,16,8,512]{3,2,1,0:T(8,128)(2,1)}) custom-call(s32[2]{0:T(128)} %pad_add_fusion.where_ref, s32[192]{0:T(256)} %owners_ref.1, bf16[4,3,16,8,512]{4,3,2,1,0:T(8,128)(2,1)} %bitcast.10, bf16[36,8,512]{2,1,0:T(8,128)(2,1)} %bitcast.12), custom_call_target="tpu_custom_call" | custom-call | flops 1572864 | bytes 3145728 | tf_op jit(solution)/shard_map/join_momentum/pallas_call | solution.py:92
  4.8 16.0 %collective-permute-start.1 = (bf16[4,16,8,512]{3,2,1,0:T(8,128)(2,1)}, bf16[4,16,8,512]{3,2,1,0:T(8,128)(2,1)S(1)}, u32[]{:S(2)}, u32[]{:S(2)}) collective-permute-start(bf16[4,16,8,512]{3,2,1,0:T(8,128)(2,1)} %get-tuple-element.10), channel_id=1, source_target_pairs={{0,704},{64,0},{128,64},{192,128},{256,192},{320,256},{384,320},{4... | collective-permute-start | bytes 1572872 | tf_op jit(solution)/shard_map/ppermute | solution.py:33
  20.8 1.9 %collective-permute-start = (bf16[4,16,8,512]{3,2,1,0:T(8,128)(2,1)}, bf16[4,16,8,512]{3,2,1,0:T(8,128)(2,1)S(1)}, u32[]{:S(2)}, u32[]{:S(2)}) collective-permute-start(bf16[4,16,8,512]{3,2,1,0:T(8,128)(2,1)} %get-tuple-element.9), channel_id=1, source_target_pairs={{0,64},{64,128},{128,192},{192,256},{256,320},{320,384},{384,448},... | collective-permute-start | bytes 1572872 | tf_op jit(solution)/shard_map/ppermute | solution.py:33
  22.8 9.0 %collective-permute-done.1 = bf16[4,16,8,512]{3,2,1,0:T(8,128)(2,1)S(1)} collective-permute-done((bf16[4,16,8,512]{3,2,1,0:T(8,128)(2,1)}, bf16[4,16,8,512]{3,2,1,0:T(8,128)(2,1)S(1)}, u32[]{:S(2)}, u32[]{:S(2)}) %collective-permute-start.1) | collective-permute-done | bytes 524320 | tf_op jit(solution)/shard_map/ppermute | solution.py:33
  31.8 4.9 %collective-permute-done = bf16[4,16,8,512]{3,2,1,0:T(8,128)(2,1)S(1)} collective-permute-done((bf16[4,16,8,512]{3,2,1,0:T(8,128)(2,1)}, bf16[4,16,8,512]{3,2,1,0:T(8,128)(2,1)S(1)}, u32[]{:S(2)}, u32[]{:S(2)}) %collective-permute-start) | collective-permute-done | bytes 524320 | tf_op jit(solution)/shard_map/ppermute | solution.py:33
  36.7 1.2 add_convert_fusion
  37.9 0.0 copy-start.1
  38.0 20.5 %all_to_all.20 = bf16[4,16,8,512]{3,2,1,0:T(8,128)(2,1)S(1)} all-to-all(bf16[4,16,8,512]{3,2,1,0:T(8,128)(2,1)S(1)} %add_convert_fusion), channel_id=1, replica_groups=mesh['da'=4,'db'=3,'ty'=8,'tx'=4,'tc'=2] {'da'}, dimensions={0} | all-to-all | bytes 1048576 | tf_op jit(solution)/shard_map/all_to_all | solution.py:28
  58.5 0.1 reduce_sum.58
  58.5 0.9 broadcast_in_dim.49
  59.4 16.2 %all-to-all-start.1 = ((bf16[64,8,512]{2,1,0:T(8,128)(2,1)}), bf16[64,8,512]{2,1,0:T(8,128)(2,1)S(1)}, u32[]{:S(2)}, u32[]{:S(2)}) async-start(bf16[64,8,512]{2,1,0:T(8,128)(2,1)} %bitcast.6), calls=%async_computation.1 | async-start | bytes 1048576 | tf_op jit(solution)/shard_map/all_to_all | solution.py:28
  75.6 0.1 dynamic_slice.3
  75.7 0.2 convert_reduce_fusion.2
  75.9 0.1 iota_compare_fusion.3
  76.0 0.1 select_reduce_fusion.1
  76.0 0.1 copy.4
  76.1 0.1 reshape.95
  76.2 0.2 convert_reduce_fusion.1
  76.4 16.9 %all-to-all-done.1.pieces_ref = bf16[64,8,512]{2,1,0:T(8,128)(2,1)S(1)} async-done(((bf16[64,8,512]{2,1,0:T(8,128)(2,1)}), bf16[64,8,512]{2,1,0:T(8,128)(2,1)S(1)}, u32[]{:S(2)}, u32[]{:S(2)}) %all-to-all-start.1) | async-done | bytes 524320 | tf_op jit(solution)/shard_map/all_to_all | solution.py:28
  93.3 0.8 copy-done
  94.1 4.9 %iterate_block.1 = bf16[16,8,512]{2,1,0:T(8,128)(2,1)} custom-call(s32[1]{0:T(128)} %bitcast.slab_ref, bf16[64,8,512]{2,1,0:T(8,128)(2,1)} %copy-done), custom_call_target="tpu_custom_call" | custom-call | flops 2415919104 | bytes 1048576 | tf_op jit(solution)/shard_map/iterate_block/pallas_call | solution.py:159
  99.0 4.6 %all-to-all-start.2 = ((bf16[16,8,512]{2,1,0:T(8,128)(2,1)}), bf16[16,8,512]{2,1,0:T(8,128)(2,1)S(1)}, u32[]{:S(2)}, u32[]{:S(2)}) async-start(bf16[16,8,512]{2,1,0:T(8,128)(2,1)} %iterate_block.1), calls=%async_computation.2 | async-start | bytes 262144 | tf_op jit(solution)/shard_map/all_to_all | solution.py:28
  103.6 8.9 %all-to-all-done.2 = bf16[16,8,512]{2,1,0:T(8,128)(2,1)S(1)} async-done(((bf16[16,8,512]{2,1,0:T(8,128)(2,1)}), bf16[16,8,512]{2,1,0:T(8,128)(2,1)S(1)}, u32[]{:S(2)}, u32[]{:S(2)}) %all-to-all-start.2) | async-done | bytes 131104 | tf_op jit(solution)/shard_map/all_to_all | solution.py:28
  112.5 1.3 gather_fusion
  113.7 3.5 %all-to-all-start.3 = ((bf16[36,8,512]{2,1,0:T(8,128)(2,1)}), bf16[36,8,512]{2,1,0:T(8,128)(2,1)S(1)}, u32[]{:S(2)}, u32[]{:S(2)}) async-start(bf16[36,8,512]{2,1,0:T(8,128)(2,1)} %gather_fusion), calls=%async_computation.3 | async-start | bytes 589824 | tf_op jit(solution)/shard_map/all_to_all | solution.py:28
  117.3 0.2 convert_reduce_fusion
  117.5 0.1 select_reduce_fusion
  117.6 0.1 fusion.3
  117.8 15.3 %all-to-all-done.3 = bf16[36,8,512]{2,1,0:T(8,128)(2,1)S(1)} async-done(((bf16[36,8,512]{2,1,0:T(8,128)(2,1)}), bf16[36,8,512]{2,1,0:T(8,128)(2,1)S(1)}, u32[]{:S(2)}, u32[]{:S(2)}) %all-to-all-start.3) | async-done | bytes 294944 | tf_op jit(solution)/shard_map/all_to_all | solution.py:28
  133.0 0.6 gather_fusion.1
  133.6 0.9 convert_select_fusion
  (8 shorter events, 0.0 us)
Async XLA Ops:
  4.8 27.0 %collective-permute-start.1 = (bf16[4,16,8,512]{3,2,1,0:T(8,128)(2,1)}, bf16[4,16,8,512]{3,2,1,0:T(8,128)(2,1)S(1)}, u32[]{:S(2)}, u32[]{:S(2)}) collective-permute-start(bf16[4,16,8,512]{3,2,1,0:T(8,128)(2,1)} %get-tuple-element.10), channel_id=1, source_target_pairs={{0,704},{64,0},{128,64},{192,128},{256,192},{320,256},{384,320},{4... | collective-permute-start | bytes 1572872 | tf_op jit(solution)/shard_map/ppermute | solution.py:33
  20.8 15.8 %collective-permute-start = (bf16[4,16,8,512]{3,2,1,0:T(8,128)(2,1)}, bf16[4,16,8,512]{3,2,1,0:T(8,128)(2,1)S(1)}, u32[]{:S(2)}, u32[]{:S(2)}) collective-permute-start(bf16[4,16,8,512]{3,2,1,0:T(8,128)(2,1)} %get-tuple-element.9), channel_id=1, source_target_pairs={{0,64},{64,128},{128,192},{192,256},{256,320},{320,384},{384,448},... | collective-permute-start | bytes 1572872 | tf_op jit(solution)/shard_map/ppermute | solution.py:33
  37.9 37.7 %copy-start.1 = (s32[192]{0:T(256)S(1)}, s32[192]{0:T(256)}, u32[]{:S(2)}) copy-start(s32[192]{0:T(256)} %owners_ref.1) | copy-start | bytes 2308
  59.4 33.9 %all-to-all-start.1 = ((bf16[64,8,512]{2,1,0:T(8,128)(2,1)}), bf16[64,8,512]{2,1,0:T(8,128)(2,1)S(1)}, u32[]{:S(2)}, u32[]{:S(2)}) async-start(bf16[64,8,512]{2,1,0:T(8,128)(2,1)} %bitcast.6), calls=%async_computation.1 | async-start | bytes 1048576 | tf_op jit(solution)/shard_map/all_to_all | solution.py:28
  93.3 0.8 copy-start
  99.0 13.5 %all-to-all-start.2 = ((bf16[16,8,512]{2,1,0:T(8,128)(2,1)}), bf16[16,8,512]{2,1,0:T(8,128)(2,1)S(1)}, u32[]{:S(2)}, u32[]{:S(2)}) async-start(bf16[16,8,512]{2,1,0:T(8,128)(2,1)} %iterate_block.1), calls=%async_computation.2 | async-start | bytes 262144 | tf_op jit(solution)/shard_map/all_to_all | solution.py:28
  113.7 19.3 %all-to-all-start.3 = ((bf16[36,8,512]{2,1,0:T(8,128)(2,1)}), bf16[36,8,512]{2,1,0:T(8,128)(2,1)S(1)}, u32[]{:S(2)}, u32[]{:S(2)}) async-start(bf16[36,8,512]{2,1,0:T(8,128)(2,1)} %gather_fusion), calls=%async_computation.3 | async-start | bytes 589824 | tf_op jit(solution)/shard_map/all_to_all | solution.py:28

commit v3 on v2

v3 whole, which is shorter than its diff:
```python
import math

import jax
import jax.numpy as jnp
from jax import lax
from jax.experimental import pallas as pl
from jax.experimental.pallas import tpu as pltpu
from jax.sharding import Mesh
from jax.sharding import PartitionSpec as P

ITERS = 3
PAIR = 3
RING = ("da", "db")
TENSOR = ("ty", "tx", "tc")
HOLD = ("ty", "tc")
SPLIT = (8, 4, 2)
FOURTHS = 4
PARTS = 2
VMEM_LIMIT = 12 * 1024 * 1024


decay_rate = 0.95
newton_a = 3.4445
newton_b = -4.775
newton_c = 2.0315
norm_eps = 1e-07


def exchange(pieces, axes):
    return lax.all_to_all(pieces, axes, split_axis=0, concat_axis=0, tiled=True)


def shifted(pieces, step):
    count = lax.axis_size(RING)
    return lax.ppermute(pieces, RING, [(i, (i + step) % count) for i in range(count)])


def mirrored(pieces, step):
    count, cores = lax.axis_size(RING), lax.axis_size("tc")
    signs = [step if core else -step for core in range(cores)]
    pairs = [
        (i * cores + core, (i + signs[core]) % count * cores + core)
        for i in range(count)
        for core in range(cores)
    ]
    return lax.ppermute(pieces, (*RING, "tc"), pairs)


def ranks_of(labels):
    length = labels.shape[0]
    places = jnp.arange(length, dtype=jnp.int32)
    earlier = (labels[None, :] == labels[:, None]) & (places[None, :] < places[:, None])
    return jnp.sum(earlier.astype(jnp.int32), axis=1)


def join_kernel(owners_ref, pieces_ref, momentum_ref, *refs):
    *outs, found_ref, sems = refs
    weight = decay_rate * decay_rate / (1.0 + decay_rate)
    fourth = lax.axis_index(RING[1])
    me = lax.axis_index(RING[0]) * FOURTHS + fourth
    trios, _, per_group = pieces_ref.shape[:3]
    width = outs[0].shape[-1]
    copies = []
    for part in range(PARTS):
        columns = pl.ds(part * width, width)
        for step in (1, 3, 2, 0):
            which = lax.rem(fourth + step, FOURTHS)
            for trio in range(trios):
                copies.append(
                    pltpu.make_async_copy(
                        pieces_ref.at[trio, which, :, :, columns],
                        outs[part * FOURTHS + step].at[trio],
                        sems.at[len(copies)],
                    )
                )
    for copy in copies:
        copy.start()

    def look(place, count):
        found_ref[count] = place
        return count + (owners_ref[place] == me).astype(jnp.int32)

    total = lax.fori_loop(0, owners_ref.shape[0], look, 0, unroll=8)
    for copy in copies:
        copy.wait()

    def add(slot, carry):
        place = found_ref[slot]
        group = lax.div(place, per_group)
        inside = place - group * per_group
        trio = lax.div(group, FOURTHS)
        step = lax.rem(group - trio * FOURTHS - fourth + FOURTHS, FOURTHS)
        extra = weight * momentum_ref[slot].astype(jnp.float32)
        for index in range(FOURTHS):

            @pl.when(step == index)
            def _():
                for part in range(PARTS):
                    out = outs[part * FOURTHS + index]
                    term = extra[:, part * width : (part + 1) * width]
                    joined = out[trio, inside].astype(jnp.float32) + term
                    out[trio, inside] = joined.astype(out.dtype)

        return carry

    lax.fori_loop(0, total, add, 0)


def join_momentum(pieces, momentum, owners):
    trios, fourths, *inside, width = pieces.shape
    out = jax.ShapeDtypeStruct((trios, *inside, width // PARTS), pieces.dtype)
    vmem = pl.BlockSpec(memory_space=pltpu.VMEM)
    outs = pl.pallas_call(
        join_kernel,
        out_shape=[out] * (fourths * PARTS),
        in_specs=[
            pl.BlockSpec(memory_space=pltpu.SMEM),
            pl.BlockSpec(memory_space=pl.ANY),
            vmem,
        ],
        out_specs=[vmem] * (fourths * PARTS),
        scratch_shapes=[
            pltpu.SMEM((owners.shape[0] + 1,), jnp.int32),
            pltpu.SemaphoreType.DMA((fourths * PARTS * trios,)),
        ],
        cost_estimate=pl.CostEstimate(
            flops=2 * pieces.size, bytes_accessed=4 * pieces.size, transcendentals=0
        ),
        name="join_momentum",
        compiler_params=pltpu.CompilerParams(vmem_limit_bytes=VMEM_LIMIT),
    )(owners, pieces, momentum)
    return [outs[part * fourths : (part + 1) * fourths] for part in range(PARTS)]


def combine_kernel(kept_ref, one_ref, two_ref, three_ref, own_ref, ahead_ref, behind_ref):
    trios, blocks = kept_ref.shape[:2]
    me = lax.axis_index(RING[0])
    for step, out in enumerate((own_ref, ahead_ref, behind_ref)):
        which = lax.rem(me + step, trios)
        for block in range(blocks):
            total = kept_ref[which, block].astype(jnp.float32)
            for ref in (one_ref, two_ref, three_ref):
                total = total + ref[which, block].astype(jnp.float32)
            out[block] = total.astype(out.dtype)


def combine(kept, *arrived):
    trios, *inside = kept.shape
    vmem = pl.BlockSpec(memory_space=pltpu.VMEM)
    own = jax.ShapeDtypeStruct(tuple(inside), jnp.float32)
    sent = jax.ShapeDtypeStruct(tuple(inside), kept.dtype)
    return pl.pallas_call(
        combine_kernel,
        out_shape=[own, sent, sent],
        in_specs=[vmem] * 4,
        out_specs=[vmem] * 3,
        cost_estimate=pl.CostEstimate(
            flops=4 * kept.size, bytes_accessed=8 * kept.size, transcendentals=0
        ),
        name="combine_terms",
        compiler_params=pltpu.CompilerParams(vmem_limit_bytes=VMEM_LIMIT),
    )(kept, *arrived)


def spread_kernel(own_ref, ahead_ref, behind_ref, out_ref):
    _, tx, tc = SPLIT
    for block in range(own_ref.shape[0]):
        total = own_ref[block] + (
            ahead_ref[block].astype(jnp.float32) + behind_ref[block].astype(jnp.float32)
        )
        total = total.astype(out_ref.dtype)
        for x in range(tx):
            out_ref[(block // tc * tx + x) * tc + block % tc] = total


def spread(own, ahead, behind):
    blocks, *inside = own.shape
    vmem = pl.BlockSpec(memory_space=pltpu.VMEM)
    return pl.pallas_call(
        spread_kernel,
        out_shape=jax.ShapeDtypeStruct((blocks * SPLIT[1], *inside), ahead.dtype),
        in_specs=[vmem] * 3,
        out_specs=vmem,
        cost_estimate=pl.CostEstimate(
            flops=4 * own.size, bytes_accessed=8 * own.size, transcendentals=0
        ),
        name="spread_sum",
        compiler_params=pltpu.CompilerParams(vmem_limit_bytes=VMEM_LIMIT),
    )(own, ahead, behind)


def iterate_kernel(*refs):
    *ins, out_ref, wide_ref = refs
    count, piece_rows, part_width = ins[0].shape
    width = PARTS * part_width
    ty, tx, tc = SPLIT
    slab = count * piece_rows // tx
    square = jnp.zeros((piece_rows, part_width), jnp.float32)
    for part in range(PARTS):
        for y in range(ty):
            for x in range(tx):
                for c in range(tc):
                    piece = ins[part][(y * tx + x) * tc + c].astype(jnp.float32)
                    square = square + piece * piece
                    row = x * slab + (y * tc + c) * piece_rows
                    wide_ref[
                        row : row + piece_rows, part * part_width : (part + 1) * part_width
                    ] = piece
    blend = 1.0 + decay_rate
    total = jnp.sum(jnp.sum(square, axis=0, keepdims=True), axis=1, keepdims=True)
    scale = blend / (blend * jnp.sqrt(total) + norm_eps)
    wide_ref[...] = wide_ref[...] * scale

    def dot(left, right, across):
        return lax.dot_general(
            left, right, (((1,), (across,)), ((), ())), preferred_element_type=jnp.float32
        )

    narrow = lambda value: value.astype(jnp.bfloat16)
    for iteration in range(ITERS):
        last = iteration == ITERS - 1
        current = wide_ref[...]
        currents = narrow(current)
        if last:
            kept = wide_ref[pl.ds(lax.axis_index("tx") * slab, slab), :]
            mine = dot(narrow(kept), currents, 1)
            squared = narrow(dot(currents, currents, 1))
            polynomial = newton_b * mine + newton_c * dot(narrow(mine), squared, 0)
        else:
            kept = current
            mine = dot(currents, currents, 1)
            squared = narrow(mine)
            polynomial = newton_b * mine + newton_c * dot(squared, squared, 0)
        following = newton_a * kept + dot(narrow(polynomial), currents, 0)
        if not last:
            wide_ref[...] = following
    result = following * math.sqrt(width)
    for piece in range(slab // piece_rows):
        rows = result[piece * piece_rows : (piece + 1) * piece_rows, :]
        out_ref[piece] = rows.astype(out_ref.dtype)


def iterate(parts):
    count, piece_rows, part_width = parts[0].shape
    rows, width = count * piece_rows, part_width * PARTS
    vmem = pl.BlockSpec(memory_space=pltpu.VMEM)
    return pl.pallas_call(
        iterate_kernel,
        out_shape=jax.ShapeDtypeStruct((count // SPLIT[1], piece_rows, width), parts[0].dtype),
        in_specs=[vmem] * PARTS,
        out_specs=vmem,
        scratch_shapes=[pltpu.VMEM((rows, width), jnp.float32)],
        cost_estimate=pl.CostEstimate(
            flops=3 * ITERS * 2 * rows * rows * width,
            bytes_accessed=4 * rows * width,
            transcendentals=0,
        ),
        name="iterate_block",
        compiler_params=pltpu.CompilerParams(vmem_limit_bytes=VMEM_LIMIT),
    )(*parts)


def sum_at_holder(kept, ahead, two, behind):
    arrived = (shifted(ahead, 1), shifted(behind, -1), mirrored(two, 2))
    own, to_ahead, to_behind = combine(kept, *arrived)
    arrived = (shifted(to_ahead, FOURTHS), shifted(to_behind, -FOURTHS))
    return spread(own, *arrived)


def body(gradients, momentum, owners):
    dp_count = lax.axis_size(RING)
    my_group = lax.axis_index(RING)
    pieces = gradients[0]
    blocks_all, piece_rows, width = pieces.shape
    per_group = blocks_all // dp_count
    capacity = momentum.shape[1]
    places = jnp.arange(blocks_all, dtype=jnp.int32)
    slot_rank = ranks_of(owners)
    slot_ids = jnp.arange(capacity, dtype=jnp.int32)
    mine = owners == my_group
    grouped = pieces.reshape(dp_count // FOURTHS, FOURTHS, per_group, piece_rows, width)
    joined = join_momentum(grouped, momentum[0], owners)
    whole = []
    for part in joined:
        whole.append(exchange(sum_at_holder(*part), TENSOR))
    back = exchange(iterate(whole), HOLD)
    groups = jnp.arange(dp_count, dtype=jnp.int32)
    held_owner = lax.dynamic_slice_in_dim(owners, my_group * per_group, per_group)
    held_rank = ranks_of(held_owner)
    held_places = jnp.arange(per_group, dtype=jnp.int32)
    pair_ids = jnp.arange(PAIR, dtype=jnp.int32)
    matched = (held_owner[:, None, None] == groups[None, :, None]) & (
        held_rank[:, None, None] == pair_ids[None, None, :]
    )
    source = jnp.sum(jnp.where(matched, held_places[:, None, None], 0), axis=0).reshape(-1)
    incoming = exchange(jnp.take(back, source, axis=0, mode="clip"), RING)
    group_rank = ranks_of(owners * dp_count + places // per_group)
    position = places // per_group * PAIR + group_rank
    my_slots = mine[:, None] & (slot_rank[:, None] == slot_ids[None, :])
    occupied = jnp.any(my_slots, axis=0)
    arriving = jnp.sum(jnp.where(my_slots, position[:, None], 0), axis=0)
    chosen = jnp.take(incoming, arriving, axis=0, mode="clip").astype(jnp.float32)
    update = jnp.where(occupied[:, None, None], chosen, 0.0)
    return update[None]


def solution(mesh):
    split = Mesh(mesh.devices.reshape(-1, FOURTHS, *SPLIT), (*RING, *TENSOR))
    in_specs = (P(RING, None, TENSOR, None), P(RING, None, TENSOR, None), P())
    out_specs = P(RING, None, TENSOR, None)
    return jax.shard_map(body, mesh=split, in_specs=in_specs, out_specs=out_specs, check_vma=False)
```

time: 136 us -> 161 us (1.18)
  starting transfers between devices: 42.3 us -> 83.8 us
  blocking collectives: 20.5 us -> 0 us
  waiting for transfers between devices: 54.9 us -> 61.3 us
  other arithmetic: 3.83 us -> 1.91 us
    ppermute x2 -> x8, starting transfers between devices: 18 us -> 42 us  [shifted(): lax.ppermute(pieces, RING, [(i, (i + step) % count) for i in range(count)])]
    all_to_all x1 -> x0, blocking collectives: 20.5 us -> none  [exchange(): return lax.all_to_all(pieces, axes, split_axis=0, concat_axis=0, tiled=True)]
    all_to_all x3 -> x4, starting transfers between devices: 24.3 us -> 36.7 us  [exchange(): return lax.all_to_all(pieces, axes, split_axis=0, concat_axis=0, tiled=True)]
    ppermute x0 -> x2, waiting for transfers between devices: none -> 11.7 us  [mirrored(): return lax.ppermute(pieces, (*RING, 'tc'), pairs)]
    ppermute x0 -> x2, starting transfers between devices: none -> 5.06 us  [mirrored(): return lax.ppermute(pieces, (*RING, 'tc'), pairs)]
    all_to_all x3 -> x4, waiting for transfers between devices: 41 us -> 36.5 us  [exchange(): return lax.all_to_all(pieces, axes, split_axis=0, concat_axis=0, tiled=True)]
    unnamed x4 -> x8, local copies, waits for them, and re-layouts: 0.8 us -> 3.05 us
    pallas_call x2 -> x6, Pallas kernels: 9.13 us -> 7.59 us  [the longest x1 3.86 us: iterate(): pl.pallas_call(iterate_kernel, out_shape=jax.ShapeDtypeStruct((count // S...]
  transfers between devices with their start and end apart: 5 -> 14, of which waited for: 5 -> 11; matrix products, arithmetic and copies ran while one was open for 1% -> 1% of each run, Pallas kernels for 0% -> 1%
where the time goes in v3:
time: 161 us; the launch traced here: 160 us
  starting transfers between devices  83.8 us (52%)
  waiting for transfers between devices  61.3 us (38%)
  Pallas kernels  7.59 us (5%)
  local copies, waits for them, and re-layouts  5.18 us (3%)
  other arithmetic  1.91 us (1%)
    ppermute x8, starting transfers between devices, shifted(): lax.ppermute(pieces, RING, [(i, (i + step) % count) for i in range(count)])  42 us
    all_to_all x4, starting transfers between devices, exchange(): return lax.all_to_all(pieces, axes, split_axis=0, concat_axis=0, tiled=True)  36.7 us
    all_to_all x4, waiting for transfers between devices, exchange(): return lax.all_to_all(pieces, axes, split_axis=0, concat_axis=0, tiled=True)  36.5 us
    ppermute x8, waiting for transfers between devices, shifted(): lax.ppermute(pieces, RING, [(i, (i + step) % count) for i in range(count)])  13.2 us
    ppermute x2, waiting for transfers between devices, mirrored(): return lax.ppermute(pieces, (*RING, 'tc'), pairs)  11.7 us
    ppermute x2, starting transfers between devices, mirrored(): return lax.ppermute(pieces, (*RING, 'tc'), pairs)  5.06 us
    pallas_call x1, Pallas kernels, iterate(): pl.pallas_call(iterate_kernel, out_shape=jax.ShapeDtypeStruct((count // S...  3.86 us
  transfers between devices with their start and end apart: 14, of which 11 were waited for; matrix products, arithmetic and copies ran while one was open for 1% of the time, Pallas kernels for 1%

profile of v3, /device:TPU:1, one launch (start us, length us, event | category | flops | bytes accessed | tf_op | source)
XLA Modules:
  0.0 160.0 jit_solution(14558672664680884576)
XLA Ops:
  0.0 1.4 copy-done
  1.4 1.0 copy-done.1
  3.1 2.1 %join_momentum.1 = (bf16[3,16,8,256]{3,2,1,0:T(8,128)(2,1)S(1)}, bf16[3,16,8,256]{3,2,1,0:T(8,128)(2,1)S(1)}, bf16[3,16,8,256]{3,2,1,0:T(8,128)(2,1)S(1)}, bf16[...) custom-call(s32[192]{0:T(256)S(1)} %copy-done.2, ...), custom_call_target="tpu_custom_call" | custom-call | flops 1572864 | bytes 3145728 | tf_op jit(solution)/shard_map/join_momentum/pallas_call | solution.py:113
  5.2 4.7 %collective-permute-start.5 = (bf16[3,16,8,256]{3,2,1,0:T(8,128)(2,1)S(1)}, bf16[3,16,8,256]{3,2,1,0:T(8,128)(2,1)S(1)}, u32[]{:S(2)}, u32[]{:S(2)}) collective-permute-start(bf16[3,16,8,256]{3,2,1,0:T(8,128)(2,1)S(1)} %get-tuple-element.27), channel_id=1, source_target_pairs={{0,64},{64,128},{128,192},{192,256},{256,320},{320,384},{384,448},... | collective-permute-start | bytes 589832 | tf_op jit(solution)/shard_map/ppermute | solution.py:35
  9.9 12.4 %collective-permute-start.6 = (bf16[3,16,8,256]{3,2,1,0:T(8,128)(2,1)S(1)}, bf16[3,16,8,256]{3,2,1,0:T(8,128)(2,1)S(1)}, u32[]{:S(2)}, u32[]{:S(2)}) collective-permute-start(bf16[3,16,8,256]{3,2,1,0:T(8,128)(2,1)S(1)} %get-tuple-element.28), channel_id=1, source_target_pairs={{0,704},{64,0},{128,64},{192,128},{256,192},{320,256},{384,320},{4... | collective-permute-start | bytes 589832 | tf_op jit(solution)/shard_map/ppermute | solution.py:35
  22.3 1.9 %collective-permute-start.7 = (bf16[3,16,8,256]{3,2,1,0:T(8,128)(2,1)S(1)}, bf16[3,16,8,256]{3,2,1,0:T(8,128)(2,1)S(1)}, u32[]{:S(2)}, u32[]{:S(2)}) collective-permute-start(bf16[3,16,8,256]{3,2,1,0:T(8,128)(2,1)S(1)} %get-tuple-element.29), channel_id=1, source_target_pairs={{0,640},{1,129},{64,704},{65,193},{128,0},{129,257},{192,64},{193,... | collective-permute-start | bytes 589832 | tf_op jit(solution)/shard_map/ppermute | solution.py:46
  24.3 0.7 collective-permute-done.5.one_ref
  25.0 0.9 collective-permute-done.6.two_ref
  25.9 7.1 %collective-permute-done.7.three_ref = bf16[3,16,8,256]{3,2,1,0:T(8,128)(2,1)S(1)} collective-permute-done((bf16[3,16,8,256]{3,2,1,0:T(8,128)(2,1)S(1)}, bf16[3,16,8,256]{3,2,1,0:T(8,128)(2,1)S(1)}, u32[]{:S(2)}, u32[]{:S(2)}) %collective-permute-start.7) | collective-permute-done | bytes 196640 | tf_op jit(solution)/shard_map/ppermute | solution.py:46
  33.1 1.9 %collective-permute-start.8 = (bf16[16,8,256]{2,1,0:T(8,128)(2,1)S(1)}, bf16[16,8,256]{2,1,0:T(8,128)(2,1)S(1)}, u32[]{:S(2)}, u32[]{:S(2)}) collective-permute-start(bf16[16,8,256]{2,1,0:T(8,128)(2,1)S(1)} %get-tuple-element.31), channel_id=1, source_target_pairs={{0,256},{64,320},{128,384},{192,448},{256,512},{320,576},{384,640}... | collective-permute-start | bytes 196616 | tf_op jit(solution)/shard_map/ppermute | solution.py:35
  35.0 7.3 %collective-permute-start.9 = (bf16[16,8,256]{2,1,0:T(8,128)(2,1)S(1)}, bf16[16,8,256]{2,1,0:T(8,128)(2,1)S(1)}, u32[]{:S(2)}, u32[]{:S(2)}) collective-permute-start(bf16[16,8,256]{2,1,0:T(8,128)(2,1)S(1)} %get-tuple-element.32), channel_id=1, source_target_pairs={{0,512},{64,576},{128,640},{192,704},{256,0},{320,64},{384,128},{4... | collective-permute-start | bytes 196616 | tf_op jit(solution)/shard_map/ppermute | solution.py:35
  42.3 2.4 %collective-permute-done.8.ahead_ref = bf16[16,8,256]{2,1,0:T(8,128)(2,1)S(1)} collective-permute-done((bf16[16,8,256]{2,1,0:T(8,128)(2,1)S(1)}, bf16[16,8,256]{2,1,0:T(8,128)(2,1)S(1)}, u32[]{:S(2)}, u32[]{:S(2)}) %collective-permute-start.8) | collective-permute-done | bytes 65568 | tf_op jit(solution)/shard_map/ppermute | solution.py:35
  44.6 0.7 spread_sum.3
  45.4 14.3 %all-to-all-start.1 = ((bf16[64,8,256]{2,1,0:T(8,128)(2,1)}), bf16[64,8,256]{2,1,0:T(8,128)(2,1)S(1)}, u32[]{:S(2)}, u32[]{:S(2)}) async-start(bf16[64,8,256]{2,1,0:T(8,128)(2,1)} %spread_sum.3), calls=%async_computation.1 | async-start | bytes 524288 | tf_op jit(solution)/shard_map/all_to_all | solution.py:30
  59.7 1.9 %collective-permute-start = (bf16[3,16,8,256]{3,2,1,0:T(8,128)(2,1)S(1)}, bf16[3,16,8,256]{3,2,1,0:T(8,128)(2,1)S(1)}, u32[]{:S(2)}, u32[]{:S(2)}) collective-permute-start(bf16[3,16,8,256]{3,2,1,0:T(8,128)(2,1)S(1)} %get-tuple-element.20), channel_id=1, source_target_pairs={{0,64},{64,128},{128,192},{192,256},{256,320},{320,384},{384,448},... | collective-permute-start | bytes 589832 | tf_op jit(solution)/shard_map/ppermute | solution.py:35
  61.6 4.6 %collective-permute-start.1 = (bf16[3,16,8,256]{3,2,1,0:T(8,128)(2,1)S(1)}, bf16[3,16,8,256]{3,2,1,0:T(8,128)(2,1)S(1)}, u32[]{:S(2)}, u32[]{:S(2)}) collective-permute-start(bf16[3,16,8,256]{3,2,1,0:T(8,128)(2,1)S(1)} %get-tuple-element.21), channel_id=1, source_target_pairs={{0,704},{64,0},{128,64},{192,128},{256,192},{320,256},{384,320},{4... | collective-permute-start | bytes 589832 | tf_op jit(solution)/shard_map/ppermute | solution.py:35
  66.2 3.1 %collective-permute-start.2 = (bf16[3,16,8,256]{3,2,1,0:T(8,128)(2,1)S(1)}, bf16[3,16,8,256]{3,2,1,0:T(8,128)(2,1)S(1)}, u32[]{:S(2)}, u32[]{:S(2)}) collective-permute-start(bf16[3,16,8,256]{3,2,1,0:T(8,128)(2,1)S(1)} %get-tuple-element.22), channel_id=1, source_target_pairs={{0,640},{1,129},{64,704},{65,193},{128,0},{129,257},{192,64},{193,... | collective-permute-start | bytes 589832 | tf_op jit(solution)/shard_map/ppermute | solution.py:46
  69.5 1.3 collective-permute-done.1.two_ref
  70.8 4.6 %collective-permute-done.2.three_ref = bf16[3,16,8,256]{3,2,1,0:T(8,128)(2,1)S(1)} collective-permute-done((bf16[3,16,8,256]{3,2,1,0:T(8,128)(2,1)S(1)}, bf16[3,16,8,256]{3,2,1,0:T(8,128)(2,1)S(1)}, u32[]{:S(2)}, u32[]{:S(2)}) %collective-permute-start.2) | collective-permute-done | bytes 196640 | tf_op jit(solution)/shard_map/ppermute | solution.py:46
  75.5 5.9 %collective-permute-start.3 = (bf16[16,8,256]{2,1,0:T(8,128)(2,1)S(1)}, bf16[16,8,256]{2,1,0:T(8,128)(2,1)S(1)}, u32[]{:S(2)}, u32[]{:S(2)}) collective-permute-start(bf16[16,8,256]{2,1,0:T(8,128)(2,1)S(1)} %get-tuple-element.24), channel_id=1, source_target_pairs={{0,256},{64,320},{128,384},{192,448},{256,512},{320,576},{384,640}... | collective-permute-start | bytes 196616 | tf_op jit(solution)/shard_map/ppermute | solution.py:35
  81.4 3.3 %collective-permute-start.4 = (bf16[16,8,256]{2,1,0:T(8,128)(2,1)S(1)}, bf16[16,8,256]{2,1,0:T(8,128)(2,1)S(1)}, u32[]{:S(2)}, u32[]{:S(2)}) collective-permute-start(bf16[16,8,256]{2,1,0:T(8,128)(2,1)S(1)} %get-tuple-element.25), channel_id=1, source_target_pairs={{0,512},{64,576},{128,640},{192,704},{256,0},{320,64},{384,128},{4... | collective-permute-start | bytes 196616 | tf_op jit(solution)/shard_map/ppermute | solution.py:35
  85.2 7.5 %collective-permute-done.4.behind_ref = bf16[16,8,256]{2,1,0:T(8,128)(2,1)S(1)} collective-permute-done((bf16[16,8,256]{2,1,0:T(8,128)(2,1)S(1)}, bf16[16,8,256]{2,1,0:T(8,128)(2,1)S(1)}, u32[]{:S(2)}, u32[]{:S(2)}) %collective-permute-start.4) | collective-permute-done | bytes 65568 | tf_op jit(solution)/shard_map/ppermute | solution.py:35
  92.7 0.7 spread_sum.2
  93.5 11.6 %all-to-all-start = ((bf16[64,8,256]{2,1,0:T(8,128)(2,1)}), bf16[64,8,256]{2,1,0:T(8,128)(2,1)S(1)}, u32[]{:S(2)}, u32[]{:S(2)}) async-start(bf16[64,8,256]{2,1,0:T(8,128)(2,1)} %spread_sum.2), calls=%async_computation | async-start | bytes 524288 | tf_op jit(solution)/shard_map/all_to_all | solution.py:30
  105.6 12.5 %all-to-all-done.refs_0_ = bf16[64,8,256]{2,1,0:T(8,128)(2,1)S(1)} async-done(((bf16[64,8,256]{2,1,0:T(8,128)(2,1)}), bf16[64,8,256]{2,1,0:T(8,128)(2,1)S(1)}, u32[]{:S(2)}, u32[]{:S(2)}) %all-to-all-start) | async-done | bytes 262176 | tf_op jit(solution)/shard_map/all_to_all | solution.py:30
  118.2 3.9 %iterate_block.1 = bf16[16,8,512]{2,1,0:T(8,128)(2,1)} custom-call(bf16[64,8,256]{2,1,0:T(8,128)(2,1)S(1)} %all-to-all-done.refs_0_, bf16[64,8,256]{2,1,0:T(8,128)(2,1)S(1)} %all-to-all-done.1.refs_1_), custom_call_target="tpu_custom_call" | custom-call | flops 2415919104 | bytes 1048576 | tf_op jit(solution)/shard_map/iterate_block/pallas_call | solution.py:247
  122.0 3.6 %all-to-all-start.2 = ((bf16[16,8,512]{2,1,0:T(8,128)(2,1)}), bf16[16,8,512]{2,1,0:T(8,128)(2,1)S(1)}, u32[]{:S(2)}, u32[]{:S(2)}) async-start(bf16[16,8,512]{2,1,0:T(8,128)(2,1)} %iterate_block.1), calls=%async_computation.2 | async-start | bytes 262144 | tf_op jit(solution)/shard_map/all_to_all | solution.py:30
  125.7 8.8 %all-to-all-done.2 = bf16[16,8,512]{2,1,0:T(8,128)(2,1)S(1)} async-done(((bf16[16,8,512]{2,1,0:T(8,128)(2,1)}), bf16[16,8,512]{2,1,0:T(8,128)(2,1)S(1)}, u32[]{:S(2)}, u32[]{:S(2)}) %all-to-all-start.2) | async-done | bytes 131104 | tf_op jit(solution)/shard_map/all_to_all | solution.py:30
  134.5 1.3 gather_fusion
  135.8 7.1 %all-to-all-start.3 = ((bf16[36,8,512]{2,1,0:T(8,128)(2,1)}), bf16[36,8,512]{2,1,0:T(8,128)(2,1)S(1)}, u32[]{:S(2)}, u32[]{:S(2)}) async-start(bf16[36,8,512]{2,1,0:T(8,128)(2,1)} %gather_fusion), calls=%async_computation.3 | async-start | bytes 589824 | tf_op jit(solution)/shard_map/all_to_all | solution.py:30
  143.4 15.1 %all-to-all-done.3 = bf16[36,8,512]{2,1,0:T(8,128)(2,1)S(1)} async-done(((bf16[36,8,512]{2,1,0:T(8,128)(2,1)}), bf16[36,8,512]{2,1,0:T(8,128)(2,1)S(1)}, u32[]{:S(2)}, u32[]{:S(2)}) %all-to-all-start.3) | async-done | bytes 294944 | tf_op jit(solution)/shard_map/all_to_all | solution.py:30
  159.0 0.9 convert_select_fusion
  (29 shorter events, 3.0 us)
Async XLA Ops:
  0.0 1.4 copy-start
  1.4 1.0 copy-start.1
  2.4 0.7 copy-start.2
  3.1 66.3 %copy-start.3 = (s32[192]{0:T(256)S(1)}, s32[192]{0:T(256)}, u32[]{:S(2)}) copy-start(s32[192]{0:T(256)} %owners_ref.1) | copy-start | bytes 2308
  5.2 19.9 %collective-permute-start.5 = (bf16[3,16,8,256]{3,2,1,0:T(8,128)(2,1)S(1)}, bf16[3,16,8,256]{3,2,1,0:T(8,128)(2,1)S(1)}, u32[]{:S(2)}, u32[]{:S(2)}) collective-permute-start(bf16[3,16,8,256]{3,2,1,0:T(8,128)(2,1)S(1)} %get-tuple-element.27), channel_id=1, source_target_pairs={{0,64},{64,128},{128,192},{192,256},{256,320},{320,384},{384,448},... | collective-permute-start | bytes 589832 | tf_op jit(solution)/shard_map/ppermute | solution.py:35
  9.9 16.0 %collective-permute-start.6 = (bf16[3,16,8,256]{3,2,1,0:T(8,128)(2,1)S(1)}, bf16[3,16,8,256]{3,2,1,0:T(8,128)(2,1)S(1)}, u32[]{:S(2)}, u32[]{:S(2)}) collective-permute-start(bf16[3,16,8,256]{3,2,1,0:T(8,128)(2,1)S(1)} %get-tuple-element.28), channel_id=1, source_target_pairs={{0,704},{64,0},{128,64},{192,128},{256,192},{320,256},{384,320},{4... | collective-permute-start | bytes 589832 | tf_op jit(solution)/shard_map/ppermute | solution.py:35
  22.3 10.6 %collective-permute-start.7 = (bf16[3,16,8,256]{3,2,1,0:T(8,128)(2,1)S(1)}, bf16[3,16,8,256]{3,2,1,0:T(8,128)(2,1)S(1)}, u32[]{:S(2)}, u32[]{:S(2)}) collective-permute-start(bf16[3,16,8,256]{3,2,1,0:T(8,128)(2,1)S(1)} %get-tuple-element.29), channel_id=1, source_target_pairs={{0,640},{1,129},{64,704},{65,193},{128,0},{129,257},{192,64},{193,... | collective-permute-start | bytes 589832 | tf_op jit(solution)/shard_map/ppermute | solution.py:46
  33.1 11.6 %collective-permute-start.8 = (bf16[16,8,256]{2,1,0:T(8,128)(2,1)S(1)}, bf16[16,8,256]{2,1,0:T(8,128)(2,1)S(1)}, u32[]{:S(2)}, u32[]{:S(2)}) collective-permute-start(bf16[16,8,256]{2,1,0:T(8,128)(2,1)S(1)} %get-tuple-element.31), channel_id=1, source_target_pairs={{0,256},{64,320},{128,384},{192,448},{256,512},{320,576},{384,640}... | collective-permute-start | bytes 196616 | tf_op jit(solution)/shard_map/ppermute | solution.py:35
  35.0 9.6 %collective-permute-start.9 = (bf16[16,8,256]{2,1,0:T(8,128)(2,1)S(1)}, bf16[16,8,256]{2,1,0:T(8,128)(2,1)S(1)}, u32[]{:S(2)}, u32[]{:S(2)}) collective-permute-start(bf16[16,8,256]{2,1,0:T(8,128)(2,1)S(1)} %get-tuple-element.32), channel_id=1, source_target_pairs={{0,512},{64,576},{128,640},{192,704},{256,0},{320,64},{384,128},{4... | collective-permute-start | bytes 196616 | tf_op jit(solution)/shard_map/ppermute | solution.py:35
  45.4 48.1 %all-to-all-start.1 = ((bf16[64,8,256]{2,1,0:T(8,128)(2,1)}), bf16[64,8,256]{2,1,0:T(8,128)(2,1)S(1)}, u32[]{:S(2)}, u32[]{:S(2)}) async-start(bf16[64,8,256]{2,1,0:T(8,128)(2,1)} %spread_sum.3), calls=%async_computation.1 | async-start | bytes 524288 | tf_op jit(solution)/shard_map/all_to_all | solution.py:30
  59.7 9.8 %collective-permute-start = (bf16[3,16,8,256]{3,2,1,0:T(8,128)(2,1)S(1)}, bf16[3,16,8,256]{3,2,1,0:T(8,128)(2,1)S(1)}, u32[]{:S(2)}, u32[]{:S(2)}) collective-permute-start(bf16[3,16,8,256]{3,2,1,0:T(8,128)(2,1)S(1)} %get-tuple-element.20), channel_id=1, source_target_pairs={{0,64},{64,128},{128,192},{192,256},{256,320},{320,384},{384,448},... | collective-permute-start | bytes 589832 | tf_op jit(solution)/shard_map/ppermute | solution.py:35
  61.6 9.2 %collective-permute-start.1 = (bf16[3,16,8,256]{3,2,1,0:T(8,128)(2,1)S(1)}, bf16[3,16,8,256]{3,2,1,0:T(8,128)(2,1)S(1)}, u32[]{:S(2)}, u32[]{:S(2)}) collective-permute-start(bf16[3,16,8,256]{3,2,1,0:T(8,128)(2,1)S(1)} %get-tuple-element.21), channel_id=1, source_target_pairs={{0,704},{64,0},{128,64},{192,128},{256,192},{320,256},{384,320},{4... | collective-permute-start | bytes 589832 | tf_op jit(solution)/shard_map/ppermute | solution.py:35
  66.2 9.2 %collective-permute-start.2 = (bf16[3,16,8,256]{3,2,1,0:T(8,128)(2,1)S(1)}, bf16[3,16,8,256]{3,2,1,0:T(8,128)(2,1)S(1)}, u32[]{:S(2)}, u32[]{:S(2)}) collective-permute-start(bf16[3,16,8,256]{3,2,1,0:T(8,128)(2,1)S(1)} %get-tuple-element.22), channel_id=1, source_target_pairs={{0,640},{1,129},{64,704},{65,193},{128,0},{129,257},{192,64},{193,... | collective-permute-start | bytes 589832 | tf_op jit(solution)/shard_map/ppermute | solution.py:46
  75.5 9.7 %collective-permute-start.3 = (bf16[16,8,256]{2,1,0:T(8,128)(2,1)S(1)}, bf16[16,8,256]{2,1,0:T(8,128)(2,1)S(1)}, u32[]{:S(2)}, u32[]{:S(2)}) collective-permute-start(bf16[16,8,256]{2,1,0:T(8,128)(2,1)S(1)} %get-tuple-element.24), channel_id=1, source_target_pairs={{0,256},{64,320},{128,384},{192,448},{256,512},{320,576},{384,640}... | collective-permute-start | bytes 196616 | tf_op jit(solution)/shard_map/ppermute | solution.py:35
  81.4 11.3 %collective-permute-start.4 = (bf16[16,8,256]{2,1,0:T(8,128)(2,1)S(1)}, bf16[16,8,256]{2,1,0:T(8,128)(2,1)S(1)}, u32[]{:S(2)}, u32[]{:S(2)}) collective-permute-start(bf16[16,8,256]{2,1,0:T(8,128)(2,1)S(1)} %get-tuple-element.25), channel_id=1, source_target_pairs={{0,512},{64,576},{128,640},{192,704},{256,0},{320,64},{384,128},{4... | collective-permute-start | bytes 196616 | tf_op jit(solution)/shard_map/ppermute | solution.py:35
  93.5 24.7 %all-to-all-start = ((bf16[64,8,256]{2,1,0:T(8,128)(2,1)}), bf16[64,8,256]{2,1,0:T(8,128)(2,1)S(1)}, u32[]{:S(2)}, u32[]{:S(2)}) async-start(bf16[64,8,256]{2,1,0:T(8,128)(2,1)} %spread_sum.2), calls=%async_computation | async-start | bytes 524288 | tf_op jit(solution)/shard_map/all_to_all | solution.py:30
  122.0 12.5 %all-to-all-start.2 = ((bf16[16,8,512]{2,1,0:T(8,128)(2,1)}), bf16[16,8,512]{2,1,0:T(8,128)(2,1)S(1)}, u32[]{:S(2)}, u32[]{:S(2)}) async-start(bf16[16,8,512]{2,1,0:T(8,128)(2,1)} %iterate_block.1), calls=%async_computation.2 | async-start | bytes 262144 | tf_op jit(solution)/shard_map/all_to_all | solution.py:30
  135.8 22.6 %all-to-all-start.3 = ((bf16[36,8,512]{2,1,0:T(8,128)(2,1)}), bf16[36,8,512]{2,1,0:T(8,128)(2,1)S(1)}, u32[]{:S(2)}, u32[]{:S(2)}) async-start(bf16[36,8,512]{2,1,0:T(8,128)(2,1)} %gather_fusion), calls=%async_computation.3 | async-start | bytes 589824 | tf_op jit(solution)/shard_map/all_to_all | solution.py:30

commit v4 on v2

v4 whole, which is shorter than its diff:
```python
import math

import jax
import jax.numpy as jnp
from jax import lax
from jax.experimental import pallas as pl
from jax.experimental.pallas import tpu as pltpu
from jax.sharding import Mesh
from jax.sharding import PartitionSpec as P

ITERS = 3
PAIR = 3
RING = ("da", "db")
TENSOR = ("yb", "ya", "tx", "tc")
CHIPS = ("yb", "ya", "tx")
HOLD = ("ya", "tx")
SPLIT = (2, 4, 4, 2)
FOURTHS = 4
VMEM_LIMIT = 12 * 1024 * 1024


decay_rate = 0.95
newton_a = 3.4445
newton_b = -4.775
newton_c = 2.0315
norm_eps = 1e-07


def exchange(pieces, axes):
    return lax.all_to_all(pieces, axes, split_axis=0, concat_axis=0, tiled=True)


def mirrored(pieces, step):
    count, cores = lax.axis_size(RING), lax.axis_size("tc")
    pairs = [
        (i * cores + core, (i + (step if core else -step)) % count * cores + core)
        for i in range(count)
        for core in range(cores)
    ]
    return lax.ppermute(pieces, (*RING, "tc"), pairs)


def ranks_of(labels):
    length = labels.shape[0]
    places = jnp.arange(length, dtype=jnp.int32)
    earlier = (labels[None, :] == labels[:, None]) & (places[None, :] < places[:, None])
    return jnp.sum(earlier.astype(jnp.int32), axis=1)


def call(kernel, outs, ins, scratch=(), flops=0, size=0, limit=VMEM_LIMIT):
    vmem = pl.BlockSpec(memory_space=pltpu.VMEM)
    return pl.pallas_call(
        kernel,
        out_shape=outs,
        in_specs=[vmem if space is None else pl.BlockSpec(memory_space=space) for space in ins],
        out_specs=jax.tree.map(lambda _: vmem, outs),
        scratch_shapes=list(scratch),
        cost_estimate=pl.CostEstimate(flops=flops, bytes_accessed=size, transcendentals=0),
        compiler_params=pltpu.CompilerParams(vmem_limit_bytes=limit),
    )


def join_kernel(owners_ref, pieces_ref, momentum_ref, *refs):
    *outs, held_owners, found_ref, slots_ref, sems = refs
    fars, owns = outs[:FOURTHS], outs[FOURTHS:]
    weight = decay_rate * decay_rate / (1.0 + decay_rate)
    trios, fourths, per_group = pieces_ref.shape[:3]
    count = trios * fourths
    me = lax.axis_index(RING[0]) * fourths + lax.axis_index(RING[1])
    side = 2 * lax.axis_index("tc") - 1
    collectors = [
        lax.rem(me + away * side + count, count) for away in (0, 1, -1, 2)
    ]
    trio_of = [lax.div(place, fourths) for place in collectors]
    fourth_of = [lax.rem(place, fourths) for place in collectors]
    table = pltpu.make_async_copy(owners_ref, held_owners, sems.at[0])
    table.start()
    slots = pltpu.make_async_copy(momentum_ref, slots_ref, sems.at[1])
    slots.start()
    copies = []
    for step in (1, 2, 3, 0):
        for rel in range(trios):
            target = owns[step] if rel == 0 else fars[step].at[rel - 1]
            source = pieces_ref.at[lax.rem(trio_of[step] + rel, trios), fourth_of[step]]
            copies.append(pltpu.make_async_copy(source, target, sems.at[2 + len(copies)]))
    for copy in copies:
        copy.start()
    table.wait()

    def look(place, found):
        found_ref[found] = place
        return found + (held_owners[place] == me).astype(jnp.int32)

    total = lax.fori_loop(0, held_owners.shape[0], look, 0, unroll=8)
    slots.wait()
    for copy in copies:
        copy.wait()

    def add(slot, carry):
        place = found_ref[slot]
        group = lax.div(place, per_group)
        inside = place - group * per_group
        trio = lax.div(group, fourths)
        fourth = group - trio * fourths
        extra = weight * slots_ref[slot].astype(jnp.float32)
        for step in range(fourths):
            rel = lax.rem(trio - trio_of[step] + trios, trios)

            @pl.when((fourth == fourth_of[step]) & (rel == 0))
            def _():
                own = owns[step]
                own[inside] = (own[inside].astype(jnp.float32) + extra).astype(own.dtype)

            @pl.when((fourth == fourth_of[step]) & (rel != 0))
            def _():
                far = fars[step]
                joined = far[rel - 1, inside].astype(jnp.float32) + extra
                far[rel - 1, inside] = joined.astype(far.dtype)

        return carry

    lax.fori_loop(0, total, add, 0)


def join_momentum(pieces, momentum, owners):
    trios, fourths, *inside = pieces.shape
    far = jax.ShapeDtypeStruct((trios - 1, *inside), pieces.dtype)
    own = jax.ShapeDtypeStruct(tuple(inside), pieces.dtype)
    outs = call(
        join_kernel,
        [far] * fourths + [own] * fourths,
        [pltpu.HBM] * 3,
        [
            pltpu.SMEM(owners.shape, jnp.int32),
            pltpu.SMEM((owners.shape[0] + 1,), jnp.int32),
            pltpu.VMEM(momentum.shape, momentum.dtype),
            pltpu.SemaphoreType.DMA((2 + trios * fourths,)),
        ],
        2 * pieces.size,
        4 * pieces.size,
    )(owners, pieces, momentum)
    return outs[:fourths], outs[fourths:]


def combine_kernel(*refs):
    *terms, first_ref, second_ref = refs
    core = lax.axis_index("tc")
    for which, out in ((1 - core, first_ref), (core, second_ref)):
        for block in range(out.shape[0]):
            total = terms[0][which, block].astype(jnp.float32)
            for term in terms[1:]:
                total = total + term[which, block].astype(jnp.float32)
            out[block] = total.astype(out.dtype)


def combine(terms):
    out = jax.ShapeDtypeStruct(terms[0].shape[1:], terms[0].dtype)
    size = len(terms) * terms[0].size
    return call(combine_kernel, [out] * 2, [None] * len(terms), (), size, 2 * size)(*terms)


def spread_kernel(*refs):
    *terms, out_ref = refs
    blocks = terms[0].shape[0]
    for block in range(blocks):
        total = terms[0][block].astype(jnp.float32)
        for term in terms[1:]:
            total = total + term[block].astype(jnp.float32)
        total = total.astype(out_ref.dtype)
        for copy in range(SPLIT[0]):
            out_ref[copy * blocks + block] = total


def spread(terms):
    blocks, *inside = terms[0].shape
    out = jax.ShapeDtypeStruct((blocks * SPLIT[0], *inside), terms[0].dtype)
    size = len(terms) * terms[0].size
    return call(spread_kernel, out, [None] * len(terms), (), size, 2 * size)(*terms)


def sum_at_holder(fars, owns):
    away = (1, -1, 2)
    arrived = [mirrored(term, step) for term, step in zip(fars[1:], away)]
    stayed = [mirrored(term, step) for term, step in zip(owns[1:], away)]
    first, second = combine([fars[0], *arrived])
    sums = [mirrored(first, FOURTHS), mirrored(second, -FOURTHS)]
    return spread([owns[0], *stayed, *sums])


def iterate_kernel(mine_ref, other_ref, out_ref, wide_ref):
    count, piece_rows, width = mine_ref.shape
    slab = count * piece_rows // SPLIT[0]
    square = jnp.zeros((piece_rows, width), jnp.float32)
    for side, ref in enumerate((mine_ref, other_ref)):
        for index in range(count):
            piece = ref[index].astype(jnp.float32)
            square = square + piece * piece
            row = (side * count + index) * piece_rows
            wide_ref[row : row + piece_rows, :] = piece
    blend = 1.0 + decay_rate
    total = jnp.sum(jnp.sum(square, axis=0, keepdims=True), axis=1, keepdims=True)
    scale = blend / (blend * jnp.sqrt(total) + norm_eps)
    wide_ref[...] = wide_ref[...] * scale

    def dot(left, right, across):
        return lax.dot_general(
            left, right, (((1,), (across,)), ((), ())), preferred_element_type=jnp.float32
        )

    narrow = lambda value: value.astype(jnp.bfloat16)
    for iteration in range(ITERS):
        last = iteration == ITERS - 1
        current = wide_ref[...]
        currents = narrow(current)
        if last:
            kept = wide_ref[pl.ds(lax.axis_index("yb") * slab, slab), :]
            mine = dot(narrow(kept), currents, 1)
            squared = narrow(dot(currents, currents, 1))
            polynomial = newton_b * mine + newton_c * dot(narrow(mine), squared, 0)
        else:
            kept = current
            mine = dot(currents, currents, 1)
            squared = narrow(mine)
            polynomial = newton_b * mine + newton_c * dot(squared, squared, 0)
        following = newton_a * kept + dot(narrow(polynomial), currents, 0)
        if not last:
            wide_ref[...] = following
    result = following * math.sqrt(width)
    for piece in range(slab // piece_rows):
        rows = result[piece * piece_rows : (piece + 1) * piece_rows, :]
        out_ref[piece] = rows.astype(out_ref.dtype)


def iterate(mine, other):
    count, piece_rows, width = mine.shape
    rows = 2 * count * piece_rows
    out = jax.ShapeDtypeStruct((count // SPLIT[0], piece_rows, width), mine.dtype)
    return call(
        iterate_kernel,
        out,
        [None] * 2,
        [pltpu.VMEM((rows, width), jnp.float32)],
        3 * ITERS * 2 * rows * rows * width,
        4 * rows * width,
    )(mine, other)


def pick_kernel(index_ref, limit_ref, table_ref, out_ref):
    for place in range(out_ref.shape[0]):
        row = table_ref[index_ref[place]].astype(out_ref.dtype)
        out_ref[place] = jnp.where(place < limit_ref[0], row, jnp.zeros_like(row))


def pick(table, index, limit, dtype):
    out = jax.ShapeDtypeStruct((*index.shape, *table.shape[1:]), dtype)
    ins = [pltpu.SMEM, pltpu.SMEM, None]
    size = 4 * math.prod(out.shape)
    return call(pick_kernel, out, ins, (), size // 4, size)(index, limit[None], table)


def body(gradients, momentum, owners):
    dp_count = lax.axis_size(RING)
    my_group = lax.axis_index(RING)
    pieces = gradients[0]
    blocks_all, piece_rows, width = pieces.shape
    per_group = blocks_all // dp_count
    capacity = momentum.shape[1]
    places = jnp.arange(blocks_all, dtype=jnp.int32)
    slot_rank = ranks_of(owners)
    slot_ids = jnp.arange(capacity, dtype=jnp.int32)
    mine = owners == my_group
    grouped = pieces.reshape(dp_count // FOURTHS, FOURTHS, per_group, piece_rows, width)
    held = sum_at_holder(*join_momentum(grouped, momentum[0], owners))
    arrived = exchange(held, CHIPS)
    partner = lax.ppermute(arrived, "tc", [(0, 1), (1, 0)])
    back = exchange(iterate(arrived, partner), HOLD)
    groups = jnp.arange(dp_count, dtype=jnp.int32)
    held_owner = lax.dynamic_slice_in_dim(owners, my_group * per_group, per_group)
    held_rank = ranks_of(held_owner)
    held_places = jnp.arange(per_group, dtype=jnp.int32)
    pair_ids = jnp.arange(PAIR, dtype=jnp.int32)
    matched = (held_owner[:, None, None] == groups[None, :, None]) & (
        held_rank[:, None, None] == pair_ids[None, None, :]
    )
    source = jnp.sum(jnp.where(matched, held_places[:, None, None], 0), axis=0).reshape(-1)
    everything = jnp.asarray(source.shape[0], jnp.int32)
    incoming = exchange(pick(back, source, everything, back.dtype), RING)
    group_rank = ranks_of(owners * dp_count + places // per_group)
    position = places // per_group * PAIR + group_rank
    my_slots = mine[:, None] & (slot_rank[:, None] == slot_ids[None, :])
    arriving = jnp.sum(jnp.where(my_slots, position[:, None], 0), axis=0)
    filled = jnp.sum(mine.astype(jnp.int32))
    return pick(incoming, arriving, filled, jnp.float32)[None]


def solution(mesh):
    split = Mesh(mesh.devices.reshape(-1, FOURTHS, *SPLIT), (*RING, *TENSOR))
    in_specs = (P(RING, None, TENSOR, None), P(RING, None, TENSOR, None), P())
    out_specs = P(RING, None, TENSOR, None)
    return jax.shard_map(body, mesh=split, in_specs=in_specs, out_specs=out_specs, check_vma=False)
```

time: 136 us -> 127 us (0.934)
  blocking collectives: 20.5 us -> 0 us
  starting transfers between devices: 42.3 us -> 60.7 us
  waiting for transfers between devices: 54.9 us -> 46.6 us
  Pallas kernels: 9.13 us -> 12.6 us
  other arithmetic: 3.83 us -> 1.49 us
    ppermute x2 -> x9, starting transfers between devices: 18 us -> 40.4 us  [the longest x8 36.9 us: mirrored(): return lax.ppermute(pieces, (*RING, 'tc'), pairs)]
    all_to_all x1 -> x0, blocking collectives: 20.5 us -> none  [exchange(): return lax.all_to_all(pieces, axes, split_axis=0, concat_axis=0, tiled=True)]
    all_to_all x3, waiting for transfers between devices: 41 us -> 33.1 us  [exchange(): return lax.all_to_all(pieces, axes, split_axis=0, concat_axis=0, tiled=True)]
    all_to_all x3, starting transfers between devices: 24.3 us -> 20.3 us  [exchange(): return lax.all_to_all(pieces, axes, split_axis=0, concat_axis=0, tiled=True)]
    pallas_call x2 -> x6, Pallas kernels: 9.13 us -> 12.6 us  [the longest x1 4.44 us: join_momentum(): call(join_kernel, [far] * fourths + [own] * fourths, [pltpu.HBM] * 3, [pl...]
    unnamed x4 -> x8, local copies, waits for them, and re-layouts: 0.8 us -> 3.05 us
    gather x2 -> x0, local copies, waits for them, and re-layouts: 1.87 us -> none  [the longest x1 1.3 us: body(): outgoing = jnp.take(back, source, axis=0, mode='clip')]
    ppermute x2 -> x9, waiting for transfers between devices: 13.9 us -> 13.5 us  [the longest x8 12.6 us: mirrored(): return lax.ppermute(pieces, (*RING, 'tc'), pairs)]
  transfers between devices with their start and end apart: 5 -> 12, of which waited for: 5 -> 7; matrix products, arithmetic and copies ran while one was open for 1% -> 1% of each run, Pallas kernels for 0% -> 0%
where the time goes in v4:
time: 127 us; the launch traced here: 125 us
  starting transfers between devices  60.7 us (48%)
  waiting for transfers between devices  46.6 us (37%)
  Pallas kernels  12.6 us (10%)
  local copies, waits for them, and re-layouts  3.31 us (3%)
  other arithmetic  1.49 us (1%)
    ppermute x8, starting transfers between devices, mirrored(): return lax.ppermute(pieces, (*RING, 'tc'), pairs)  36.9 us
    all_to_all x3, waiting for transfers between devices, exchange(): return lax.all_to_all(pieces, axes, split_axis=0, concat_axis=0, tiled=True)  33.1 us
    all_to_all x3, starting transfers between devices, exchange(): return lax.all_to_all(pieces, axes, split_axis=0, concat_axis=0, tiled=True)  20.3 us
    ppermute x8, waiting for transfers between devices, mirrored(): return lax.ppermute(pieces, (*RING, 'tc'), pairs)  12.6 us
    pallas_call x1, Pallas kernels, join_momentum(): call(join_kernel, [far] * fourths + [own] * fourths, [pltpu.HBM] * 3, [pl...  4.44 us
    pallas_call x1, Pallas kernels, iterate(): call(iterate_kernel, out, [None] * 2, [pltpu.VMEM((rows, width), jnp.floa...  3.88 us
    ppermute x1, starting transfers between devices, body(): partner = lax.ppermute(arrived, 'tc', [(0, 1), (1, 0)])  3.56 us
    pallas_call x2, Pallas kernels, pick(): call(pick_kernel, out, ins, (), size // 4, size)(index, limit[None], table)  3.35 us
  transfers between devices with their start and end apart: 12, of which 7 were waited for; matrix products, arithmetic and copies ran while one was open for 1% of the time, Pallas kernels for 0%

profile of v4, /device:TPU:1, one launch (start us, length us, event | category | flops | bytes accessed | tf_op | source)
XLA Modules:
  0.0 125.0 jit_solution(9846882854805686456)
XLA Ops:
  0.0 1.4 %copy-done = bf16[1,192,8,512]{3,2,1,0:T(8,128)(2,1)S(1)} copy-done((bf16[1,192,8,512]{3,2,1,0:T(8,128)(2,1)S(1)}, bf16[1,192,8,512]{3,2,1,0:T(8,128)(2,1)}, u32[]{:S(2)}) %copy-start) | copy-done | bytes 1572888
  1.4 1.0 copy-done.1
  2.4 0.7 copy-done.2
  3.1 4.4 %shard_map.37 = (bf16[2,16,8,512]{3,2,1,0:T(8,128)(2,1)S(1)}, bf16[2,16,8,512]{3,2,1,0:T(8,128)(2,1)S(1)}, bf16[2,16,8,512]{3,2,1,0:T(8,128)(2,1)S(1)}, bf16[2,1...) custom-call(s32[192]{0:T(256)S(1)} %copy-done.2, ...), custom_call_target="tpu_custom_call" | custom-call | flops 1572864 | bytes 3145728 | tf_op jit(solution)/shard_map/pallas_call | solution.py:129
  7.5 4.6 %collective-permute-start.3 = (bf16[2,16,8,512]{3,2,1,0:T(8,128)(2,1)S(1)}, bf16[2,16,8,512]{3,2,1,0:T(8,128)(2,1)S(1)}, u32[]{:S(2)}, u32[]{:S(2)}) collective-permute-start(bf16[2,16,8,512]{3,2,1,0:T(8,128)(2,1)S(1)} %get-tuple-element.20), channel_id=1, source_target_pairs={{0,704},{1,65},{64,0},{65,129},{128,64},{129,193},{192,128},{193,2... | collective-permute-start | bytes 786440 | tf_op jit(solution)/shard_map/ppermute | solution.py:40
  12.1 12.8 %collective-permute-start.4 = (bf16[2,16,8,512]{3,2,1,0:T(8,128)(2,1)S(1)}, bf16[2,16,8,512]{3,2,1,0:T(8,128)(2,1)S(1)}, u32[]{:S(2)}, u32[]{:S(2)}) collective-permute-start(bf16[2,16,8,512]{3,2,1,0:T(8,128)(2,1)S(1)} %get-tuple-element.21), channel_id=1, source_target_pairs={{0,64},{1,705},{64,128},{65,1},{128,192},{129,65},{192,256},{193,1... | collective-permute-start | bytes 786440 | tf_op jit(solution)/shard_map/ppermute | solution.py:40
  24.9 1.9 %collective-permute-start.5 = (bf16[2,16,8,512]{3,2,1,0:T(8,128)(2,1)S(1)}, bf16[2,16,8,512]{3,2,1,0:T(8,128)(2,1)S(1)}, u32[]{:S(2)}, u32[]{:S(2)}) collective-permute-start(bf16[2,16,8,512]{3,2,1,0:T(8,128)(2,1)S(1)} %get-tuple-element.22), channel_id=1, source_target_pairs={{0,640},{1,129},{64,704},{65,193},{128,0},{129,257},{192,64},{193,... | collective-permute-start | bytes 786440 | tf_op jit(solution)/shard_map/ppermute | solution.py:40
  26.8 1.9 %collective-permute-start = (bf16[16,8,512]{2,1,0:T(8,128)(2,1)S(1)}, bf16[16,8,512]{2,1,0:T(8,128)(2,1)S(1)}, u32[]{:S(2)}, u32[]{:S(2)}) collective-permute-start(bf16[16,8,512]{2,1,0:T(8,128)(2,1)S(1)} %get-tuple-element.16), channel_id=1, source_target_pairs={{0,704},{1,65},{64,0},{65,129},{128,64},{129,193},{192,128},{193,2... | collective-permute-start | bytes 393224 | tf_op jit(solution)/shard_map/ppermute | solution.py:40
  28.7 4.6 %collective-permute-start.1 = (bf16[16,8,512]{2,1,0:T(8,128)(2,1)S(1)}, bf16[16,8,512]{2,1,0:T(8,128)(2,1)S(1)}, u32[]{:S(2)}, u32[]{:S(2)}) collective-permute-start(bf16[16,8,512]{2,1,0:T(8,128)(2,1)S(1)} %get-tuple-element.17), channel_id=1, source_target_pairs={{0,64},{1,705},{64,128},{65,1},{128,192},{129,65},{192,256},{193,1... | collective-permute-start | bytes 393224 | tf_op jit(solution)/shard_map/ppermute | solution.py:40
  33.3 1.9 %collective-permute-start.2 = (bf16[16,8,512]{2,1,0:T(8,128)(2,1)S(1)}, bf16[16,8,512]{2,1,0:T(8,128)(2,1)S(1)}, u32[]{:S(2)}, u32[]{:S(2)}) collective-permute-start(bf16[16,8,512]{2,1,0:T(8,128)(2,1)S(1)} %get-tuple-element.18), channel_id=1, source_target_pairs={{0,640},{1,129},{64,704},{65,193},{128,0},{129,257},{192,64},{193,... | collective-permute-start | bytes 393224 | tf_op jit(solution)/shard_map/ppermute | solution.py:40
  35.3 1.6 %collective-permute-done.5.refs_3_ = bf16[2,16,8,512]{3,2,1,0:T(8,128)(2,1)S(1)} collective-permute-done((bf16[2,16,8,512]{3,2,1,0:T(8,128)(2,1)S(1)}, bf16[2,16,8,512]{3,2,1,0:T(8,128)(2,1)S(1)}, u32[]{:S(2)}, u32[]{:S(2)}) %collective-permute-start.5) | collective-permute-done | bytes 262176 | tf_op jit(solution)/shard_map/ppermute | solution.py:40
  36.9 0.1 shard_map.38
  37.0 6.7 %collective-permute-start.6 = (bf16[16,8,512]{2,1,0:T(8,128)(2,1)S(1)}, bf16[16,8,512]{2,1,0:T(8,128)(2,1)S(1)}, u32[]{:S(2)}, u32[]{:S(2)}) collective-permute-start(bf16[16,8,512]{2,1,0:T(8,128)(2,1)S(1)} %get-tuple-element.23), channel_id=1, source_target_pairs={{0,512},{1,257},{64,576},{65,321},{128,640},{129,385},{192,704},{1... | collective-permute-start | bytes 393224 | tf_op jit(solution)/shard_map/ppermute | solution.py:40
  43.7 2.5 %collective-permute-start.7 = (bf16[16,8,512]{2,1,0:T(8,128)(2,1)S(1)}, bf16[16,8,512]{2,1,0:T(8,128)(2,1)S(1)}, u32[]{:S(2)}, u32[]{:S(2)}) collective-permute-start(bf16[16,8,512]{2,1,0:T(8,128)(2,1)S(1)} %get-tuple-element.24), channel_id=1, source_target_pairs={{0,256},{1,513},{64,320},{65,577},{128,384},{129,641},{192,448},{1... | collective-permute-start | bytes 393224 | tf_op jit(solution)/shard_map/ppermute | solution.py:40
  46.3 3.3 %collective-permute-done.6.refs_4_ = bf16[16,8,512]{2,1,0:T(8,128)(2,1)S(1)} collective-permute-done((bf16[16,8,512]{2,1,0:T(8,128)(2,1)S(1)}, bf16[16,8,512]{2,1,0:T(8,128)(2,1)S(1)}, u32[]{:S(2)}, u32[]{:S(2)}) %collective-permute-start.6) | collective-permute-done | bytes 131104 | tf_op jit(solution)/shard_map/ppermute | solution.py:40
  49.6 7.7 %collective-permute-done.7.refs_5_ = bf16[16,8,512]{2,1,0:T(8,128)(2,1)S(1)} collective-permute-done((bf16[16,8,512]{2,1,0:T(8,128)(2,1)S(1)}, bf16[16,8,512]{2,1,0:T(8,128)(2,1)S(1)}, u32[]{:S(2)}, u32[]{:S(2)}) %collective-permute-start.7) | collective-permute-done | bytes 131104 | tf_op jit(solution)/shard_map/ppermute | solution.py:40
  57.3 0.8 shard_map.39
  58.1 10.3 %all-to-all-start = ((bf16[32,8,512]{2,1,0:T(8,128)(2,1)}), bf16[32,8,512]{2,1,0:T(8,128)(2,1)S(1)}, u32[]{:S(2)}, u32[]{:S(2)}) async-start(bf16[32,8,512]{2,1,0:T(8,128)(2,1)} %shard_map.39), calls=%async_computation | async-start | bytes 524288 | tf_op jit(solution)/shard_map/all_to_all | solution.py:30
  68.5 12.1 %all-to-all-done.mine_ref = bf16[32,8,512]{2,1,0:T(8,128)(2,1)S(1)} async-done(((bf16[32,8,512]{2,1,0:T(8,128)(2,1)}), bf16[32,8,512]{2,1,0:T(8,128)(2,1)S(1)}, u32[]{:S(2)}, u32[]{:S(2)}) %all-to-all-start) | async-done | bytes 262176 | tf_op jit(solution)/shard_map/all_to_all | solution.py:30
  80.6 3.6 %collective-permute-start.8 = (bf16[32,8,512]{2,1,0:T(8,128)(2,1)S(1)}, bf16[32,8,512]{2,1,0:T(8,128)(2,1)S(1)}, u32[]{:S(2)}, u32[]{:S(2)}) collective-permute-start(bf16[32,8,512]{2,1,0:T(8,128)(2,1)S(1)} %all-to-all-done.mine_ref), channel_id=1, source_target_pairs={{0,1},{1,0},{2,3},{3,2},{4,5},{5,4},{6,7},{7,6},{8,9},{9,8},{10,11... | collective-permute-start | bytes 786440 | tf_op jit(solution)/shard_map/ppermute | solution.py:275
  84.1 0.2 convert_reduce_fusion.2
  84.4 0.9 collective-permute-done.8.other_ref
  85.3 3.9 %shard_map.40 = bf16[16,8,512]{2,1,0:T(8,128)(2,1)} custom-call(bf16[32,8,512]{2,1,0:T(8,128)(2,1)S(1)} %all-to-all-done.mine_ref, bf16[32,8,512]{2,1,0:T(8,128)(2,1)S(1)} %collective-permute-done.8.other_ref), custom_call_target="tpu_custom_call" | custom-call | flops 2415919104 | bytes 1048576 | tf_op jit(solution)/shard_map/pallas_call | solution.py:238
  89.2 3.5 %all-to-all-start.1 = ((bf16[16,8,512]{2,1,0:T(8,128)(2,1)}), bf16[16,8,512]{2,1,0:T(8,128)(2,1)S(1)}, u32[]{:S(2)}, u32[]{:S(2)}) async-start(bf16[16,8,512]{2,1,0:T(8,128)(2,1)} %shard_map.40), calls=%async_computation.1 | async-start | bytes 262144 | tf_op jit(solution)/shard_map/all_to_all | solution.py:30
  93.0 7.7 %all-to-all-done.1.table_ref = bf16[16,8,512]{2,1,0:T(8,128)(2,1)S(1)} async-done(((bf16[16,8,512]{2,1,0:T(8,128)(2,1)}), bf16[16,8,512]{2,1,0:T(8,128)(2,1)S(1)}, u32[]{:S(2)}, u32[]{:S(2)}) %all-to-all-start.1) | async-done | bytes 131104 | tf_op jit(solution)/shard_map/all_to_all | solution.py:30
  100.7 1.3 %shard_map.41 = bf16[36,8,512]{2,1,0:T(8,128)(2,1)} custom-call(s32[36]{0:T(128)S(1)} %reshape.74.index_ref, s32[1]{0:T(128)} %constant.42.clone.1.limit_ref, bf16[16,8,512]{2,1,0:T(8,128)(2,1)S(1)} %all-to-all-done.1.table_ref), custom_call_target="tpu_custom_call" | custom-call | flops 147456 | bytes 589824 | tf_op jit(solution)/shard_map/pallas_call | solution.py:258
  102.0 6.5 %all-to-all-start.2 = ((bf16[36,8,512]{2,1,0:T(8,128)(2,1)}), bf16[36,8,512]{2,1,0:T(8,128)(2,1)S(1)}, u32[]{:S(2)}, u32[]{:S(2)}) async-start(bf16[36,8,512]{2,1,0:T(8,128)(2,1)} %shard_map.41), calls=%async_computation.2 | async-start | bytes 589824 | tf_op jit(solution)/shard_map/all_to_all | solution.py:30
  108.5 0.2 convert_reduce_fusion.1
  108.7 0.6 convert_reduce_fusion.3
  109.3 0.2 convert_reduce_fusion
  109.6 13.3 %all-to-all-done.2.table_ref = bf16[36,8,512]{2,1,0:T(8,128)(2,1)S(1)} async-done(((bf16[36,8,512]{2,1,0:T(8,128)(2,1)}), bf16[36,8,512]{2,1,0:T(8,128)(2,1)S(1)}, u32[]{:S(2)}, u32[]{:S(2)}) %all-to-all-start.2) | async-done | bytes 294944 | tf_op jit(solution)/shard_map/all_to_all | solution.py:30
  122.9 2.0 %shard_map.42 = f32[36,8,512]{2,1,0:T(8,128)} custom-call(s32[36]{0:T(128)S(1)} %select_reduce_fusion.index_ref, s32[1]{0:T(128)} %bitcast.limit_ref, bf16[36,8,512]{2,1,0:T(8,128)(2,1)S(1)} %all-to-all-done.2.table_ref), custom_call_target="tpu_custom_call" | custom-call | flops 147456 | bytes 589824 | tf_op jit(solution)/shard_map/pallas_call | solution.py:258
  (18 shorter events, 0.6 us)
Async XLA Ops:
  0.0 1.4 %copy-start = (bf16[1,192,8,512]{3,2,1,0:T(8,128)(2,1)S(1)}, bf16[1,192,8,512]{3,2,1,0:T(8,128)(2,1)}, u32[]{:S(2)}) copy-start(bf16[1,192,8,512]{3,2,1,0:T(8,128)(2,1)} %param.3) | copy-start | bytes 4718596
  1.4 1.0 copy-start.1
  2.4 0.7 copy-start.2
  7.5 60.9 %copy-start.3 = (s32[192]{0:T(256)S(1)}, s32[192]{0:T(256)}, u32[]{:S(2)}) copy-start(s32[192]{0:T(256)} %owners_ref.1) | copy-start | bytes 2308
  7.5 25.8 %collective-permute-start.3 = (bf16[2,16,8,512]{3,2,1,0:T(8,128)(2,1)S(1)}, bf16[2,16,8,512]{3,2,1,0:T(8,128)(2,1)S(1)}, u32[]{:S(2)}, u32[]{:S(2)}) collective-permute-start(bf16[2,16,8,512]{3,2,1,0:T(8,128)(2,1)S(1)} %get-tuple-element.20), channel_id=1, source_target_pairs={{0,704},{1,65},{64,0},{65,129},{128,64},{129,193},{192,128},{193,2... | collective-permute-start | bytes 786440 | tf_op jit(solution)/shard_map/ppermute | solution.py:40
  12.1 23.1 %collective-permute-start.4 = (bf16[2,16,8,512]{3,2,1,0:T(8,128)(2,1)S(1)}, bf16[2,16,8,512]{3,2,1,0:T(8,128)(2,1)S(1)}, u32[]{:S(2)}, u32[]{:S(2)}) collective-permute-start(bf16[2,16,8,512]{3,2,1,0:T(8,128)(2,1)S(1)} %get-tuple-element.21), channel_id=1, source_target_pairs={{0,64},{1,705},{64,128},{65,1},{128,192},{129,65},{192,256},{193,1... | collective-permute-start | bytes 786440 | tf_op jit(solution)/shard_map/ppermute | solution.py:40
  24.9 12.0 %collective-permute-start.5 = (bf16[2,16,8,512]{3,2,1,0:T(8,128)(2,1)S(1)}, bf16[2,16,8,512]{3,2,1,0:T(8,128)(2,1)S(1)}, u32[]{:S(2)}, u32[]{:S(2)}) collective-permute-start(bf16[2,16,8,512]{3,2,1,0:T(8,128)(2,1)S(1)} %get-tuple-element.22), channel_id=1, source_target_pairs={{0,640},{1,129},{64,704},{65,193},{128,0},{129,257},{192,64},{193,... | collective-permute-start | bytes 786440 | tf_op jit(solution)/shard_map/ppermute | solution.py:40
  26.8 19.4 %collective-permute-start = (bf16[16,8,512]{2,1,0:T(8,128)(2,1)S(1)}, bf16[16,8,512]{2,1,0:T(8,128)(2,1)S(1)}, u32[]{:S(2)}, u32[]{:S(2)}) collective-permute-start(bf16[16,8,512]{2,1,0:T(8,128)(2,1)S(1)} %get-tuple-element.16), channel_id=1, source_target_pairs={{0,704},{1,65},{64,0},{65,129},{128,64},{129,193},{192,128},{193,2... | collective-permute-start | bytes 393224 | tf_op jit(solution)/shard_map/ppermute | solution.py:40
  28.7 17.5 %collective-permute-start.1 = (bf16[16,8,512]{2,1,0:T(8,128)(2,1)S(1)}, bf16[16,8,512]{2,1,0:T(8,128)(2,1)S(1)}, u32[]{:S(2)}, u32[]{:S(2)}) collective-permute-start(bf16[16,8,512]{2,1,0:T(8,128)(2,1)S(1)} %get-tuple-element.17), channel_id=1, source_target_pairs={{0,64},{1,705},{64,128},{65,1},{128,192},{129,65},{192,256},{193,1... | collective-permute-start | bytes 393224 | tf_op jit(solution)/shard_map/ppermute | solution.py:40
  33.3 12.9 %collective-permute-start.2 = (bf16[16,8,512]{2,1,0:T(8,128)(2,1)S(1)}, bf16[16,8,512]{2,1,0:T(8,128)(2,1)S(1)}, u32[]{:S(2)}, u32[]{:S(2)}) collective-permute-start(bf16[16,8,512]{2,1,0:T(8,128)(2,1)S(1)} %get-tuple-element.18), channel_id=1, source_target_pairs={{0,640},{1,129},{64,704},{65,193},{128,0},{129,257},{192,64},{193,... | collective-permute-start | bytes 393224 | tf_op jit(solution)/shard_map/ppermute | solution.py:40
  37.0 12.5 %collective-permute-start.6 = (bf16[16,8,512]{2,1,0:T(8,128)(2,1)S(1)}, bf16[16,8,512]{2,1,0:T(8,128)(2,1)S(1)}, u32[]{:S(2)}, u32[]{:S(2)}) collective-permute-start(bf16[16,8,512]{2,1,0:T(8,128)(2,1)S(1)} %get-tuple-element.23), channel_id=1, source_target_pairs={{0,512},{1,257},{64,576},{65,321},{128,640},{129,385},{192,704},{1... | collective-permute-start | bytes 393224 | tf_op jit(solution)/shard_map/ppermute | solution.py:40
  43.7 13.5 %collective-permute-start.7 = (bf16[16,8,512]{2,1,0:T(8,128)(2,1)S(1)}, bf16[16,8,512]{2,1,0:T(8,128)(2,1)S(1)}, u32[]{:S(2)}, u32[]{:S(2)}) collective-permute-start(bf16[16,8,512]{2,1,0:T(8,128)(2,1)S(1)} %get-tuple-element.24), channel_id=1, source_target_pairs={{0,256},{1,513},{64,320},{65,577},{128,384},{129,641},{192,448},{1... | collective-permute-start | bytes 393224 | tf_op jit(solution)/shard_map/ppermute | solution.py:40
  58.1 22.5 %all-to-all-start = ((bf16[32,8,512]{2,1,0:T(8,128)(2,1)}), bf16[32,8,512]{2,1,0:T(8,128)(2,1)S(1)}, u32[]{:S(2)}, u32[]{:S(2)}) async-start(bf16[32,8,512]{2,1,0:T(8,128)(2,1)} %shard_map.39), calls=%async_computation | async-start | bytes 524288 | tf_op jit(solution)/shard_map/all_to_all | solution.py:30
  80.6 4.7 %collective-permute-start.8 = (bf16[32,8,512]{2,1,0:T(8,128)(2,1)S(1)}, bf16[32,8,512]{2,1,0:T(8,128)(2,1)S(1)}, u32[]{:S(2)}, u32[]{:S(2)}) collective-permute-start(bf16[32,8,512]{2,1,0:T(8,128)(2,1)S(1)} %all-to-all-done.mine_ref), channel_id=1, source_target_pairs={{0,1},{1,0},{2,3},{3,2},{4,5},{5,4},{6,7},{7,6},{8,9},{9,8},{10,11... | collective-permute-start | bytes 786440 | tf_op jit(solution)/shard_map/ppermute | solution.py:275
  89.2 11.5 %all-to-all-start.1 = ((bf16[16,8,512]{2,1,0:T(8,128)(2,1)}), bf16[16,8,512]{2,1,0:T(8,128)(2,1)S(1)}, u32[]{:S(2)}, u32[]{:S(2)}) async-start(bf16[16,8,512]{2,1,0:T(8,128)(2,1)} %shard_map.40), calls=%async_computation.1 | async-start | bytes 262144 | tf_op jit(solution)/shard_map/all_to_all | solution.py:30
  102.0 20.9 %all-to-all-start.2 = ((bf16[36,8,512]{2,1,0:T(8,128)(2,1)}), bf16[36,8,512]{2,1,0:T(8,128)(2,1)S(1)}, u32[]{:S(2)}, u32[]{:S(2)}) async-start(bf16[36,8,512]{2,1,0:T(8,128)(2,1)} %shard_map.41), calls=%async_computation.2 | async-start | bytes 589824 | tf_op jit(solution)/shard_map/all_to_all | solution.py:30

commit v5 on v4

--- a/solution.py
+++ b/solution.py
@@ -17,6 +17,7 @@
 SPLIT = (2, 4, 4, 2)
 FOURTHS = 4
 VMEM_LIMIT = 12 * 1024 * 1024
+JOIN_LIMIT = 65_400_000
 
 
 decay_rate = 0.95
@@ -61,7 +62,7 @@
 
 
 def join_kernel(owners_ref, pieces_ref, momentum_ref, *refs):
-    *outs, held_owners, found_ref, slots_ref, sems = refs
+    *outs, held_owners, found_ref, bounds_ref, slots_ref, sems = refs
     fars, owns = outs[:FOURTHS], outs[FOURTHS:]
     weight = decay_rate * decay_rate / (1.0 + decay_rate)
     trios, fourths, per_group = pieces_ref.shape[:3]
@@ -87,39 +88,27 @@
         copy.start()
     table.wait()
 
-    def look(place, found):
-        found_ref[found] = place
-        return found + (held_owners[place] == me).astype(jnp.int32)
-
-    total = lax.fori_loop(0, held_owners.shape[0], look, 0, unroll=8)
+    found = jnp.int32(0)
+    for group in range(count):
+        bounds_ref[group] = found
+        for inside in range(per_group):
+            found_ref[found] = inside
+            found = found + (held_owners[group * per_group + inside] == me).astype(jnp.int32)
+    bounds_ref[count] = found
     slots.wait()
-    for copy in copies:
+    for index, copy in enumerate(copies):
+        step, rel = (1, 2, 3, 0)[index // trios], index % trios
+        target = owns[step] if rel == 0 else fars[step].at[rel - 1]
+        group = lax.rem(trio_of[step] + rel, trios) * fourths + fourth_of[step]
         copy.wait()
 
-    def add(slot, carry):
-        place = found_ref[slot]
-        group = lax.div(place, per_group)
-        inside = place - group * per_group
-        trio = lax.div(group, fourths)
-        fourth = group - trio * fourths
-        extra = weight * slots_ref[slot].astype(jnp.float32)
-        for step in range(fourths):
-            rel = lax.rem(trio - trio_of[step] + trios, trios)
-
-            @pl.when((fourth == fourth_of[step]) & (rel == 0))
-            def _():
-                own = owns[step]
-                own[inside] = (own[inside].astype(jnp.float32) + extra).astype(own.dtype)
-
-            @pl.when((fourth == fourth_of[step]) & (rel != 0))
-            def _():
-                far = fars[step]
-                joined = far[rel - 1, inside].astype(jnp.float32) + extra
-                far[rel - 1, inside] = joined.astype(far.dtype)
-
-        return carry
-
-    lax.fori_loop(0, total, add, 0)
+        def add(slot, carry, target=target):
+            inside = found_ref[slot]
+            extra = weight * slots_ref[slot].astype(jnp.float32)
+            target[inside] = (target[inside].astype(jnp.float32) + extra).astype(target.dtype)
+            return carry
+
+        lax.fori_loop(bounds_ref[group], bounds_ref[group + 1], add, 0)
 
 
 def join_momentum(pieces, momentum, owners):
@@ -133,11 +122,13 @@
         [
             pltpu.SMEM(owners.shape, jnp.int32),
             pltpu.SMEM((owners.shape[0] + 1,), jnp.int32),
+            pltpu.SMEM((trios * fourths + 1,), jnp.int32),
             pltpu.VMEM(momentum.shape, momentum.dtype),
             pltpu.SemaphoreType.DMA((2 + trios * fourths,)),
         ],
         2 * pieces.size,
         4 * pieces.size,
+        JOIN_LIMIT,
     )(owners, pieces, momentum)
     return outs[:fourths], outs[fourths:]
 
@@ -243,19 +234,6 @@
         3 * ITERS * 2 * rows * rows * width,
         4 * rows * width,
     )(mine, other)
-
-
-def pick_kernel(index_ref, limit_ref, table_ref, out_ref):
-    for place in range(out_ref.shape[0]):
-        row = table_ref[index_ref[place]].astype(out_ref.dtype)
-        out_ref[place] = jnp.where(place < limit_ref[0], row, jnp.zeros_like(row))
-
-
-def pick(table, index, limit, dtype):
-    out = jax.ShapeDtypeStruct((*index.shape, *table.shape[1:]), dtype)
-    ins = [pltpu.SMEM, pltpu.SMEM, None]
-    size = 4 * math.prod(out.shape)
-    return call(pick_kernel, out, ins, (), size // 4, size)(index, limit[None], table)
 
 
 def body(gradients, momentum, owners):
@@ -283,14 +261,14 @@
         held_rank[:, None, None] == pair_ids[None, None, :]
     )
     source = jnp.sum(jnp.where(matched, held_places[:, None, None], 0), axis=0).reshape(-1)
-    everything = jnp.asarray(source.shape[0], jnp.int32)
-    incoming = exchange(pick(back, source, everything, back.dtype), RING)
+    incoming = exchange(jnp.take(back, source, axis=0, mode="clip"), RING)
     group_rank = ranks_of(owners * dp_count + places // per_group)
     position = places // per_group * PAIR + group_rank
     my_slots = mine[:, None] & (slot_rank[:, None] == slot_ids[None, :])
     arriving = jnp.sum(jnp.where(my_slots, position[:, None], 0), axis=0)
-    filled = jnp.sum(mine.astype(jnp.int32))
-    return pick(incoming, arriving, filled, jnp.float32)[None]
+    occupied = jnp.any(my_slots, axis=0)
+    chosen = jnp.take(incoming, arriving, axis=0, mode="clip").astype(jnp.float32)
+    return jnp.where(occupied[:, None, None], chosen, 0.0)[None]
 
 
 def solution(mesh):

time: 127 us -> 123 us (0.969)
  Pallas kernels: 12.6 us -> 7.55 us
  waiting for transfers between devices: 46.6 us -> 44 us
  starting transfers between devices: 60.7 us -> 63 us
    pallas_call x2 -> x0, Pallas kernels: 3.35 us -> none  [pick(): call(pick_kernel, out, ins, (), size // 4, size)(index, limit[None], table)]
    ppermute x1, starting transfers between devices: 3.56 us -> 5.65 us  [body(): partner = lax.ppermute(arrived, 'tc', [(0, 1), (1, 0)])]
    gather x0 -> x2, local copies, waits for them, and re-layouts: none -> 1.87 us  [the longest x1 1.3 us: body(): incoming = exchange(jnp.take(back, source, axis=0, mode='clip'), RING)]
    pallas_call x1, Pallas kernels: 4.44 us -> 2.74 us  [join_momentum(): call(join_kernel, [far] * fourths + [own] * fourths, [pltpu.HBM] * 3, [pl...]
    unnamed x8 -> x6, local copies, waits for them, and re-layouts: 3.05 us -> 1.86 us
where the time goes in v5:
time: 123 us; the launch traced here: 121 us
  starting transfers between devices  63 us (51%)
  waiting for transfers between devices  44 us (36%)
  Pallas kernels  7.55 us (6%)
  local copies, waits for them, and re-layouts  3.99 us (3%)
  other arithmetic  1.91 us (2%)
    ppermute x8, starting transfers between devices, mirrored(): return lax.ppermute(pieces, (*RING, 'tc'), pairs)  36.6 us
    all_to_all x3, waiting for transfers between devices, exchange(): return lax.all_to_all(pieces, axes, split_axis=0, concat_axis=0, tiled=True)  31.9 us
    all_to_all x3, starting transfers between devices, exchange(): return lax.all_to_all(pieces, axes, split_axis=0, concat_axis=0, tiled=True)  20.8 us
    ppermute x8, waiting for transfers between devices, mirrored(): return lax.ppermute(pieces, (*RING, 'tc'), pairs)  11.4 us
    ppermute x1, starting transfers between devices, body(): partner = lax.ppermute(arrived, 'tc', [(0, 1), (1, 0)])  5.65 us
    pallas_call x1, Pallas kernels, iterate(): call(iterate_kernel, out, [None] * 2, [pltpu.VMEM((rows, width), jnp.floa...  3.88 us
    pallas_call x1, Pallas kernels, join_momentum(): call(join_kernel, [far] * fourths + [own] * fourths, [pltpu.HBM] * 3, [pl...  2.74 us
  transfers between devices with their start and end apart: 12, of which 7 were waited for; matrix products, arithmetic and copies ran while one was open for 1% of the time, Pallas kernels for 0%

profile of v5, /device:TPU:1, one launch (start us, length us, event | category | flops | bytes accessed | tf_op | source)
XLA Modules:
  0.0 120.7 jit_solution(1887583580426771882)
XLA Ops:
  0.0 2.7 %shard_map.37 = (bf16[2,16,8,512]{3,2,1,0:T(8,128)(2,1)}, bf16[2,16,8,512]{3,2,1,0:T(8,128)(2,1)}, bf16[2,16,8,512]{3,2,1,0:T(8,128)(2,1)}, bf16[2,16,8,512]{3,2...) custom-call(s32[192]{0:T(256)} %owners_ref.1, ...), custom_call_target="tpu_custom_call" | custom-call | flops 1572864 | bytes 3145728 | tf_op jit(solution)/shard_map/pallas_call | solution.py:118
  2.8 4.8 %collective-permute-start.3 = (bf16[2,16,8,512]{3,2,1,0:T(8,128)(2,1)}, bf16[2,16,8,512]{3,2,1,0:T(8,128)(2,1)S(1)}, u32[]{:S(2)}, u32[]{:S(2)}) collective-permute-start(bf16[2,16,8,512]{3,2,1,0:T(8,128)(2,1)} %get-tuple-element.20), channel_id=1, source_target_pairs={{0,704},{1,65},{64,0},{65,129},{128,64},{129,193},{192,128},{193,2... | collective-permute-start | bytes 786440 | tf_op jit(solution)/shard_map/ppermute | solution.py:41
  7.6 12.2 %collective-permute-start.4 = (bf16[2,16,8,512]{3,2,1,0:T(8,128)(2,1)}, bf16[2,16,8,512]{3,2,1,0:T(8,128)(2,1)S(1)}, u32[]{:S(2)}, u32[]{:S(2)}) collective-permute-start(bf16[2,16,8,512]{3,2,1,0:T(8,128)(2,1)} %get-tuple-element.21), channel_id=1, source_target_pairs={{0,64},{1,705},{64,128},{65,1},{128,192},{129,65},{192,256},{193,1... | collective-permute-start | bytes 786440 | tf_op jit(solution)/shard_map/ppermute | solution.py:41
  19.8 1.9 %collective-permute-start.5 = (bf16[2,16,8,512]{3,2,1,0:T(8,128)(2,1)}, bf16[2,16,8,512]{3,2,1,0:T(8,128)(2,1)S(1)}, u32[]{:S(2)}, u32[]{:S(2)}) collective-permute-start(bf16[2,16,8,512]{3,2,1,0:T(8,128)(2,1)} %get-tuple-element.22), channel_id=1, source_target_pairs={{0,640},{1,129},{64,704},{65,193},{128,0},{129,257},{192,64},{193,... | collective-permute-start | bytes 786440 | tf_op jit(solution)/shard_map/ppermute | solution.py:41
  21.7 1.9 %collective-permute-start = (bf16[16,8,512]{2,1,0:T(8,128)(2,1)}, bf16[16,8,512]{2,1,0:T(8,128)(2,1)S(1)}, u32[]{:S(2)}, u32[]{:S(2)}) collective-permute-start(bf16[16,8,512]{2,1,0:T(8,128)(2,1)} %get-tuple-element.16), channel_id=1, source_target_pairs={{0,704},{1,65},{64,0},{65,129},{128,64},{129,193},{192,128},{193,2... | collective-permute-start | bytes 393224 | tf_op jit(solution)/shard_map/ppermute | solution.py:41
  23.7 4.6 %collective-permute-start.1 = (bf16[16,8,512]{2,1,0:T(8,128)(2,1)}, bf16[16,8,512]{2,1,0:T(8,128)(2,1)S(1)}, u32[]{:S(2)}, u32[]{:S(2)}) collective-permute-start(bf16[16,8,512]{2,1,0:T(8,128)(2,1)} %get-tuple-element.17), channel_id=1, source_target_pairs={{0,64},{1,705},{64,128},{65,1},{128,192},{129,65},{192,256},{193,1... | collective-permute-start | bytes 393224 | tf_op jit(solution)/shard_map/ppermute | solution.py:41
  28.3 1.9 %collective-permute-start.2 = (bf16[16,8,512]{2,1,0:T(8,128)(2,1)}, bf16[16,8,512]{2,1,0:T(8,128)(2,1)S(1)}, u32[]{:S(2)}, u32[]{:S(2)}) collective-permute-start(bf16[16,8,512]{2,1,0:T(8,128)(2,1)} %get-tuple-element.18), channel_id=1, source_target_pairs={{0,640},{1,129},{64,704},{65,193},{128,0},{129,257},{192,64},{193,... | collective-permute-start | bytes 393224 | tf_op jit(solution)/shard_map/ppermute | solution.py:41
  30.2 0.3 collective-permute-done.5.refs_3_
  30.5 0.9 copy-done
  31.4 0.1 shard_map.38
  31.6 6.0 %collective-permute-start.6 = (bf16[16,8,512]{2,1,0:T(8,128)(2,1)S(1)}, bf16[16,8,512]{2,1,0:T(8,128)(2,1)S(1)}, u32[]{:S(2)}, u32[]{:S(2)}) collective-permute-start(bf16[16,8,512]{2,1,0:T(8,128)(2,1)S(1)} %get-tuple-element.23), channel_id=1, source_target_pairs={{0,512},{1,257},{64,576},{65,321},{128,640},{129,385},{192,704},{1... | collective-permute-start | bytes 393224 | tf_op jit(solution)/shard_map/ppermute | solution.py:41
  37.6 3.2 %collective-permute-start.7 = (bf16[16,8,512]{2,1,0:T(8,128)(2,1)S(1)}, bf16[16,8,512]{2,1,0:T(8,128)(2,1)S(1)}, u32[]{:S(2)}, u32[]{:S(2)}) collective-permute-start(bf16[16,8,512]{2,1,0:T(8,128)(2,1)S(1)} %get-tuple-element.24), channel_id=1, source_target_pairs={{0,256},{1,513},{64,320},{65,577},{128,384},{129,641},{192,448},{1... | collective-permute-start | bytes 393224 | tf_op jit(solution)/shard_map/ppermute | solution.py:41
  40.8 1.1 collective-permute-done.6.refs_4_
  41.9 10.0 %collective-permute-done.7.refs_5_ = bf16[16,8,512]{2,1,0:T(8,128)(2,1)S(1)} collective-permute-done((bf16[16,8,512]{2,1,0:T(8,128)(2,1)S(1)}, bf16[16,8,512]{2,1,0:T(8,128)(2,1)S(1)}, u32[]{:S(2)}, u32[]{:S(2)}) %collective-permute-start.7) | collective-permute-done | bytes 131104 | tf_op jit(solution)/shard_map/ppermute | solution.py:41
  51.9 0.9 copy-done.1
  52.8 0.8 shard_map.39
  53.6 9.7 %all-to-all-start = ((bf16[32,8,512]{2,1,0:T(8,128)(2,1)}), bf16[32,8,512]{2,1,0:T(8,128)(2,1)S(1)}, u32[]{:S(2)}, u32[]{:S(2)}) async-start(bf16[32,8,512]{2,1,0:T(8,128)(2,1)} %shard_map.39), calls=%async_computation | async-start | bytes 524288 | tf_op jit(solution)/shard_map/all_to_all | solution.py:31
  63.4 0.2 convert_reduce_fusion.2
  63.6 10.0 %all-to-all-done.mine_ref = bf16[32,8,512]{2,1,0:T(8,128)(2,1)S(1)} async-done(((bf16[32,8,512]{2,1,0:T(8,128)(2,1)}), bf16[32,8,512]{2,1,0:T(8,128)(2,1)S(1)}, u32[]{:S(2)}, u32[]{:S(2)}) %all-to-all-start) | async-done | bytes 262176 | tf_op jit(solution)/shard_map/all_to_all | solution.py:31
  73.7 5.7 %collective-permute-start.8 = (bf16[32,8,512]{2,1,0:T(8,128)(2,1)S(1)}, bf16[32,8,512]{2,1,0:T(8,128)(2,1)S(1)}, u32[]{:S(2)}, u32[]{:S(2)}) collective-permute-start(bf16[32,8,512]{2,1,0:T(8,128)(2,1)S(1)} %all-to-all-done.mine_ref), channel_id=1, source_target_pairs={{0,1},{1,0},{2,3},{3,2},{4,5},{5,4},{6,7},{7,6},{8,9},{9,8},{10,11... | collective-permute-start | bytes 786440 | tf_op jit(solution)/shard_map/ppermute | solution.py:253
  79.6 0.2 convert_reduce_fusion.1
  79.8 0.7 collective-permute-done.8.other_ref
  80.5 3.9 %shard_map.40 = bf16[16,8,512]{2,1,0:T(8,128)(2,1)} custom-call(bf16[32,8,512]{2,1,0:T(8,128)(2,1)S(1)} %all-to-all-done.mine_ref, bf16[32,8,512]{2,1,0:T(8,128)(2,1)S(1)} %collective-permute-done.8.other_ref), custom_call_target="tpu_custom_call" | custom-call | flops 2415919104 | bytes 1048576 | tf_op jit(solution)/shard_map/pallas_call | solution.py:229
  84.4 3.5 %all-to-all-start.1 = ((bf16[16,8,512]{2,1,0:T(8,128)(2,1)}), bf16[16,8,512]{2,1,0:T(8,128)(2,1)S(1)}, u32[]{:S(2)}, u32[]{:S(2)}) async-start(bf16[16,8,512]{2,1,0:T(8,128)(2,1)} %shard_map.40), calls=%async_computation.1 | async-start | bytes 262144 | tf_op jit(solution)/shard_map/all_to_all | solution.py:31
  87.9 8.0 %all-to-all-done.1 = bf16[16,8,512]{2,1,0:T(8,128)(2,1)S(1)} async-done(((bf16[16,8,512]{2,1,0:T(8,128)(2,1)}), bf16[16,8,512]{2,1,0:T(8,128)(2,1)S(1)}, u32[]{:S(2)}, u32[]{:S(2)}) %all-to-all-start.1) | async-done | bytes 131104 | tf_op jit(solution)/shard_map/all_to_all | solution.py:31
  95.9 1.3 %gather_fusion = bf16[36,8,512]{2,1,0:T(8,128)(2,1)} fusion(bf16[16,8,512]{2,1,0:T(8,128)(2,1)S(1)} %all-to-all-done.1, s32[1024]{0:T(1024)S(1)} %pad_clamp_fusion.1), kind=kCustom, calls=%fused_computation | custom fusion | bytes 589968 | tf_op jit(solution)/shard_map/jit(_take)/gather | solution.py:264
  97.2 7.6 %all-to-all-start.2 = ((bf16[36,8,512]{2,1,0:T(8,128)(2,1)}), bf16[36,8,512]{2,1,0:T(8,128)(2,1)S(1)}, u32[]{:S(2)}, u32[]{:S(2)}) async-start(bf16[36,8,512]{2,1,0:T(8,128)(2,1)} %gather_fusion), calls=%async_computation.2 | async-start | bytes 589824 | tf_op jit(solution)/shard_map/all_to_all | solution.py:31
  104.8 0.2 convert_reduce_fusion
  105.0 0.1 select_reduce_fusion
  105.3 13.9 %all-to-all-done.2 = bf16[36,8,512]{2,1,0:T(8,128)(2,1)S(1)} async-done(((bf16[36,8,512]{2,1,0:T(8,128)(2,1)}), bf16[36,8,512]{2,1,0:T(8,128)(2,1)S(1)}, u32[]{:S(2)}, u32[]{:S(2)}) %all-to-all-start.2) | async-done | bytes 294944 | tf_op jit(solution)/shard_map/all_to_all | solution.py:31
  119.2 0.6 gather_fusion.1
  119.8 0.9 convert_select_fusion
  (21 shorter events, 0.6 us)
Async XLA Ops:
  2.7 60.5 %copy-start.2 = (s32[192]{0:T(256)S(1)}, s32[192]{0:T(256)}, u32[]{:S(2)}) copy-start(s32[192]{0:T(256)} %owners_ref.1) | copy-start | bytes 2308
  2.8 25.5 %collective-permute-start.3 = (bf16[2,16,8,512]{3,2,1,0:T(8,128)(2,1)}, bf16[2,16,8,512]{3,2,1,0:T(8,128)(2,1)S(1)}, u32[]{:S(2)}, u32[]{:S(2)}) collective-permute-start(bf16[2,16,8,512]{3,2,1,0:T(8,128)(2,1)} %get-tuple-element.20), channel_id=1, source_target_pairs={{0,704},{1,65},{64,0},{65,129},{128,64},{129,193},{192,128},{193,2... | collective-permute-start | bytes 786440 | tf_op jit(solution)/shard_map/ppermute | solution.py:41
  7.6 22.6 %collective-permute-start.4 = (bf16[2,16,8,512]{3,2,1,0:T(8,128)(2,1)}, bf16[2,16,8,512]{3,2,1,0:T(8,128)(2,1)S(1)}, u32[]{:S(2)}, u32[]{:S(2)}) collective-permute-start(bf16[2,16,8,512]{3,2,1,0:T(8,128)(2,1)} %get-tuple-element.21), channel_id=1, source_target_pairs={{0,64},{1,705},{64,128},{65,1},{128,192},{129,65},{192,256},{193,1... | collective-permute-start | bytes 786440 | tf_op jit(solution)/shard_map/ppermute | solution.py:41
  19.8 10.7 %collective-permute-start.5 = (bf16[2,16,8,512]{3,2,1,0:T(8,128)(2,1)}, bf16[2,16,8,512]{3,2,1,0:T(8,128)(2,1)S(1)}, u32[]{:S(2)}, u32[]{:S(2)}) collective-permute-start(bf16[2,16,8,512]{3,2,1,0:T(8,128)(2,1)} %get-tuple-element.22), channel_id=1, source_target_pairs={{0,640},{1,129},{64,704},{65,193},{128,0},{129,257},{192,64},{193,... | collective-permute-start | bytes 786440 | tf_op jit(solution)/shard_map/ppermute | solution.py:41
  21.7 19.0 %collective-permute-start = (bf16[16,8,512]{2,1,0:T(8,128)(2,1)}, bf16[16,8,512]{2,1,0:T(8,128)(2,1)S(1)}, u32[]{:S(2)}, u32[]{:S(2)}) collective-permute-start(bf16[16,8,512]{2,1,0:T(8,128)(2,1)} %get-tuple-element.16), channel_id=1, source_target_pairs={{0,704},{1,65},{64,0},{65,129},{128,64},{129,193},{192,128},{193,2... | collective-permute-start | bytes 393224 | tf_op jit(solution)/shard_map/ppermute | solution.py:41
  23.7 17.1 %collective-permute-start.1 = (bf16[16,8,512]{2,1,0:T(8,128)(2,1)}, bf16[16,8,512]{2,1,0:T(8,128)(2,1)S(1)}, u32[]{:S(2)}, u32[]{:S(2)}) collective-permute-start(bf16[16,8,512]{2,1,0:T(8,128)(2,1)} %get-tuple-element.17), channel_id=1, source_target_pairs={{0,64},{1,705},{64,128},{65,1},{128,192},{129,65},{192,256},{193,1... | collective-permute-start | bytes 393224 | tf_op jit(solution)/shard_map/ppermute | solution.py:41
  28.3 12.5 %collective-permute-start.2 = (bf16[16,8,512]{2,1,0:T(8,128)(2,1)}, bf16[16,8,512]{2,1,0:T(8,128)(2,1)S(1)}, u32[]{:S(2)}, u32[]{:S(2)}) collective-permute-start(bf16[16,8,512]{2,1,0:T(8,128)(2,1)} %get-tuple-element.18), channel_id=1, source_target_pairs={{0,640},{1,129},{64,704},{65,193},{128,0},{129,257},{192,64},{193,... | collective-permute-start | bytes 393224 | tf_op jit(solution)/shard_map/ppermute | solution.py:41
  30.5 1.0 copy-start
  31.6 10.3 %collective-permute-start.6 = (bf16[16,8,512]{2,1,0:T(8,128)(2,1)S(1)}, bf16[16,8,512]{2,1,0:T(8,128)(2,1)S(1)}, u32[]{:S(2)}, u32[]{:S(2)}) collective-permute-start(bf16[16,8,512]{2,1,0:T(8,128)(2,1)S(1)} %get-tuple-element.23), channel_id=1, source_target_pairs={{0,512},{1,257},{64,576},{65,321},{128,640},{129,385},{192,704},{1... | collective-permute-start | bytes 393224 | tf_op jit(solution)/shard_map/ppermute | solution.py:41
  37.6 14.3 %collective-permute-start.7 = (bf16[16,8,512]{2,1,0:T(8,128)(2,1)S(1)}, bf16[16,8,512]{2,1,0:T(8,128)(2,1)S(1)}, u32[]{:S(2)}, u32[]{:S(2)}) collective-permute-start(bf16[16,8,512]{2,1,0:T(8,128)(2,1)S(1)} %get-tuple-element.24), channel_id=1, source_target_pairs={{0,256},{1,513},{64,320},{65,577},{128,384},{129,641},{192,448},{1... | collective-permute-start | bytes 393224 | tf_op jit(solution)/shard_map/ppermute | solution.py:41
  51.9 0.9 copy-start.1
  53.6 20.1 %all-to-all-start = ((bf16[32,8,512]{2,1,0:T(8,128)(2,1)}), bf16[32,8,512]{2,1,0:T(8,128)(2,1)S(1)}, u32[]{:S(2)}, u32[]{:S(2)}) async-start(bf16[32,8,512]{2,1,0:T(8,128)(2,1)} %shard_map.39), calls=%async_computation | async-start | bytes 524288 | tf_op jit(solution)/shard_map/all_to_all | solution.py:31
  73.7 6.8 %collective-permute-start.8 = (bf16[32,8,512]{2,1,0:T(8,128)(2,1)S(1)}, bf16[32,8,512]{2,1,0:T(8,128)(2,1)S(1)}, u32[]{:S(2)}, u32[]{:S(2)}) collective-permute-start(bf16[32,8,512]{2,1,0:T(8,128)(2,1)S(1)} %all-to-all-done.mine_ref), channel_id=1, source_target_pairs={{0,1},{1,0},{2,3},{3,2},{4,5},{5,4},{6,7},{7,6},{8,9},{9,8},{10,11... | collective-permute-start | bytes 786440 | tf_op jit(solution)/shard_map/ppermute | solution.py:253
  84.4 11.5 %all-to-all-start.1 = ((bf16[16,8,512]{2,1,0:T(8,128)(2,1)}), bf16[16,8,512]{2,1,0:T(8,128)(2,1)S(1)}, u32[]{:S(2)}, u32[]{:S(2)}) async-start(bf16[16,8,512]{2,1,0:T(8,128)(2,1)} %shard_map.40), calls=%async_computation.1 | async-start | bytes 262144 | tf_op jit(solution)/shard_map/all_to_all | solution.py:31
  97.2 22.0 %all-to-all-start.2 = ((bf16[36,8,512]{2,1,0:T(8,128)(2,1)}), bf16[36,8,512]{2,1,0:T(8,128)(2,1)S(1)}, u32[]{:S(2)}, u32[]{:S(2)}) async-start(bf16[36,8,512]{2,1,0:T(8,128)(2,1)} %gather_fusion), calls=%async_computation.2 | async-start | bytes 589824 | tf_op jit(solution)/shard_map/all_to_all | solution.py:31

commit v6 on v5

v6 whole, which is shorter than its diff:
```python
import math

import jax
import jax.numpy as jnp
from jax import lax
from jax.experimental import pallas as pl
from jax.experimental.pallas import tpu as pltpu
from jax.sharding import Mesh
from jax.sharding import PartitionSpec as P

ITERS = 3
PAIR = 3
TENSOR = ("yb", "ya", "tx", "tc")
CHIPS = ("yb", "ya", "tx")
HOLD = ("ya", "tx")
SPLIT = (2, 4, 4, 2)
VMEM_LIMIT = 12 * 1024 * 1024
PLACES = ((5, -3, 2), (-5, 3, -2), (6,), (4, -4, 1, -1), (0,))


decay_rate = 0.95
newton_a = 3.4445
newton_b = -4.775
newton_c = 2.0315
norm_eps = 1e-07


def exchange(pieces, axes):
    return lax.all_to_all(pieces, axes, split_axis=0, concat_axis=0, tiled=True)


def mirrored(pieces, step):
    count, cores = lax.axis_size("dp"), lax.axis_size("tc")
    pairs = [
        (i * cores + core, (i + (step if core else -step)) % count * cores + core)
        for i in range(count)
        for core in range(cores)
    ]
    return lax.ppermute(pieces, ("dp", "tc"), pairs)


def ranks_of(labels):
    length = labels.shape[0]
    places = jnp.arange(length, dtype=jnp.int32)
    earlier = (labels[None, :] == labels[:, None]) & (places[None, :] < places[:, None])
    return jnp.sum(earlier.astype(jnp.int32), axis=1)


def call(kernel, name, outs, ins, scratch=(), flops=0, size=0, limit=VMEM_LIMIT):
    vmem = pl.BlockSpec(memory_space=pltpu.VMEM)
    return pl.pallas_call(
        kernel,
        out_shape=outs,
        in_specs=[vmem if space is None else pl.BlockSpec(memory_space=space) for space in ins],
        out_specs=jax.tree.map(lambda _: vmem, outs),
        scratch_shapes=list(scratch),
        cost_estimate=pl.CostEstimate(flops=flops, bytes_accessed=size, transcendentals=0),
        compiler_params=pltpu.CompilerParams(vmem_limit_bytes=limit),
        name=name,
    )


def join_kernel(owners_ref, pieces_ref, momentum_ref, *refs):
    *outs, held_owners, found_ref, bounds_ref, slots_ref, sems = refs
    weight = decay_rate * decay_rate / (1.0 + decay_rate)
    count, per_group = pieces_ref.shape[:2]
    me = lax.axis_index("dp")
    side = 2 * lax.axis_index("tc") - 1
    table = pltpu.make_async_copy(owners_ref, held_owners, sems.at[0])
    table.start()
    slots = pltpu.make_async_copy(momentum_ref, slots_ref, sems.at[1])
    slots.start()
    jobs = []
    for out, aways in zip(outs, PLACES):
        for index, away in enumerate(aways):
            group = lax.rem(me + away * side + count, count)
            copy = pltpu.make_async_copy(
                pieces_ref.at[group], out.at[index], sems.at[2 + len(jobs)]
            )
            jobs.append((copy, group, out.at[index]))
    for copy, _, _ in jobs:
        copy.start()
    table.wait()
    found = jnp.int32(0)
    for group in range(count):
        bounds_ref[group] = found
        for inside in range(per_group):
            found_ref[found] = inside
            found = found + (held_owners[group * per_group + inside] == me).astype(jnp.int32)
    bounds_ref[count] = found
    slots.wait()
    for copy, group, target in jobs:
        copy.wait()

        def add(slot, carry, target=target):
            inside = found_ref[slot]
            extra = weight * slots_ref[slot].astype(jnp.float32)
            target[inside] = (target[inside].astype(jnp.float32) + extra).astype(target.dtype)
            return carry

        lax.fori_loop(bounds_ref[group], bounds_ref[group + 1], add, 0)


def join_momentum(pieces, momentum, owners):
    count, *inside = pieces.shape
    outs = [jax.ShapeDtypeStruct((len(aways), *inside), pieces.dtype) for aways in PLACES]
    scratch = [
        pltpu.SMEM(owners.shape, jnp.int32),
        pltpu.SMEM((owners.shape[0] + 1,), jnp.int32),
        pltpu.SMEM((count + 1,), jnp.int32),
        pltpu.VMEM(momentum.shape, momentum.dtype),
        pltpu.SemaphoreType.DMA((2 + count,)),
    ]
    hbm = [pltpu.with_memory_space_constraint(x, pltpu.HBM) for x in (owners, pieces, momentum)]
    size = 2 * pieces.size
    return call(join_kernel, "join_momentum", outs, [pltpu.HBM] * 3, scratch, size, 2 * size)(*hbm)


def combine_kernel(one_ref, two_ref, three_ref, kept_ref, *outs):
    wide = lambda ref, index, block: ref[index, block].astype(jnp.float32)
    for block in range(kept_ref.shape[1]):
        ahead = wide(one_ref, 0, block) + wide(two_ref, 1, block) + wide(three_ref, 0, block)
        behind = wide(one_ref, 1, block) + wide(two_ref, 0, block)
        sums = (ahead, behind, wide(one_ref, 2, block), wide(two_ref, 2, block))
        for index, (out, total) in enumerate(zip(outs, sums)):
            out[block] = (wide(kept_ref, index, block) + total).astype(out.dtype)


def combine(arrived, kept):
    outs = [jax.ShapeDtypeStruct(kept.shape[1:], kept.dtype)] * kept.shape[0]
    size = 3 * kept.size
    return call(combine_kernel, "combine_terms", outs, [None] * 4, (), size, 2 * size)(*arrived, kept)


def spread_kernel(*refs):
    own_ref, *terms, out_ref = refs
    blocks = own_ref.shape[1]
    for block in range(blocks):
        total = own_ref[0, block].astype(jnp.float32)
        for term in terms:
            total = total + term[block].astype(jnp.float32)
        total = total.astype(out_ref.dtype)
        for copy in range(SPLIT[0]):
            out_ref[copy * blocks + block] = total


def spread(own, terms):
    blocks, *inside = own.shape[1:]
    out = jax.ShapeDtypeStruct((blocks * SPLIT[0], *inside), own.dtype)
    ins = [None] * (1 + len(terms))
    size = len(ins) * own.size
    return call(spread_kernel, "spread_sum", out, ins, (), size, 2 * size)(own, *terms)


def sum_at_holder(one, two, three, kept, own):
    arrived = (mirrored(one, 1), mirrored(two, -1), mirrored(three, 2))
    sums = combine(arrived, kept)
    return spread(own, [mirrored(total, step) for total, step in zip(sums, (4, -4, 1, -1))])


def iterate_kernel(mine_ref, other_ref, out_ref, wide_ref):
    count, piece_rows, width = mine_ref.shape
    slab = count * piece_rows // SPLIT[0]
    square = jnp.zeros((piece_rows, width), jnp.float32)
    for side, ref in enumerate((mine_ref, other_ref)):
        for index in range(count):
            piece = ref[index].astype(jnp.float32)
            square = square + piece * piece
            row = (side * count + index) * piece_rows
            wide_ref[row : row + piece_rows, :] = piece
    blend = 1.0 + decay_rate
    total = jnp.sum(jnp.sum(square, axis=0, keepdims=True), axis=1, keepdims=True)
    scale = blend / (blend * jnp.sqrt(total) + norm_eps)
    wide_ref[...] = wide_ref[...] * scale

    def dot(left, right, across):
        return lax.dot_general(
            left, right, (((1,), (across,)), ((), ())), preferred_element_type=jnp.float32
        )

    narrow = lambda value: value.astype(jnp.bfloat16)
    for iteration in range(ITERS):
        last = iteration == ITERS - 1
        current = wide_ref[...]
        currents = narrow(current)
        if last:
            kept = wide_ref[pl.ds(lax.axis_index("yb") * slab, slab), :]
            mine = dot(narrow(kept), currents, 1)
            squared = narrow(dot(currents, currents, 1))
            polynomial = newton_b * mine + newton_c * dot(narrow(mine), squared, 0)
        else:
            kept = current
            mine = dot(currents, currents, 1)
            squared = narrow(mine)
            polynomial = newton_b * mine + newton_c * dot(squared, squared, 0)
        following = newton_a * kept + dot(narrow(polynomial), currents, 0)
        if not last:
            wide_ref[...] = following
    result = following * math.sqrt(width)
    for piece in range(slab // piece_rows):
        rows = result[piece * piece_rows : (piece + 1) * piece_rows, :]
        out_ref[piece] = rows.astype(out_ref.dtype)


def iterate(mine, other):
    count, piece_rows, width = mine.shape
    rows = 2 * count * piece_rows
    out = jax.ShapeDtypeStruct((count // SPLIT[0], piece_rows, width), mine.dtype)
    return call(
        iterate_kernel,
        "iterate_block",
        out,
        [None] * 2,
        [pltpu.VMEM((rows, width), jnp.float32)],
        3 * ITERS * 2 * rows * rows * width,
        4 * rows * width,
    )(mine, other)


def body(gradients, momentum, owners):
    dp_count = lax.axis_size("dp")
    my_group = lax.axis_index("dp")
    pieces = gradients[0]
    blocks_all, piece_rows, width = pieces.shape
    per_group = blocks_all // dp_count
    capacity = momentum.shape[1]
    places = jnp.arange(blocks_all, dtype=jnp.int32)
    slot_rank = ranks_of(owners)
    slot_ids = jnp.arange(capacity, dtype=jnp.int32)
    mine = owners == my_group
    grouped = pieces.reshape(dp_count, per_group, piece_rows, width)
    held = sum_at_holder(*join_momentum(grouped, momentum[0], owners))
    arrived = exchange(held, CHIPS)
    partner = lax.ppermute(arrived, "tc", [(0, 1), (1, 0)])
    back = exchange(iterate(arrived, partner), HOLD)
    groups = jnp.arange(dp_count, dtype=jnp.int32)
    held_owner = lax.dynamic_slice_in_dim(owners, my_group * per_group, per_group)
    held_rank = ranks_of(held_owner)
    held_places = jnp.arange(per_group, dtype=jnp.int32)
    pair_ids = jnp.arange(PAIR, dtype=jnp.int32)
    matched = (held_owner[:, None, None] == groups[None, :, None]) & (
        held_rank[:, None, None] == pair_ids[None, None, :]
    )
    source = jnp.sum(jnp.where(matched, held_places[:, None, None], 0), axis=0).reshape(-1)
    incoming = exchange(jnp.take(back, source, axis=0, mode="clip"), "dp")
    group_rank = ranks_of(owners * dp_count + places // per_group)
    position = places // per_group * PAIR + group_rank
    my_slots = mine[:, None] & (slot_rank[:, None] == slot_ids[None, :])
    arriving = jnp.sum(jnp.where(my_slots, position[:, None], 0), axis=0)
    occupied = jnp.any(my_slots, axis=0)
    chosen = jnp.take(incoming, arriving, axis=0, mode="clip").astype(jnp.float32)
    return jnp.where(occupied[:, None, None], chosen, 0.0)[None]


def solution(mesh):
    split = Mesh(mesh.devices.reshape(mesh.shape["dp"], *SPLIT), ("dp", *TENSOR))
    in_specs = (P("dp", None, TENSOR, None), P("dp", None, TENSOR, None), P())
    out_specs = P("dp", None, TENSOR, None)
    return jax.shard_map(body, mesh=split, in_specs=in_specs, out_specs=out_specs, check_vma=False)
```

time: 123 us -> 119 us (0.967)
  starting transfers between devices: 63 us -> 59.4 us
  waiting for transfers between devices: 44 us -> 47.3 us
  local copies, waits for them, and re-layouts: 3.99 us -> 2.13 us
    ppermute x8 -> x7, waiting for transfers between devices: 11.4 us -> 14.4 us  [mirrored(): return lax.ppermute(pieces, ('dp', 'tc'), pairs)]
    unnamed x6 -> x2, local copies, waits for them, and re-layouts: 1.86 us -> 0.01 us
    ppermute x8 -> x7, starting transfers between devices: 36.6 us -> 34.8 us  [mirrored(): return lax.ppermute(pieces, ('dp', 'tc'), pairs)]
    all_to_all x3, starting transfers between devices: 20.8 us -> 19.5 us  [exchange(): return lax.all_to_all(pieces, axes, split_axis=0, concat_axis=0, tiled=True)]
  transfers between devices with their start and end apart: 12 -> 11, of which waited for: 7 -> 7; matrix products, arithmetic and copies ran while one was open for 1% -> 1% of each run, Pallas kernels for 0% -> 0%
where the time goes in v6:
time: 119 us; the launch traced here: 117 us
  starting transfers between devices  59.4 us (50%)
  waiting for transfers between devices  47.3 us (40%)
  Pallas kernels  6.44 us (5%)
  local copies, waits for them, and re-layouts  2.13 us (2%)
  other arithmetic  1.91 us (2%)
    ppermute x7, starting transfers between devices, mirrored(): return lax.ppermute(pieces, ('dp', 'tc'), pairs)  34.8 us
    all_to_all x3, waiting for transfers between devices, exchange(): return lax.all_to_all(pieces, axes, split_axis=0, concat_axis=0, tiled=True)  32.2 us
    all_to_all x3, starting transfers between devices, exchange(): return lax.all_to_all(pieces, axes, split_axis=0, concat_axis=0, tiled=True)  19.5 us
    ppermute x7, waiting for transfers between devices, mirrored(): return lax.ppermute(pieces, ('dp', 'tc'), pairs)  14.4 us
    ppermute x1, starting transfers between devices, body(): partner = lax.ppermute(arrived, 'tc', [(0, 1), (1, 0)])  5.11 us
    pallas_call x1, Pallas kernels, iterate(): call(iterate_kernel, 'iterate_block', out, [None] * 2, [pltpu.VMEM((rows,...  3.88 us
  transfers between devices with their start and end apart: 11, of which 7 were waited for; matrix products, arithmetic and copies ran while one was open for 1% of the time, Pallas kernels for 0%

profile of v6, /device:TPU:1, one launch (start us, length us, event | category | flops | bytes accessed | tf_op | source)
XLA Modules:
  0.0 117.4 jit_solution(1215631841945255848)
XLA Ops:
  0.0 1.6 %join_momentum.1 = (bf16[3,16,8,512]{3,2,1,0:T(8,128)(2,1)S(1)}, bf16[3,16,8,512]{3,2,1,0:T(8,128)(2,1)S(1)}, bf16[1,16,8,512]{3,2,1,0:T(8,128)(2,1)S(1)}, bf16[...) custom-call(s32[192]{0:T(256)} %owners_ref.1, bf16[12,16,8,512]{3,2,1,0:T(8,128)(2,1)} %bitcast.5, ...), custom_call_target="tpu_custom_call" | custom-call | flops 1572864 | bytes 3145728 | tf_op jit(solution)/shard_map/join_momentum/pallas_call | solution.py:116
  1.6 4.8 %collective-permute-start = (bf16[3,16,8,512]{3,2,1,0:T(8,128)(2,1)S(1)}, bf16[3,16,8,512]{3,2,1,0:T(8,128)(2,1)S(1)}, u32[]{:S(2)}, u32[]{:S(2)}) collective-permute-start(bf16[3,16,8,512]{3,2,1,0:T(8,128)(2,1)S(1)} %get-tuple-element.15), channel_id=1, source_target_pairs={{0,704},{1,65},{64,0},{65,129},{128,64},{129,193},{192,128},{193,2... | collective-permute-start | bytes 1179656 | tf_op jit(solution)/shard_map/ppermute | solution.py:39
  6.4 12.2 %collective-permute-start.1 = (bf16[3,16,8,512]{3,2,1,0:T(8,128)(2,1)S(1)}, bf16[3,16,8,512]{3,2,1,0:T(8,128)(2,1)S(1)}, u32[]{:S(2)}, u32[]{:S(2)}) collective-permute-start(bf16[3,16,8,512]{3,2,1,0:T(8,128)(2,1)S(1)} %get-tuple-element.16), channel_id=1, source_target_pairs={{0,64},{1,705},{64,128},{65,1},{128,192},{129,65},{192,256},{193,1... | collective-permute-start | bytes 1179656 | tf_op jit(solution)/shard_map/ppermute | solution.py:39
  18.7 1.9 %collective-permute-start.2 = (bf16[1,16,8,512]{3,2,1,0:T(8,128)(2,1)S(1)}, bf16[1,16,8,512]{3,2,1,0:T(8,128)(2,1)S(1)}, u32[]{:S(2)}, u32[]{:S(2)}) collective-permute-start(bf16[1,16,8,512]{3,2,1,0:T(8,128)(2,1)S(1)} %get-tuple-element.17), channel_id=1, source_target_pairs={{0,640},{1,129},{64,704},{65,193},{128,0},{129,257},{192,64},{193,... | collective-permute-start | bytes 393224 | tf_op jit(solution)/shard_map/ppermute | solution.py:39
  20.6 8.7 %collective-permute-done.2.three_ref = bf16[1,16,8,512]{3,2,1,0:T(8,128)(2,1)S(1)} collective-permute-done((bf16[1,16,8,512]{3,2,1,0:T(8,128)(2,1)S(1)}, bf16[1,16,8,512]{3,2,1,0:T(8,128)(2,1)S(1)}, u32[]{:S(2)}, u32[]{:S(2)}) %collective-permute-start.2) | collective-permute-done | bytes 131104 | tf_op jit(solution)/shard_map/ppermute | solution.py:39
  29.3 0.2 combine_terms.1
  29.5 1.9 %collective-permute-start.3 = (bf16[16,8,512]{2,1,0:T(8,128)(2,1)S(1)}, bf16[16,8,512]{2,1,0:T(8,128)(2,1)S(1)}, u32[]{:S(2)}, u32[]{:S(2)}) collective-permute-start(bf16[16,8,512]{2,1,0:T(8,128)(2,1)S(1)} %get-tuple-element.19), channel_id=1, source_target_pairs={{0,512},{1,257},{64,576},{65,321},{128,640},{129,385},{192,704},{1... | collective-permute-start | bytes 393224 | tf_op jit(solution)/shard_map/ppermute | solution.py:39
  31.4 7.3 %collective-permute-start.4 = (bf16[16,8,512]{2,1,0:T(8,128)(2,1)S(1)}, bf16[16,8,512]{2,1,0:T(8,128)(2,1)S(1)}, u32[]{:S(2)}, u32[]{:S(2)}) collective-permute-start(bf16[16,8,512]{2,1,0:T(8,128)(2,1)S(1)} %get-tuple-element.20), channel_id=1, source_target_pairs={{0,256},{1,513},{64,320},{65,577},{128,384},{129,641},{192,448},{1... | collective-permute-start | bytes 393224 | tf_op jit(solution)/shard_map/ppermute | solution.py:39
  38.7 1.9 %collective-permute-start.5 = (bf16[16,8,512]{2,1,0:T(8,128)(2,1)S(1)}, bf16[16,8,512]{2,1,0:T(8,128)(2,1)S(1)}, u32[]{:S(2)}, u32[]{:S(2)}) collective-permute-start(bf16[16,8,512]{2,1,0:T(8,128)(2,1)S(1)} %get-tuple-element.21), channel_id=1, source_target_pairs={{0,704},{1,65},{64,0},{65,129},{128,64},{129,193},{192,128},{193,2... | collective-permute-start | bytes 393224 | tf_op jit(solution)/shard_map/ppermute | solution.py:39
  40.6 4.7 %collective-permute-start.6 = (bf16[16,8,512]{2,1,0:T(8,128)(2,1)S(1)}, bf16[16,8,512]{2,1,0:T(8,128)(2,1)S(1)}, u32[]{:S(2)}, u32[]{:S(2)}) collective-permute-start(bf16[16,8,512]{2,1,0:T(8,128)(2,1)S(1)} %get-tuple-element.22), channel_id=1, source_target_pairs={{0,64},{1,705},{64,128},{65,1},{128,192},{129,65},{192,256},{193,1... | collective-permute-start | bytes 393224 | tf_op jit(solution)/shard_map/ppermute | solution.py:39
  45.3 4.4 %collective-permute-done.4.refs_2_ = bf16[16,8,512]{2,1,0:T(8,128)(2,1)S(1)} collective-permute-done((bf16[16,8,512]{2,1,0:T(8,128)(2,1)S(1)}, bf16[16,8,512]{2,1,0:T(8,128)(2,1)S(1)}, u32[]{:S(2)}, u32[]{:S(2)}) %collective-permute-start.4) | collective-permute-done | bytes 131104 | tf_op jit(solution)/shard_map/ppermute | solution.py:39
  49.8 1.3 %collective-permute-done.6.refs_4_ = bf16[16,8,512]{2,1,0:T(8,128)(2,1)S(1)} collective-permute-done((bf16[16,8,512]{2,1,0:T(8,128)(2,1)S(1)}, bf16[16,8,512]{2,1,0:T(8,128)(2,1)S(1)}, u32[]{:S(2)}, u32[]{:S(2)}) %collective-permute-start.6) | collective-permute-done | bytes 131104 | tf_op jit(solution)/shard_map/ppermute | solution.py:39
  51.1 0.8 spread_sum.1
  51.9 9.7 %all-to-all-start = ((bf16[32,8,512]{2,1,0:T(8,128)(2,1)}), bf16[32,8,512]{2,1,0:T(8,128)(2,1)S(1)}, u32[]{:S(2)}, u32[]{:S(2)}) async-start(bf16[32,8,512]{2,1,0:T(8,128)(2,1)} %spread_sum.1), calls=%async_computation | async-start | bytes 524288 | tf_op jit(solution)/shard_map/all_to_all | solution.py:29
  61.6 0.2 convert_reduce_fusion.2
  61.9 10.3 %all-to-all-done.mine_ref = bf16[32,8,512]{2,1,0:T(8,128)(2,1)S(1)} async-done(((bf16[32,8,512]{2,1,0:T(8,128)(2,1)}), bf16[32,8,512]{2,1,0:T(8,128)(2,1)S(1)}, u32[]{:S(2)}, u32[]{:S(2)}) %all-to-all-start) | async-done | bytes 262176 | tf_op jit(solution)/shard_map/all_to_all | solution.py:29
  72.2 5.1 %collective-permute-start.7 = (bf16[32,8,512]{2,1,0:T(8,128)(2,1)S(1)}, bf16[32,8,512]{2,1,0:T(8,128)(2,1)S(1)}, u32[]{:S(2)}, u32[]{:S(2)}) collective-permute-start(bf16[32,8,512]{2,1,0:T(8,128)(2,1)S(1)} %all-to-all-done.mine_ref), channel_id=1, source_target_pairs={{0,1},{1,0},{2,3},{3,2},{4,5},{5,4},{6,7},{7,6},{8,9},{9,8},{10,11... | collective-permute-start | bytes 786440 | tf_op jit(solution)/shard_map/ppermute | solution.py:234
  77.4 0.1 select_reduce_fusion.1
  77.5 0.1 copy.4
  77.6 0.2 convert_reduce_fusion.1
  77.8 0.7 collective-permute-done.7.other_ref
  78.5 3.9 %iterate_block.1 = bf16[16,8,512]{2,1,0:T(8,128)(2,1)} custom-call(bf16[32,8,512]{2,1,0:T(8,128)(2,1)S(1)} %all-to-all-done.mine_ref, bf16[32,8,512]{2,1,0:T(8,128)(2,1)S(1)} %collective-permute-done.7.other_ref), custom_call_target="tpu_custom_call" | custom-call | flops 2415919104 | bytes 1048576 | tf_op jit(solution)/shard_map/iterate_block/pallas_call | solution.py:209
  82.4 3.5 %all-to-all-start.1 = ((bf16[16,8,512]{2,1,0:T(8,128)(2,1)}), bf16[16,8,512]{2,1,0:T(8,128)(2,1)S(1)}, u32[]{:S(2)}, u32[]{:S(2)}) async-start(bf16[16,8,512]{2,1,0:T(8,128)(2,1)} %iterate_block.1), calls=%async_computation.1 | async-start | bytes 262144 | tf_op jit(solution)/shard_map/all_to_all | solution.py:29
  85.9 7.9 %all-to-all-done.1 = bf16[16,8,512]{2,1,0:T(8,128)(2,1)S(1)} async-done(((bf16[16,8,512]{2,1,0:T(8,128)(2,1)}), bf16[16,8,512]{2,1,0:T(8,128)(2,1)S(1)}, u32[]{:S(2)}, u32[]{:S(2)}) %all-to-all-start.1) | async-done | bytes 131104 | tf_op jit(solution)/shard_map/all_to_all | solution.py:29
  93.9 1.3 %gather_fusion = bf16[36,8,512]{2,1,0:T(8,128)(2,1)} fusion(bf16[16,8,512]{2,1,0:T(8,128)(2,1)S(1)} %all-to-all-done.1, s32[1024]{0:T(1024)S(1)} %pad_clamp_fusion.1), kind=kCustom, calls=%fused_computation | custom fusion | bytes 589968 | tf_op jit(solution)/shard_map/jit(_take)/gather | solution.py:245
  95.2 6.3 %all-to-all-start.2 = ((bf16[36,8,512]{2,1,0:T(8,128)(2,1)}), bf16[36,8,512]{2,1,0:T(8,128)(2,1)S(1)}, u32[]{:S(2)}, u32[]{:S(2)}) async-start(bf16[36,8,512]{2,1,0:T(8,128)(2,1)} %gather_fusion), calls=%async_computation.2 | async-start | bytes 589824 | tf_op jit(solution)/shard_map/all_to_all | solution.py:29
  101.5 0.2 convert_reduce_fusion
  101.7 0.1 select_reduce_fusion
  101.8 0.1 fusion.3
  101.9 13.9 %all-to-all-done.2 = bf16[36,8,512]{2,1,0:T(8,128)(2,1)S(1)} async-done(((bf16[36,8,512]{2,1,0:T(8,128)(2,1)}), bf16[36,8,512]{2,1,0:T(8,128)(2,1)S(1)}, u32[]{:S(2)}, u32[]{:S(2)}) %all-to-all-start.2) | async-done | bytes 294944 | tf_op jit(solution)/shard_map/all_to_all | solution.py:29
  115.9 0.6 gather_fusion.1
  116.5 0.9 convert_select_fusion
  (15 shorter events, 0.3 us)
Async XLA Ops:
  1.6 59.9 %copy-start = (s32[192]{0:T(256)S(1)}, s32[192]{0:T(256)}, u32[]{:S(2)}) copy-start(s32[192]{0:T(256)} %owners_ref.1) | copy-start | bytes 2308
  1.6 27.7 %collective-permute-start = (bf16[3,16,8,512]{3,2,1,0:T(8,128)(2,1)S(1)}, bf16[3,16,8,512]{3,2,1,0:T(8,128)(2,1)S(1)}, u32[]{:S(2)}, u32[]{:S(2)}) collective-permute-start(bf16[3,16,8,512]{3,2,1,0:T(8,128)(2,1)S(1)} %get-tuple-element.15), channel_id=1, source_target_pairs={{0,704},{1,65},{64,0},{65,129},{128,64},{129,193},{192,128},{193,2... | collective-permute-start | bytes 1179656 | tf_op jit(solution)/shard_map/ppermute | solution.py:39
  6.4 22.9 %collective-permute-start.1 = (bf16[3,16,8,512]{3,2,1,0:T(8,128)(2,1)S(1)}, bf16[3,16,8,512]{3,2,1,0:T(8,128)(2,1)S(1)}, u32[]{:S(2)}, u32[]{:S(2)}) collective-permute-start(bf16[3,16,8,512]{3,2,1,0:T(8,128)(2,1)S(1)} %get-tuple-element.16), channel_id=1, source_target_pairs={{0,64},{1,705},{64,128},{65,1},{128,192},{129,65},{192,256},{193,1... | collective-permute-start | bytes 1179656 | tf_op jit(solution)/shard_map/ppermute | solution.py:39
  18.7 10.6 %collective-permute-start.2 = (bf16[1,16,8,512]{3,2,1,0:T(8,128)(2,1)S(1)}, bf16[1,16,8,512]{3,2,1,0:T(8,128)(2,1)S(1)}, u32[]{:S(2)}, u32[]{:S(2)}) collective-permute-start(bf16[1,16,8,512]{3,2,1,0:T(8,128)(2,1)S(1)} %get-tuple-element.17), channel_id=1, source_target_pairs={{0,640},{1,129},{64,704},{65,193},{128,0},{129,257},{192,64},{193,... | collective-permute-start | bytes 393224 | tf_op jit(solution)/shard_map/ppermute | solution.py:39
  29.5 15.9 %collective-permute-start.3 = (bf16[16,8,512]{2,1,0:T(8,128)(2,1)S(1)}, bf16[16,8,512]{2,1,0:T(8,128)(2,1)S(1)}, u32[]{:S(2)}, u32[]{:S(2)}) collective-permute-start(bf16[16,8,512]{2,1,0:T(8,128)(2,1)S(1)} %get-tuple-element.19), channel_id=1, source_target_pairs={{0,512},{1,257},{64,576},{65,321},{128,640},{129,385},{192,704},{1... | collective-permute-start | bytes 393224 | tf_op jit(solution)/shard_map/ppermute | solution.py:39
  31.4 18.4 %collective-permute-start.4 = (bf16[16,8,512]{2,1,0:T(8,128)(2,1)S(1)}, bf16[16,8,512]{2,1,0:T(8,128)(2,1)S(1)}, u32[]{:S(2)}, u32[]{:S(2)}) collective-permute-start(bf16[16,8,512]{2,1,0:T(8,128)(2,1)S(1)} %get-tuple-element.20), channel_id=1, source_target_pairs={{0,256},{1,513},{64,320},{65,577},{128,384},{129,641},{192,448},{1... | collective-permute-start | bytes 393224 | tf_op jit(solution)/shard_map/ppermute | solution.py:39
  38.7 11.1 %collective-permute-start.5 = (bf16[16,8,512]{2,1,0:T(8,128)(2,1)S(1)}, bf16[16,8,512]{2,1,0:T(8,128)(2,1)S(1)}, u32[]{:S(2)}, u32[]{:S(2)}) collective-permute-start(bf16[16,8,512]{2,1,0:T(8,128)(2,1)S(1)} %get-tuple-element.21), channel_id=1, source_target_pairs={{0,704},{1,65},{64,0},{65,129},{128,64},{129,193},{192,128},{193,2... | collective-permute-start | bytes 393224 | tf_op jit(solution)/shard_map/ppermute | solution.py:39
  40.6 10.5 %collective-permute-start.6 = (bf16[16,8,512]{2,1,0:T(8,128)(2,1)S(1)}, bf16[16,8,512]{2,1,0:T(8,128)(2,1)S(1)}, u32[]{:S(2)}, u32[]{:S(2)}) collective-permute-start(bf16[16,8,512]{2,1,0:T(8,128)(2,1)S(1)} %get-tuple-element.22), channel_id=1, source_target_pairs={{0,64},{1,705},{64,128},{65,1},{128,192},{129,65},{192,256},{193,1... | collective-permute-start | bytes 393224 | tf_op jit(solution)/shard_map/ppermute | solution.py:39
  51.9 20.4 %all-to-all-start = ((bf16[32,8,512]{2,1,0:T(8,128)(2,1)}), bf16[32,8,512]{2,1,0:T(8,128)(2,1)S(1)}, u32[]{:S(2)}, u32[]{:S(2)}) async-start(bf16[32,8,512]{2,1,0:T(8,128)(2,1)} %spread_sum.1), calls=%async_computation | async-start | bytes 524288 | tf_op jit(solution)/shard_map/all_to_all | solution.py:29
  72.2 6.3 %collective-permute-start.7 = (bf16[32,8,512]{2,1,0:T(8,128)(2,1)S(1)}, bf16[32,8,512]{2,1,0:T(8,128)(2,1)S(1)}, u32[]{:S(2)}, u32[]{:S(2)}) collective-permute-start(bf16[32,8,512]{2,1,0:T(8,128)(2,1)S(1)} %all-to-all-done.mine_ref), channel_id=1, source_target_pairs={{0,1},{1,0},{2,3},{3,2},{4,5},{5,4},{6,7},{7,6},{8,9},{9,8},{10,11... | collective-permute-start | bytes 786440 | tf_op jit(solution)/shard_map/ppermute | solution.py:234
  82.4 11.5 %all-to-all-start.1 = ((bf16[16,8,512]{2,1,0:T(8,128)(2,1)}), bf16[16,8,512]{2,1,0:T(8,128)(2,1)S(1)}, u32[]{:S(2)}, u32[]{:S(2)}) async-start(bf16[16,8,512]{2,1,0:T(8,128)(2,1)} %iterate_block.1), calls=%async_computation.1 | async-start | bytes 262144 | tf_op jit(solution)/shard_map/all_to_all | solution.py:29
  95.2 20.7 %all-to-all-start.2 = ((bf16[36,8,512]{2,1,0:T(8,128)(2,1)}), bf16[36,8,512]{2,1,0:T(8,128)(2,1)S(1)}, u32[]{:S(2)}, u32[]{:S(2)}) async-start(bf16[36,8,512]{2,1,0:T(8,128)(2,1)} %gather_fusion), calls=%async_computation.2 | async-start | bytes 589824 | tf_op jit(solution)/shard_map/all_to_all | solution.py:29

commit v7 on v6

--- a/solution.py
+++ b/solution.py
@@ -15,7 +15,7 @@
 HOLD = ("ya", "tx")
 SPLIT = (2, 4, 4, 2)
 VMEM_LIMIT = 12 * 1024 * 1024
-PLACES = ((5, -3, 2), (-5, 3, -2), (6,), (4, -4, 1, -1), (0,))
+PLACES = ((5, -3, 1), (-5, 3, -1), (6,), (2,), (-2,), (4, -4), (0,))
 
 
 decay_rate = 0.95
@@ -46,7 +46,7 @@
     return jnp.sum(earlier.astype(jnp.int32), axis=1)
 
 
-def call(kernel, name, outs, ins, scratch=(), flops=0, size=0, limit=VMEM_LIMIT):
+def call(kernel, outs, ins, scratch=(), flops=0, size=0, limit=VMEM_LIMIT):
     vmem = pl.BlockSpec(memory_space=pltpu.VMEM)
     return pl.pallas_call(
         kernel,
@@ -56,7 +56,6 @@
         scratch_shapes=list(scratch),
         cost_estimate=pl.CostEstimate(flops=flops, bytes_accessed=size, transcendentals=0),
         compiler_params=pltpu.CompilerParams(vmem_limit_bytes=limit),
-        name=name,
     )
 
 
@@ -113,49 +112,49 @@
     ]
     hbm = [pltpu.with_memory_space_constraint(x, pltpu.HBM) for x in (owners, pieces, momentum)]
     size = 2 * pieces.size
-    return call(join_kernel, "join_momentum", outs, [pltpu.HBM] * 3, scratch, size, 2 * size)(*hbm)
-
-
-def combine_kernel(one_ref, two_ref, three_ref, kept_ref, *outs):
+    return call(join_kernel, outs, [pltpu.HBM] * 3, scratch, size, 2 * size)(*hbm)
+
+
+def combine_kernel(one_ref, two_ref, three_ref, kept_ref, ahead_ref, behind_ref):
     wide = lambda ref, index, block: ref[index, block].astype(jnp.float32)
     for block in range(kept_ref.shape[1]):
         ahead = wide(one_ref, 0, block) + wide(two_ref, 1, block) + wide(three_ref, 0, block)
         behind = wide(one_ref, 1, block) + wide(two_ref, 0, block)
-        sums = (ahead, behind, wide(one_ref, 2, block), wide(two_ref, 2, block))
-        for index, (out, total) in enumerate(zip(outs, sums)):
-            out[block] = (wide(kept_ref, index, block) + total).astype(out.dtype)
+        ahead_ref[block] = (wide(kept_ref, 0, block) + ahead).astype(ahead_ref.dtype)
+        behind_ref[block] = (wide(kept_ref, 1, block) + behind).astype(behind_ref.dtype)
 
 
 def combine(arrived, kept):
     outs = [jax.ShapeDtypeStruct(kept.shape[1:], kept.dtype)] * kept.shape[0]
-    size = 3 * kept.size
-    return call(combine_kernel, "combine_terms", outs, [None] * 4, (), size, 2 * size)(*arrived, kept)
+    size = 4 * kept.size
+    return call(combine_kernel, outs, [None] * 4, (), size, 2 * size)(*arrived, kept)
 
 
 def spread_kernel(*refs):
-    own_ref, *terms, out_ref = refs
-    blocks = own_ref.shape[1]
+    *terms, out_ref = refs
+    blocks = terms[0].shape[1]
     for block in range(blocks):
-        total = own_ref[0, block].astype(jnp.float32)
-        for term in terms:
-            total = total + term[block].astype(jnp.float32)
+        total = terms[0][terms[0].shape[0] - 1, block].astype(jnp.float32)
+        for term in terms[1:]:
+            total = total + term[term.shape[0] - 1, block].astype(jnp.float32)
         total = total.astype(out_ref.dtype)
         for copy in range(SPLIT[0]):
             out_ref[copy * blocks + block] = total
 
 
-def spread(own, terms):
-    blocks, *inside = own.shape[1:]
-    out = jax.ShapeDtypeStruct((blocks * SPLIT[0], *inside), own.dtype)
-    ins = [None] * (1 + len(terms))
-    size = len(ins) * own.size
-    return call(spread_kernel, "spread_sum", out, ins, (), size, 2 * size)(own, *terms)
-
-
-def sum_at_holder(one, two, three, kept, own):
-    arrived = (mirrored(one, 1), mirrored(two, -1), mirrored(three, 2))
-    sums = combine(arrived, kept)
-    return spread(own, [mirrored(total, step) for total, step in zip(sums, (4, -4, 1, -1))])
+def spread(terms):
+    blocks, *inside = terms[0].shape[1:]
+    out = jax.ShapeDtypeStruct((blocks * SPLIT[0], *inside), terms[0].dtype)
+    size = len(terms) * blocks * math.prod(inside)
+    return call(spread_kernel, out, [None] * len(terms), (), size, 2 * size)(*terms)
+
+
+def sum_at_holder(one, two, three, four, five, kept, own):
+    corner = mirrored(three, 2)
+    arrived = (mirrored(one, 1), mirrored(two, -1), corner)
+    direct = [mirrored(four, 2), mirrored(five, -2)]
+    sums = [mirrored(total, step)[None] for total, step in zip(combine(arrived, kept), (4, -4))]
+    return spread([own, *arrived[:2], *direct, *sums])
 
 
 def iterate_kernel(mine_ref, other_ref, out_ref, wide_ref):
@@ -208,7 +207,6 @@
     out = jax.ShapeDtypeStruct((count // SPLIT[0], piece_rows, width), mine.dtype)
     return call(
         iterate_kernel,
-        "iterate_block",
         out,
         [None] * 2,
         [pltpu.VMEM((rows, width), jnp.float32)],

time: 119 us -> 117 us (0.983)
  waiting for transfers between devices: 47.3 us -> 43.3 us
  starting transfers between devices: 59.4 us -> 61.4 us
    ppermute x7, waiting for transfers between devices: 14.4 us -> 10.7 us  [mirrored(): return lax.ppermute(pieces, ('dp', 'tc'), pairs)]
    ppermute x1, starting transfers between devices: 5.11 us -> 7.46 us  [body(): partner = lax.ppermute(arrived, 'tc', [(0, 1), (1, 0)])]
where the time goes in v7:
time: 117 us; the launch traced here: 115 us
  starting transfers between devices  61.4 us (52%)
  waiting for transfers between devices  43.3 us (37%)
  Pallas kernels  6.43 us (5%)
  local copies, waits for them, and re-layouts  2.13 us (2%)
  other arithmetic  1.91 us (2%)
    ppermute x7, starting transfers between devices, mirrored(): return lax.ppermute(pieces, ('dp', 'tc'), pairs)  35.5 us
    all_to_all x3, waiting for transfers between devices, exchange(): return lax.all_to_all(pieces, axes, split_axis=0, concat_axis=0, tiled=True)  31.9 us
    all_to_all x3, starting transfers between devices, exchange(): return lax.all_to_all(pieces, axes, split_axis=0, concat_axis=0, tiled=True)  18.4 us
    ppermute x7, waiting for transfers between devices, mirrored(): return lax.ppermute(pieces, ('dp', 'tc'), pairs)  10.7 us
    ppermute x1, starting transfers between devices, body(): partner = lax.ppermute(arrived, 'tc', [(0, 1), (1, 0)])  7.46 us
    pallas_call x1, Pallas kernels, iterate(): call(iterate_kernel, out, [None] * 2, [pltpu.VMEM((rows, width), jnp.floa...  3.88 us
  transfers between devices with their start and end apart: 11, of which 7 were waited for; matrix products, arithmetic and copies ran while one was open for 1% of the time, Pallas kernels for 0%

profile of v7, /device:TPU:1, one launch (start us, length us, event | category | flops | bytes accessed | tf_op | source)
XLA Modules:
  0.0 115.4 jit_solution(954536265958746915)
XLA Ops:
  0.0 1.6 %shard_map.37 = (bf16[3,16,8,512]{3,2,1,0:T(8,128)(2,1)S(1)}, bf16[3,16,8,512]{3,2,1,0:T(8,128)(2,1)S(1)}, bf16[1,16,8,512]{3,2,1,0:T(8,128)(2,1)S(1)}, bf16[1,1...) custom-call(s32[192]{0:T(256)} %owners_ref.1, ...), custom_call_target="tpu_custom_call" | custom-call | flops 1572864 | bytes 3145728 | tf_op jit(solution)/shard_map/pallas_call | solution.py:115
  1.6 4.8 %collective-permute-start = (bf16[3,16,8,512]{3,2,1,0:T(8,128)(2,1)S(1)}, bf16[3,16,8,512]{3,2,1,0:T(8,128)(2,1)S(1)}, u32[]{:S(2)}, u32[]{:S(2)}) collective-permute-start(bf16[3,16,8,512]{3,2,1,0:T(8,128)(2,1)S(1)} %get-tuple-element.15), channel_id=1, source_target_pairs={{0,704},{1,65},{64,0},{65,129},{128,64},{129,193},{192,128},{193,2... | collective-permute-start | bytes 1179656 | tf_op jit(solution)/shard_map/ppermute | solution.py:39
  6.4 12.2 %collective-permute-start.1 = (bf16[3,16,8,512]{3,2,1,0:T(8,128)(2,1)S(1)}, bf16[3,16,8,512]{3,2,1,0:T(8,128)(2,1)S(1)}, u32[]{:S(2)}, u32[]{:S(2)}) collective-permute-start(bf16[3,16,8,512]{3,2,1,0:T(8,128)(2,1)S(1)} %get-tuple-element.16), channel_id=1, source_target_pairs={{0,64},{1,705},{64,128},{65,1},{128,192},{129,65},{192,256},{193,1... | collective-permute-start | bytes 1179656 | tf_op jit(solution)/shard_map/ppermute | solution.py:39
  18.7 1.9 %collective-permute-start.4 = (bf16[1,16,8,512]{3,2,1,0:T(8,128)(2,1)S(1)}, bf16[1,16,8,512]{3,2,1,0:T(8,128)(2,1)S(1)}, u32[]{:S(2)}, u32[]{:S(2)}) collective-permute-start(bf16[1,16,8,512]{3,2,1,0:T(8,128)(2,1)S(1)} %get-tuple-element.19), channel_id=1, source_target_pairs={{0,640},{1,129},{64,704},{65,193},{128,0},{129,257},{192,64},{193,... | collective-permute-start | bytes 393224 | tf_op jit(solution)/shard_map/ppermute | solution.py:39
  20.6 1.9 %collective-permute-start.2 = (bf16[1,16,8,512]{3,2,1,0:T(8,128)(2,1)S(1)}, bf16[1,16,8,512]{3,2,1,0:T(8,128)(2,1)S(1)}, u32[]{:S(2)}, u32[]{:S(2)}) collective-permute-start(bf16[1,16,8,512]{3,2,1,0:T(8,128)(2,1)S(1)} %get-tuple-element.17), channel_id=1, source_target_pairs={{0,640},{1,129},{64,704},{65,193},{128,0},{129,257},{192,64},{193,... | collective-permute-start | bytes 393224 | tf_op jit(solution)/shard_map/ppermute | solution.py:39
  22.5 5.5 %collective-permute-start.3 = (bf16[1,16,8,512]{3,2,1,0:T(8,128)(2,1)S(1)}, bf16[1,16,8,512]{3,2,1,0:T(8,128)(2,1)S(1)}, u32[]{:S(2)}, u32[]{:S(2)}) collective-permute-start(bf16[1,16,8,512]{3,2,1,0:T(8,128)(2,1)S(1)} %get-tuple-element.18), channel_id=1, source_target_pairs={{0,128},{1,641},{64,192},{65,705},{128,256},{129,1},{192,320},{193... | collective-permute-start | bytes 393224 | tf_op jit(solution)/shard_map/ppermute | solution.py:39
  28.0 1.3 %collective-permute-done.4.three_ref = bf16[1,16,8,512]{3,2,1,0:T(8,128)(2,1)S(1)} collective-permute-done((bf16[1,16,8,512]{3,2,1,0:T(8,128)(2,1)S(1)}, bf16[1,16,8,512]{3,2,1,0:T(8,128)(2,1)S(1)}, u32[]{:S(2)}, u32[]{:S(2)}) %collective-permute-start.4) | collective-permute-done | bytes 131104 | tf_op jit(solution)/shard_map/ppermute | solution.py:39
  29.3 0.1 shard_map.38
  29.4 2.7 %collective-permute-start.5 = (bf16[16,8,512]{2,1,0:T(8,128)(2,1)S(1)}, bf16[16,8,512]{2,1,0:T(8,128)(2,1)S(1)}, u32[]{:S(2)}, u32[]{:S(2)}) collective-permute-start(bf16[16,8,512]{2,1,0:T(8,128)(2,1)S(1)} %get-tuple-element.21), channel_id=1, source_target_pairs={{0,512},{1,257},{64,576},{65,321},{128,640},{129,385},{192,704},{1... | collective-permute-start | bytes 393224 | tf_op jit(solution)/shard_map/ppermute | solution.py:39
  32.1 6.5 %collective-permute-start.6 = (bf16[16,8,512]{2,1,0:T(8,128)(2,1)S(1)}, bf16[16,8,512]{2,1,0:T(8,128)(2,1)S(1)}, u32[]{:S(2)}, u32[]{:S(2)}) collective-permute-start(bf16[16,8,512]{2,1,0:T(8,128)(2,1)S(1)} %get-tuple-element.22), channel_id=1, source_target_pairs={{0,256},{1,513},{64,320},{65,577},{128,384},{129,641},{192,448},{1... | collective-permute-start | bytes 393224 | tf_op jit(solution)/shard_map/ppermute | solution.py:39
  38.6 0.7 collective-permute-done.5
  39.3 8.7 %collective-permute-done.6 = bf16[16,8,512]{2,1,0:T(8,128)(2,1)S(1)} collective-permute-done((bf16[16,8,512]{2,1,0:T(8,128)(2,1)S(1)}, bf16[16,8,512]{2,1,0:T(8,128)(2,1)S(1)}, u32[]{:S(2)}, u32[]{:S(2)}) %collective-permute-start.6) | collective-permute-done | bytes 131104 | tf_op jit(solution)/shard_map/ppermute | solution.py:39
  48.0 0.8 shard_map.39
  48.8 9.7 %all-to-all-start = ((bf16[32,8,512]{2,1,0:T(8,128)(2,1)}), bf16[32,8,512]{2,1,0:T(8,128)(2,1)S(1)}, u32[]{:S(2)}, u32[]{:S(2)}) async-start(bf16[32,8,512]{2,1,0:T(8,128)(2,1)} %shard_map.39), calls=%async_computation | async-start | bytes 524288 | tf_op jit(solution)/shard_map/all_to_all | solution.py:29
  58.6 0.2 convert_reduce_fusion.2
  58.9 10.0 %all-to-all-done.mine_ref = bf16[32,8,512]{2,1,0:T(8,128)(2,1)S(1)} async-done(((bf16[32,8,512]{2,1,0:T(8,128)(2,1)}), bf16[32,8,512]{2,1,0:T(8,128)(2,1)S(1)}, u32[]{:S(2)}, u32[]{:S(2)}) %all-to-all-start) | async-done | bytes 262176 | tf_op jit(solution)/shard_map/all_to_all | solution.py:29
  68.9 7.5 %collective-permute-start.7 = (bf16[32,8,512]{2,1,0:T(8,128)(2,1)S(1)}, bf16[32,8,512]{2,1,0:T(8,128)(2,1)S(1)}, u32[]{:S(2)}, u32[]{:S(2)}) collective-permute-start(bf16[32,8,512]{2,1,0:T(8,128)(2,1)S(1)} %all-to-all-done.mine_ref), channel_id=1, source_target_pairs={{0,1},{1,0},{2,3},{3,2},{4,5},{5,4},{6,7},{7,6},{8,9},{9,8},{10,11... | collective-permute-start | bytes 786440 | tf_op jit(solution)/shard_map/ppermute | solution.py:232
  76.4 0.1 select_reduce_fusion.1
  76.5 0.1 copy.4
  76.7 0.2 convert_reduce_fusion.1
  76.9 0.7 collective-permute-done.7.other_ref
  77.5 3.9 %shard_map.40 = bf16[16,8,512]{2,1,0:T(8,128)(2,1)} custom-call(bf16[32,8,512]{2,1,0:T(8,128)(2,1)S(1)} %all-to-all-done.mine_ref, bf16[32,8,512]{2,1,0:T(8,128)(2,1)S(1)} %collective-permute-done.7.other_ref), custom_call_target="tpu_custom_call" | custom-call | flops 2415919104 | bytes 1048576 | tf_op jit(solution)/shard_map/pallas_call | solution.py:208
  81.4 3.5 %all-to-all-start.1 = ((bf16[16,8,512]{2,1,0:T(8,128)(2,1)}), bf16[16,8,512]{2,1,0:T(8,128)(2,1)S(1)}, u32[]{:S(2)}, u32[]{:S(2)}) async-start(bf16[16,8,512]{2,1,0:T(8,128)(2,1)} %shard_map.40), calls=%async_computation.1 | async-start | bytes 262144 | tf_op jit(solution)/shard_map/all_to_all | solution.py:29
  85.0 8.0 %all-to-all-done.1 = bf16[16,8,512]{2,1,0:T(8,128)(2,1)S(1)} async-done(((bf16[16,8,512]{2,1,0:T(8,128)(2,1)}), bf16[16,8,512]{2,1,0:T(8,128)(2,1)S(1)}, u32[]{:S(2)}, u32[]{:S(2)}) %all-to-all-start.1) | async-done | bytes 131104 | tf_op jit(solution)/shard_map/all_to_all | solution.py:29
  92.9 1.3 %gather_fusion = bf16[36,8,512]{2,1,0:T(8,128)(2,1)} fusion(bf16[16,8,512]{2,1,0:T(8,128)(2,1)S(1)} %all-to-all-done.1, s32[1024]{0:T(1024)S(1)} %pad_clamp_fusion.1), kind=kCustom, calls=%fused_computation | custom fusion | bytes 589968 | tf_op jit(solution)/shard_map/jit(_take)/gather | solution.py:243
  94.2 5.2 %all-to-all-start.2 = ((bf16[36,8,512]{2,1,0:T(8,128)(2,1)}), bf16[36,8,512]{2,1,0:T(8,128)(2,1)S(1)}, u32[]{:S(2)}, u32[]{:S(2)}) async-start(bf16[36,8,512]{2,1,0:T(8,128)(2,1)} %gather_fusion), calls=%async_computation.2 | async-start | bytes 589824 | tf_op jit(solution)/shard_map/all_to_all | solution.py:29
  99.5 0.2 convert_reduce_fusion
  99.7 0.1 select_reduce_fusion
  99.8 0.1 fusion.3
  99.9 13.9 %all-to-all-done.2 = bf16[36,8,512]{2,1,0:T(8,128)(2,1)S(1)} async-done(((bf16[36,8,512]{2,1,0:T(8,128)(2,1)}), bf16[36,8,512]{2,1,0:T(8,128)(2,1)S(1)}, u32[]{:S(2)}, u32[]{:S(2)}) %all-to-all-start.2) | async-done | bytes 294944 | tf_op jit(solution)/shard_map/all_to_all | solution.py:29
  113.8 0.6 gather_fusion.1
  114.4 0.9 convert_select_fusion
  (15 shorter events, 0.3 us)
Async XLA Ops:
  1.6 27.7 %collective-permute-start = (bf16[3,16,8,512]{3,2,1,0:T(8,128)(2,1)S(1)}, bf16[3,16,8,512]{3,2,1,0:T(8,128)(2,1)S(1)}, u32[]{:S(2)}, u32[]{:S(2)}) collective-permute-start(bf16[3,16,8,512]{3,2,1,0:T(8,128)(2,1)S(1)} %get-tuple-element.15), channel_id=1, source_target_pairs={{0,704},{1,65},{64,0},{65,129},{128,64},{129,193},{192,128},{193,2... | collective-permute-start | bytes 1179656 | tf_op jit(solution)/shard_map/ppermute | solution.py:39
  6.4 22.8 %collective-permute-start.1 = (bf16[3,16,8,512]{3,2,1,0:T(8,128)(2,1)S(1)}, bf16[3,16,8,512]{3,2,1,0:T(8,128)(2,1)S(1)}, u32[]{:S(2)}, u32[]{:S(2)}) collective-permute-start(bf16[3,16,8,512]{3,2,1,0:T(8,128)(2,1)S(1)} %get-tuple-element.16), channel_id=1, source_target_pairs={{0,64},{1,705},{64,128},{65,1},{128,192},{129,65},{192,256},{193,1... | collective-permute-start | bytes 1179656 | tf_op jit(solution)/shard_map/ppermute | solution.py:39
  18.7 10.6 %collective-permute-start.4 = (bf16[1,16,8,512]{3,2,1,0:T(8,128)(2,1)S(1)}, bf16[1,16,8,512]{3,2,1,0:T(8,128)(2,1)S(1)}, u32[]{:S(2)}, u32[]{:S(2)}) collective-permute-start(bf16[1,16,8,512]{3,2,1,0:T(8,128)(2,1)S(1)} %get-tuple-element.19), channel_id=1, source_target_pairs={{0,640},{1,129},{64,704},{65,193},{128,0},{129,257},{192,64},{193,... | collective-permute-start | bytes 393224 | tf_op jit(solution)/shard_map/ppermute | solution.py:39
  20.6 18.0 %collective-permute-start.2 = (bf16[1,16,8,512]{3,2,1,0:T(8,128)(2,1)S(1)}, bf16[1,16,8,512]{3,2,1,0:T(8,128)(2,1)S(1)}, u32[]{:S(2)}, u32[]{:S(2)}) collective-permute-start(bf16[1,16,8,512]{3,2,1,0:T(8,128)(2,1)S(1)} %get-tuple-element.17), channel_id=1, source_target_pairs={{0,640},{1,129},{64,704},{65,193},{128,0},{129,257},{192,64},{193,... | collective-permute-start | bytes 393224 | tf_op jit(solution)/shard_map/ppermute | solution.py:39
  22.5 16.1 %collective-permute-start.3 = (bf16[1,16,8,512]{3,2,1,0:T(8,128)(2,1)S(1)}, bf16[1,16,8,512]{3,2,1,0:T(8,128)(2,1)S(1)}, u32[]{:S(2)}, u32[]{:S(2)}) collective-permute-start(bf16[1,16,8,512]{3,2,1,0:T(8,128)(2,1)S(1)} %get-tuple-element.18), channel_id=1, source_target_pairs={{0,128},{1,641},{64,192},{65,705},{128,256},{129,1},{192,320},{193... | collective-permute-start | bytes 393224 | tf_op jit(solution)/shard_map/ppermute | solution.py:39
  29.3 29.3 %copy-start = (s32[192]{0:T(256)S(1)}, s32[192]{0:T(256)}, u32[]{:S(2)}) copy-start(s32[192]{0:T(256)} %owners_ref.1) | copy-start | bytes 2308
  29.4 9.9 %collective-permute-start.5 = (bf16[16,8,512]{2,1,0:T(8,128)(2,1)S(1)}, bf16[16,8,512]{2,1,0:T(8,128)(2,1)S(1)}, u32[]{:S(2)}, u32[]{:S(2)}) collective-permute-start(bf16[16,8,512]{2,1,0:T(8,128)(2,1)S(1)} %get-tuple-element.21), channel_id=1, source_target_pairs={{0,512},{1,257},{64,576},{65,321},{128,640},{129,385},{192,704},{1... | collective-permute-start | bytes 393224 | tf_op jit(solution)/shard_map/ppermute | solution.py:39
  32.1 15.9 %collective-permute-start.6 = (bf16[16,8,512]{2,1,0:T(8,128)(2,1)S(1)}, bf16[16,8,512]{2,1,0:T(8,128)(2,1)S(1)}, u32[]{:S(2)}, u32[]{:S(2)}) collective-permute-start(bf16[16,8,512]{2,1,0:T(8,128)(2,1)S(1)} %get-tuple-element.22), channel_id=1, source_target_pairs={{0,256},{1,513},{64,320},{65,577},{128,384},{129,641},{192,448},{1... | collective-permute-start | bytes 393224 | tf_op jit(solution)/shard_map/ppermute | solution.py:39
  48.8 20.1 %all-to-all-start = ((bf16[32,8,512]{2,1,0:T(8,128)(2,1)}), bf16[32,8,512]{2,1,0:T(8,128)(2,1)S(1)}, u32[]{:S(2)}, u32[]{:S(2)}) async-start(bf16[32,8,512]{2,1,0:T(8,128)(2,1)} %shard_map.39), calls=%async_computation | async-start | bytes 524288 | tf_op jit(solution)/shard_map/all_to_all | solution.py:29
  68.9 8.6 %collective-permute-start.7 = (bf16[32,8,512]{2,1,0:T(8,128)(2,1)S(1)}, bf16[32,8,512]{2,1,0:T(8,128)(2,1)S(1)}, u32[]{:S(2)}, u32[]{:S(2)}) collective-permute-start(bf16[32,8,512]{2,1,0:T(8,128)(2,1)S(1)} %all-to-all-done.mine_ref), channel_id=1, source_target_pairs={{0,1},{1,0},{2,3},{3,2},{4,5},{5,4},{6,7},{7,6},{8,9},{9,8},{10,11... | collective-permute-start | bytes 786440 | tf_op jit(solution)/shard_map/ppermute | solution.py:232
  81.4 11.5 %all-to-all-start.1 = ((bf16[16,8,512]{2,1,0:T(8,128)(2,1)}), bf16[16,8,512]{2,1,0:T(8,128)(2,1)S(1)}, u32[]{:S(2)}, u32[]{:S(2)}) async-start(bf16[16,8,512]{2,1,0:T(8,128)(2,1)} %shard_map.40), calls=%async_computation.1 | async-start | bytes 262144 | tf_op jit(solution)/shard_map/all_to_all | solution.py:29
  94.2 19.6 %all-to-all-start.2 = ((bf16[36,8,512]{2,1,0:T(8,128)(2,1)}), bf16[36,8,512]{2,1,0:T(8,128)(2,1)S(1)}, u32[]{:S(2)}, u32[]{:S(2)}) async-start(bf16[36,8,512]{2,1,0:T(8,128)(2,1)} %gather_fusion), calls=%async_computation.2 | async-start | bytes 589824 | tf_op jit(solution)/shard_map/all_to_all | solution.py:29

commit v8 on v6

--- a/solution.py
+++ b/solution.py
@@ -46,7 +46,7 @@
     return jnp.sum(earlier.astype(jnp.int32), axis=1)
 
 
-def call(kernel, name, outs, ins, scratch=(), flops=0, size=0, limit=VMEM_LIMIT):
+def call(kernel, outs, ins, scratch=(), flops=0, size=0, limit=VMEM_LIMIT):
     vmem = pl.BlockSpec(memory_space=pltpu.VMEM)
     return pl.pallas_call(
         kernel,
@@ -56,7 +56,6 @@
         scratch_shapes=list(scratch),
         cost_estimate=pl.CostEstimate(flops=flops, bytes_accessed=size, transcendentals=0),
         compiler_params=pltpu.CompilerParams(vmem_limit_bytes=limit),
-        name=name,
     )
 
 
@@ -113,7 +112,13 @@
     ]
     hbm = [pltpu.with_memory_space_constraint(x, pltpu.HBM) for x in (owners, pieces, momentum)]
     size = 2 * pieces.size
-    return call(join_kernel, "join_momentum", outs, [pltpu.HBM] * 3, scratch, size, 2 * size)(*hbm)
+    return call(join_kernel, outs, [pltpu.HBM] * 3, scratch, size, 2 * size)(*hbm)
+
+
+def near_kernel(one_ref, kept_ref, out_ref):
+    for block in range(out_ref.shape[0]):
+        total = kept_ref[2, block].astype(jnp.float32) + one_ref[2, block].astype(jnp.float32)
+        out_ref[block] = total.astype(out_ref.dtype)
 
 
 def combine_kernel(one_ref, two_ref, three_ref, kept_ref, *outs):
@@ -121,15 +126,16 @@
     for block in range(kept_ref.shape[1]):
         ahead = wide(one_ref, 0, block) + wide(two_ref, 1, block) + wide(three_ref, 0, block)
         behind = wide(one_ref, 1, block) + wide(two_ref, 0, block)
-        sums = (ahead, behind, wide(one_ref, 2, block), wide(two_ref, 2, block))
-        for index, (out, total) in enumerate(zip(outs, sums)):
-            out[block] = (wide(kept_ref, index, block) + total).astype(out.dtype)
-
-
-def combine(arrived, kept):
-    outs = [jax.ShapeDtypeStruct(kept.shape[1:], kept.dtype)] * kept.shape[0]
-    size = 3 * kept.size
-    return call(combine_kernel, "combine_terms", outs, [None] * 4, (), size, 2 * size)(*arrived, kept)
+        sums = (ahead, behind, wide(two_ref, 2, block))
+        for kept, out, total in zip((0, 1, 3), outs, sums):
+            out[block] = (wide(kept_ref, kept, block) + total).astype(out.dtype)
+
+
+def combine(kernel, count, *terms):
+    outs = [jax.ShapeDtypeStruct(terms[0].shape[1:], terms[0].dtype)] * count
+    size = 3 * count * math.prod(outs[0].shape)
+    ins = [None] * len(terms)
+    return call(kernel, outs, ins, (), size, 2 * size)(*terms)
 
 
 def spread_kernel(*refs):
@@ -149,13 +155,17 @@
     out = jax.ShapeDtypeStruct((blocks * SPLIT[0], *inside), own.dtype)
     ins = [None] * (1 + len(terms))
     size = len(ins) * own.size
-    return call(spread_kernel, "spread_sum", out, ins, (), size, 2 * size)(own, *terms)
+    return call(spread_kernel, out, ins, (), size, 2 * size)(own, *terms)
 
 
 def sum_at_holder(one, two, three, kept, own):
-    arrived = (mirrored(one, 1), mirrored(two, -1), mirrored(three, 2))
-    sums = combine(arrived, kept)
-    return spread(own, [mirrored(total, step) for total, step in zip(sums, (4, -4, 1, -1))])
+    three = mirrored(three, 2)
+    one = mirrored(one, 1)
+    two = mirrored(two, -1)
+    (near,) = combine(near_kernel, 1, one, kept)
+    near = mirrored(near, 1)
+    sums = combine(combine_kernel, 3, one, two, three, kept)
+    return spread(own, [near, *(mirrored(total, step) for total, step in zip(sums, (4, -4, -1)))])
 
 
 def iterate_kernel(mine_ref, other_ref, out_ref, wide_ref):
@@ -208,7 +218,6 @@
     out = jax.ShapeDtypeStruct((count // SPLIT[0], piece_rows, width), mine.dtype)
     return call(
         iterate_kernel,
-        "iterate_block",
         out,
         [None] * 2,
         [pltpu.VMEM((rows, width), jnp.float32)],

time: 119 us -> 118 us (level)
  starting transfers between devices: 59.4 us -> 55.8 us
  waiting for transfers between devices: 47.3 us -> 49.5 us
    all_to_all x3, starting transfers between devices: 19.5 us -> 17.1 us  [exchange(): return lax.all_to_all(pieces, axes, split_axis=0, concat_axis=0, tiled=True)]
    all_to_all x3, waiting for transfers between devices: 32.2 us -> 33.5 us  [exchange(): return lax.all_to_all(pieces, axes, split_axis=0, concat_axis=0, tiled=True)]
    pallas_call x4 -> x5, Pallas kernels: 6.44 us -> 6.46 us  [the longest x1 3.88 us: iterate(): call(iterate_kernel, out, [None] * 2, [pltpu.VMEM((rows, width), jnp.floa...]
  transfers between devices with their start and end apart: 11 -> 11, of which waited for: 7 -> 8; matrix products, arithmetic and copies ran while one was open for 1% -> 1% of each run, Pallas kernels for 0% -> 0%
where the time goes in v8:
time: 118 us; the launch traced here: 116 us
  starting transfers between devices  55.8 us (47%)
  waiting for transfers between devices  49.5 us (42%)
  Pallas kernels  6.46 us (5%)
  local copies, waits for them, and re-layouts  2.13 us (2%)
  other arithmetic  1.91 us (2%)
    ppermute x7, starting transfers between devices, mirrored(): return lax.ppermute(pieces, ('dp', 'tc'), pairs)  34.8 us
    all_to_all x3, waiting for transfers between devices, exchange(): return lax.all_to_all(pieces, axes, split_axis=0, concat_axis=0, tiled=True)  33.5 us
    all_to_all x3, starting transfers between devices, exchange(): return lax.all_to_all(pieces, axes, split_axis=0, concat_axis=0, tiled=True)  17.1 us
    ppermute x7, waiting for transfers between devices, mirrored(): return lax.ppermute(pieces, ('dp', 'tc'), pairs)  15.3 us
    ppermute x1, starting transfers between devices, body(): partner = lax.ppermute(arrived, 'tc', [(0, 1), (1, 0)])  3.92 us
    pallas_call x1, Pallas kernels, iterate(): call(iterate_kernel, out, [None] * 2, [pltpu.VMEM((rows, width), jnp.floa...  3.88 us
  transfers between devices with their start and end apart: 11, of which 8 were waited for; matrix products, arithmetic and copies ran while one was open for 1% of the time, Pallas kernels for 0%

profile of v8, /device:TPU:1, one launch (start us, length us, event | category | flops | bytes accessed | tf_op | source)
XLA Modules:
  0.0 116.0 jit_solution(13443309506333358587)
XLA Ops:
  0.0 1.6 %shard_map.37 = (bf16[3,16,8,512]{3,2,1,0:T(8,128)(2,1)S(1)}, bf16[3,16,8,512]{3,2,1,0:T(8,128)(2,1)S(1)}, bf16[1,16,8,512]{3,2,1,0:T(8,128)(2,1)S(1)}, bf16[4,1...) custom-call(s32[192]{0:T(256)} %owners_ref.1, bf16[12,16,8,512]{3,2,1,0:T(8,128)(2,1)} %bitcast.5, ...), custom_call_target="tpu_custom_call" | custom-call | flops 1572864 | bytes 3145728 | tf_op jit(solution)/shard_map/pallas_call | solution.py:115
  1.6 4.8 %collective-permute-start = (bf16[3,16,8,512]{3,2,1,0:T(8,128)(2,1)S(1)}, bf16[3,16,8,512]{3,2,1,0:T(8,128)(2,1)S(1)}, u32[]{:S(2)}, u32[]{:S(2)}) collective-permute-start(bf16[3,16,8,512]{3,2,1,0:T(8,128)(2,1)S(1)} %get-tuple-element.14), channel_id=1, source_target_pairs={{0,704},{1,65},{64,0},{65,129},{128,64},{129,193},{192,128},{193,2... | collective-permute-start | bytes 1179656 | tf_op jit(solution)/shard_map/ppermute | solution.py:39
  6.4 12.2 %collective-permute-start.2 = (bf16[3,16,8,512]{3,2,1,0:T(8,128)(2,1)S(1)}, bf16[3,16,8,512]{3,2,1,0:T(8,128)(2,1)S(1)}, u32[]{:S(2)}, u32[]{:S(2)}) collective-permute-start(bf16[3,16,8,512]{3,2,1,0:T(8,128)(2,1)S(1)} %get-tuple-element.16), channel_id=1, source_target_pairs={{0,64},{1,705},{64,128},{65,1},{128,192},{129,65},{192,256},{193,1... | collective-permute-start | bytes 1179656 | tf_op jit(solution)/shard_map/ppermute | solution.py:39
  18.7 1.9 %collective-permute-start.3 = (bf16[1,16,8,512]{3,2,1,0:T(8,128)(2,1)S(1)}, bf16[1,16,8,512]{3,2,1,0:T(8,128)(2,1)S(1)}, u32[]{:S(2)}, u32[]{:S(2)}) collective-permute-start(bf16[1,16,8,512]{3,2,1,0:T(8,128)(2,1)S(1)} %get-tuple-element.17), channel_id=1, source_target_pairs={{0,640},{1,129},{64,704},{65,193},{128,0},{129,257},{192,64},{193,... | collective-permute-start | bytes 393224 | tf_op jit(solution)/shard_map/ppermute | solution.py:39
  20.6 8.7 %collective-permute-done.3.three_ref = bf16[1,16,8,512]{3,2,1,0:T(8,128)(2,1)S(1)} collective-permute-done((bf16[1,16,8,512]{3,2,1,0:T(8,128)(2,1)S(1)}, bf16[1,16,8,512]{3,2,1,0:T(8,128)(2,1)S(1)}, u32[]{:S(2)}, u32[]{:S(2)}) %collective-permute-start.3) | collective-permute-done | bytes 131104 | tf_op jit(solution)/shard_map/ppermute | solution.py:39
  29.3 0.1 shard_map.39
  29.5 1.9 %collective-permute-start.4 = (bf16[16,8,512]{2,1,0:T(8,128)(2,1)S(1)}, bf16[16,8,512]{2,1,0:T(8,128)(2,1)S(1)}, u32[]{:S(2)}, u32[]{:S(2)}) collective-permute-start(bf16[16,8,512]{2,1,0:T(8,128)(2,1)S(1)} %get-tuple-element.18), channel_id=1, source_target_pairs={{0,512},{1,257},{64,576},{65,321},{128,640},{129,385},{192,704},{1... | collective-permute-start | bytes 393224 | tf_op jit(solution)/shard_map/ppermute | solution.py:39
  31.4 7.3 %collective-permute-start.5 = (bf16[16,8,512]{2,1,0:T(8,128)(2,1)S(1)}, bf16[16,8,512]{2,1,0:T(8,128)(2,1)S(1)}, u32[]{:S(2)}, u32[]{:S(2)}) collective-permute-start(bf16[16,8,512]{2,1,0:T(8,128)(2,1)S(1)} %get-tuple-element.19), channel_id=1, source_target_pairs={{0,256},{1,513},{64,320},{65,577},{128,384},{129,641},{192,448},{1... | collective-permute-start | bytes 393224 | tf_op jit(solution)/shard_map/ppermute | solution.py:39
  38.7 4.7 %collective-permute-start.6 = (bf16[16,8,512]{2,1,0:T(8,128)(2,1)S(1)}, bf16[16,8,512]{2,1,0:T(8,128)(2,1)S(1)}, u32[]{:S(2)}, u32[]{:S(2)}) collective-permute-start(bf16[16,8,512]{2,1,0:T(8,128)(2,1)S(1)} %get-tuple-element.20), channel_id=1, source_target_pairs={{0,64},{1,705},{64,128},{65,1},{128,192},{129,65},{192,256},{193,1... | collective-permute-start | bytes 393224 | tf_op jit(solution)/shard_map/ppermute | solution.py:39
  43.4 1.9 %collective-permute-start.1 = (bf16[16,8,512]{2,1,0:T(8,128)(2,1)S(1)}, bf16[16,8,512]{2,1,0:T(8,128)(2,1)S(1)}, u32[]{:S(2)}, u32[]{:S(2)}) collective-permute-start(bf16[16,8,512]{2,1,0:T(8,128)(2,1)S(1)} %shard_map.38), channel_id=1, source_target_pairs={{0,704},{1,65},{64,0},{65,129},{128,64},{129,193},{192,128},{193,2... | collective-permute-start | bytes 393224 | tf_op jit(solution)/shard_map/ppermute | solution.py:39
  45.4 4.2 %collective-permute-done.5.refs_3_ = bf16[16,8,512]{2,1,0:T(8,128)(2,1)S(1)} collective-permute-done((bf16[16,8,512]{2,1,0:T(8,128)(2,1)S(1)}, bf16[16,8,512]{2,1,0:T(8,128)(2,1)S(1)}, u32[]{:S(2)}, u32[]{:S(2)}) %collective-permute-start.5) | collective-permute-done | bytes 131104 | tf_op jit(solution)/shard_map/ppermute | solution.py:39
  49.6 0.7 collective-permute-done.6.refs_4_
  50.2 1.7 %collective-permute-done.1.refs_1_ = bf16[16,8,512]{2,1,0:T(8,128)(2,1)S(1)} collective-permute-done((bf16[16,8,512]{2,1,0:T(8,128)(2,1)S(1)}, bf16[16,8,512]{2,1,0:T(8,128)(2,1)S(1)}, u32[]{:S(2)}, u32[]{:S(2)}) %collective-permute-start.1) | collective-permute-done | bytes 131104 | tf_op jit(solution)/shard_map/ppermute | solution.py:39
  52.0 0.8 shard_map.40
  52.7 9.7 %all-to-all-start = ((bf16[32,8,512]{2,1,0:T(8,128)(2,1)}), bf16[32,8,512]{2,1,0:T(8,128)(2,1)S(1)}, u32[]{:S(2)}, u32[]{:S(2)}) async-start(bf16[32,8,512]{2,1,0:T(8,128)(2,1)} %shard_map.40), calls=%async_computation | async-start | bytes 524288 | tf_op jit(solution)/shard_map/all_to_all | solution.py:29
  62.5 0.2 convert_reduce_fusion.2
  62.8 11.6 %all-to-all-done.mine_ref = bf16[32,8,512]{2,1,0:T(8,128)(2,1)S(1)} async-done(((bf16[32,8,512]{2,1,0:T(8,128)(2,1)}), bf16[32,8,512]{2,1,0:T(8,128)(2,1)S(1)}, u32[]{:S(2)}, u32[]{:S(2)}) %all-to-all-start) | async-done | bytes 262176 | tf_op jit(solution)/shard_map/all_to_all | solution.py:29
  74.4 3.9 %collective-permute-start.7 = (bf16[32,8,512]{2,1,0:T(8,128)(2,1)S(1)}, bf16[32,8,512]{2,1,0:T(8,128)(2,1)S(1)}, u32[]{:S(2)}, u32[]{:S(2)}) collective-permute-start(bf16[32,8,512]{2,1,0:T(8,128)(2,1)S(1)} %all-to-all-done.mine_ref), channel_id=1, source_target_pairs={{0,1},{1,0},{2,3},{3,2},{4,5},{5,4},{6,7},{7,6},{8,9},{9,8},{10,11... | collective-permute-start | bytes 786440 | tf_op jit(solution)/shard_map/ppermute | solution.py:243
  78.4 0.1 copy.4
  78.6 0.2 convert_reduce_fusion.1
  78.8 0.7 collective-permute-done.7.other_ref
  79.5 3.9 %shard_map.41 = bf16[16,8,512]{2,1,0:T(8,128)(2,1)} custom-call(bf16[32,8,512]{2,1,0:T(8,128)(2,1)S(1)} %all-to-all-done.mine_ref, bf16[32,8,512]{2,1,0:T(8,128)(2,1)S(1)} %collective-permute-done.7.other_ref), custom_call_target="tpu_custom_call" | custom-call | flops 2415919104 | bytes 1048576 | tf_op jit(solution)/shard_map/pallas_call | solution.py:219
  83.3 3.5 %all-to-all-start.1 = ((bf16[16,8,512]{2,1,0:T(8,128)(2,1)}), bf16[16,8,512]{2,1,0:T(8,128)(2,1)S(1)}, u32[]{:S(2)}, u32[]{:S(2)}) async-start(bf16[16,8,512]{2,1,0:T(8,128)(2,1)} %shard_map.41), calls=%async_computation.1 | async-start | bytes 262144 | tf_op jit(solution)/shard_map/all_to_all | solution.py:29
  86.9 8.0 %all-to-all-done.1 = bf16[16,8,512]{2,1,0:T(8,128)(2,1)S(1)} async-done(((bf16[16,8,512]{2,1,0:T(8,128)(2,1)}), bf16[16,8,512]{2,1,0:T(8,128)(2,1)S(1)}, u32[]{:S(2)}, u32[]{:S(2)}) %all-to-all-start.1) | async-done | bytes 131104 | tf_op jit(solution)/shard_map/all_to_all | solution.py:29
  94.9 1.3 %gather_fusion = bf16[36,8,512]{2,1,0:T(8,128)(2,1)} fusion(bf16[16,8,512]{2,1,0:T(8,128)(2,1)S(1)} %all-to-all-done.1, s32[1024]{0:T(1024)S(1)} %pad_clamp_fusion.1), kind=kCustom, calls=%fused_computation | custom fusion | bytes 589968 | tf_op jit(solution)/shard_map/jit(_take)/gather | solution.py:254
  96.2 3.9 %all-to-all-start.2 = ((bf16[36,8,512]{2,1,0:T(8,128)(2,1)}), bf16[36,8,512]{2,1,0:T(8,128)(2,1)S(1)}, u32[]{:S(2)}, u32[]{:S(2)}) async-start(bf16[36,8,512]{2,1,0:T(8,128)(2,1)} %gather_fusion), calls=%async_computation.2 | async-start | bytes 589824 | tf_op jit(solution)/shard_map/all_to_all | solution.py:29
  100.1 0.2 convert_reduce_fusion
  100.3 0.1 select_reduce_fusion
  100.4 0.1 fusion.3
  100.5 13.9 %all-to-all-done.2 = bf16[36,8,512]{2,1,0:T(8,128)(2,1)S(1)} async-done(((bf16[36,8,512]{2,1,0:T(8,128)(2,1)}), bf16[36,8,512]{2,1,0:T(8,128)(2,1)S(1)}, u32[]{:S(2)}, u32[]{:S(2)}) %all-to-all-start.2) | async-done | bytes 294944 | tf_op jit(solution)/shard_map/all_to_all | solution.py:29
  114.5 0.6 gather_fusion.1
  115.0 0.9 convert_select_fusion
  (16 shorter events, 0.4 us)
Async XLA Ops:
  1.6 27.7 %collective-permute-start = (bf16[3,16,8,512]{3,2,1,0:T(8,128)(2,1)S(1)}, bf16[3,16,8,512]{3,2,1,0:T(8,128)(2,1)S(1)}, u32[]{:S(2)}, u32[]{:S(2)}) collective-permute-start(bf16[3,16,8,512]{3,2,1,0:T(8,128)(2,1)S(1)} %get-tuple-element.14), channel_id=1, source_target_pairs={{0,704},{1,65},{64,0},{65,129},{128,64},{129,193},{192,128},{193,2... | collective-permute-start | bytes 1179656 | tf_op jit(solution)/shard_map/ppermute | solution.py:39
  6.4 22.9 %collective-permute-start.2 = (bf16[3,16,8,512]{3,2,1,0:T(8,128)(2,1)S(1)}, bf16[3,16,8,512]{3,2,1,0:T(8,128)(2,1)S(1)}, u32[]{:S(2)}, u32[]{:S(2)}) collective-permute-start(bf16[3,16,8,512]{3,2,1,0:T(8,128)(2,1)S(1)} %get-tuple-element.16), channel_id=1, source_target_pairs={{0,64},{1,705},{64,128},{65,1},{128,192},{129,65},{192,256},{193,1... | collective-permute-start | bytes 1179656 | tf_op jit(solution)/shard_map/ppermute | solution.py:39
  18.7 10.6 %collective-permute-start.3 = (bf16[1,16,8,512]{3,2,1,0:T(8,128)(2,1)S(1)}, bf16[1,16,8,512]{3,2,1,0:T(8,128)(2,1)S(1)}, u32[]{:S(2)}, u32[]{:S(2)}) collective-permute-start(bf16[1,16,8,512]{3,2,1,0:T(8,128)(2,1)S(1)} %get-tuple-element.17), channel_id=1, source_target_pairs={{0,640},{1,129},{64,704},{65,193},{128,0},{129,257},{192,64},{193,... | collective-permute-start | bytes 393224 | tf_op jit(solution)/shard_map/ppermute | solution.py:39
  29.4 33.0 %copy-start = (s32[192]{0:T(256)S(1)}, s32[192]{0:T(256)}, u32[]{:S(2)}) copy-start(s32[192]{0:T(256)} %owners_ref.1) | copy-start | bytes 2308
  29.5 15.9 %collective-permute-start.4 = (bf16[16,8,512]{2,1,0:T(8,128)(2,1)S(1)}, bf16[16,8,512]{2,1,0:T(8,128)(2,1)S(1)}, u32[]{:S(2)}, u32[]{:S(2)}) collective-permute-start(bf16[16,8,512]{2,1,0:T(8,128)(2,1)S(1)} %get-tuple-element.18), channel_id=1, source_target_pairs={{0,512},{1,257},{64,576},{65,321},{128,640},{129,385},{192,704},{1... | collective-permute-start | bytes 393224 | tf_op jit(solution)/shard_map/ppermute | solution.py:39
  31.4 18.2 %collective-permute-start.5 = (bf16[16,8,512]{2,1,0:T(8,128)(2,1)S(1)}, bf16[16,8,512]{2,1,0:T(8,128)(2,1)S(1)}, u32[]{:S(2)}, u32[]{:S(2)}) collective-permute-start(bf16[16,8,512]{2,1,0:T(8,128)(2,1)S(1)} %get-tuple-element.19), channel_id=1, source_target_pairs={{0,256},{1,513},{64,320},{65,577},{128,384},{129,641},{192,448},{1... | collective-permute-start | bytes 393224 | tf_op jit(solution)/shard_map/ppermute | solution.py:39
  38.7 11.6 %collective-permute-start.6 = (bf16[16,8,512]{2,1,0:T(8,128)(2,1)S(1)}, bf16[16,8,512]{2,1,0:T(8,128)(2,1)S(1)}, u32[]{:S(2)}, u32[]{:S(2)}) collective-permute-start(bf16[16,8,512]{2,1,0:T(8,128)(2,1)S(1)} %get-tuple-element.20), channel_id=1, source_target_pairs={{0,64},{1,705},{64,128},{65,1},{128,192},{129,65},{192,256},{193,1... | collective-permute-start | bytes 393224 | tf_op jit(solution)/shard_map/ppermute | solution.py:39
  43.4 8.5 %collective-permute-start.1 = (bf16[16,8,512]{2,1,0:T(8,128)(2,1)S(1)}, bf16[16,8,512]{2,1,0:T(8,128)(2,1)S(1)}, u32[]{:S(2)}, u32[]{:S(2)}) collective-permute-start(bf16[16,8,512]{2,1,0:T(8,128)(2,1)S(1)} %shard_map.38), channel_id=1, source_target_pairs={{0,704},{1,65},{64,0},{65,129},{128,64},{129,193},{192,128},{193,2... | collective-permute-start | bytes 393224 | tf_op jit(solution)/shard_map/ppermute | solution.py:39
  52.7 21.6 %all-to-all-start = ((bf16[32,8,512]{2,1,0:T(8,128)(2,1)}), bf16[32,8,512]{2,1,0:T(8,128)(2,1)S(1)}, u32[]{:S(2)}, u32[]{:S(2)}) async-start(bf16[32,8,512]{2,1,0:T(8,128)(2,1)} %shard_map.40), calls=%async_computation | async-start | bytes 524288 | tf_op jit(solution)/shard_map/all_to_all | solution.py:29
  74.4 5.1 %collective-permute-start.7 = (bf16[32,8,512]{2,1,0:T(8,128)(2,1)S(1)}, bf16[32,8,512]{2,1,0:T(8,128)(2,1)S(1)}, u32[]{:S(2)}, u32[]{:S(2)}) collective-permute-start(bf16[32,8,512]{2,1,0:T(8,128)(2,1)S(1)} %all-to-all-done.mine_ref), channel_id=1, source_target_pairs={{0,1},{1,0},{2,3},{3,2},{4,5},{5,4},{6,7},{7,6},{8,9},{9,8},{10,11... | collective-permute-start | bytes 786440 | tf_op jit(solution)/shard_map/ppermute | solution.py:243
  83.3 11.5 %all-to-all-start.1 = ((bf16[16,8,512]{2,1,0:T(8,128)(2,1)}), bf16[16,8,512]{2,1,0:T(8,128)(2,1)S(1)}, u32[]{:S(2)}, u32[]{:S(2)}) async-start(bf16[16,8,512]{2,1,0:T(8,128)(2,1)} %shard_map.41), calls=%async_computation.1 | async-start | bytes 262144 | tf_op jit(solution)/shard_map/all_to_all | solution.py:29
  96.2 18.3 %all-to-all-start.2 = ((bf16[36,8,512]{2,1,0:T(8,128)(2,1)}), bf16[36,8,512]{2,1,0:T(8,128)(2,1)S(1)}, u32[]{:S(2)}, u32[]{:S(2)}) async-start(bf16[36,8,512]{2,1,0:T(8,128)(2,1)} %gather_fusion), calls=%async_computation.2 | async-start | bytes 589824 | tf_op jit(solution)/shard_map/all_to_all | solution.py:29
